TPU v7x, 256 devices: a whole 4x4x8 slice. The times are simulated.
256 devices in a mesh: wave: 16 (over z, y_hi), lat: 16 (over x, y_lo, core).
Axes of the slice: x: 4, y: 4 (y_hi: 2, y_lo: 2; y = y_hi * 2 + y_lo), z: 8, core: 2. Of those that a mesh axis runs over, the one named last changes fastest.
Arguments:
- control: bfloat16 [640, 640, 256], P('wave', 'lat'), may hold values from -6 to 6
- vert_root: bfloat16 [640, 128, 128], P('wave'), may hold values from -0.5 to 0.5
- legendre: bfloat16 [640, 640, 256], P('lat', 'wave'), may hold values from -0.3125 to 0.3125
- row_wavenumber: int32 [640], P('wave'), may hold values from 0 to 639, each once
- courant_east: float32 [256, 1280, 128], P('wave', 'lat'), may hold values from 0.05 to 0.45
- courant_north: float32 [256, 1280, 128], P('wave', 'lat'), may hold values from 0.05 to 0.45
- east_flags: int32 [256, 1280, 128], P('wave', 'lat'), may hold values 0 or 1
- north_flags: int32 [256, 1280, 128], P('wave', 'lat'), may hold values 0 or 1
Outputs:
- tracer: float32 [256, 1280, 128], P('wave', 'lat')
Inputs may be any that keep to these rules, and one draw needn't show every extreme that they name: `row_wavenumber`: A permutation of 0 to 639.
All inputs are finite; a program needn't handle non-finite values. No bound on the sum of `east_flags` or of `north_flags` on one device may be relied on, other than what follows from the above.
Results may differ from a plain program's by a relative error of at most 0.0069.
Values may be sent and summed in bfloat16 or wider, within the bound.
No kernel may reach another device: no remote copies, remote signals or barrier semaphores. Data moves between devices by JAX's collectives and lax.ppermute only.
A program may use at most 64 MiB of HBM per device.

v0:
```python
import math

import jax
import jax.numpy as jnp
from jax import lax
from jax.sharding import PartitionSpec as P

LEV = 128
STEPS = 4


def cut_along(array, dim, length):
    shape = array.shape
    blocks = array.reshape(*shape[:dim], length, shape[dim] // length, *shape[dim + 1 :])
    return jnp.moveaxis(blocks, dim, 0)


def sum_at_owner(array, axis, dim):
    length = lax.axis_size(axis)
    blocks = lax.all_to_all(cut_along(array, dim, length), axis, 0, 0, tiled=True)
    return jnp.sum(blocks.astype(jnp.float32), axis=0)


def passed_along(value, axis, steps):
    count = lax.axis_size(axis)
    pairs = [(source, (source + steps) % count) for source in range(count)]
    return lax.ppermute(value, axis, pairs)


def passed_along_2(block, axis, distance):
    devices = range(lax.axis_size(axis))
    route = [(i - distance, i) for i in devices if i - distance in devices]
    return lax.ppermute(block, axis, route)


def with_halo(array, sides, width, wrap):
    for axis, dim in sides:
        size, length = (lax.axis_size(axis), array.shape[dim])
        up = [(i, (i + 1) % size) for i in range(size if wrap else size - 1)]
        down = [(j, i) for i, j in up]
        last = lax.slice_in_dim(array, length - width, length, axis=dim)
        leading = lax.slice_in_dim(array, 0, width, axis=dim)
        before = lax.ppermute(last, axis, up)
        after = lax.ppermute(leading, axis, down)
        array = jnp.concatenate([before, array, after], axis=dim)
    return array


def minmod(first_jump, second_jump):
    return jnp.maximum(0.0, jnp.minimum(first_jump, second_jump)) + jnp.minimum(
        0.0, jnp.maximum(first_jump, second_jump)
    )


def window(values, begin_at, end_at, axis_dim):
    return lax.slice_in_dim(values, begin_at, end_at, axis=axis_dim)


def transport(padded, winds, axis_dim, cell_count):
    jumps = window(padded, 1, cell_count + 4, axis_dim) - window(
        padded, 0, cell_count + 3, axis_dim
    )
    limited = minmod(
        window(jumps, 1, cell_count + 3, axis_dim), window(jumps, 0, cell_count + 2, axis_dim)
    )
    below_cells = window(padded, 1, cell_count + 2, axis_dim)
    above_cells = window(padded, 2, cell_count + 3, axis_dim)
    lower_slope = window(limited, 0, cell_count + 1, axis_dim)
    upper_slope = window(limited, 1, cell_count + 2, axis_dim)
    courant = jnp.abs(winds)
    fluxes = jnp.maximum(winds, 0.0) * (
        below_cells + 0.5 * (1.0 - courant) * lower_slope
    ) + jnp.minimum(winds, 0.0) * (above_cells - 0.5 * (1.0 - courant) * upper_slope)
    return window(fluxes, 1, cell_count + 1, axis_dim) - window(fluxes, 0, cell_count, axis_dim)


def dft_basis(order_ids, lon_ids, total_lon, total_orders):
    product = order_ids[:, None] * lon_ids[None, :] % total_lon
    phases = product.astype(jnp.float32) * (2.0 * math.pi / total_lon)
    weight = jnp.where(order_ids == 0, 1.0, 2.0).astype(jnp.float32) * (
        1.0 / math.sqrt(2.0 * total_orders)
    )
    return jnp.stack(
        [weight[:, None] * jnp.cos(phases), -weight[:, None] * jnp.sin(phases)]
    ).astype(jnp.bfloat16)


def per_device(
    control,
    vert_root,
    legendre,
    row_wavenumber,
    courant_east,
    courant_north,
    east_flags,
    north_flags,
):
    row_count, order_count, double_levels = control.shape
    wave_count = lax.axis_size("wave")
    lat_count = lax.axis_size("lat")
    total_orders = order_count * lat_count
    total_lon = 2 * total_orders
    level_local = LEV // wave_count
    latitudes = legendre.shape[2]
    orders = lax.axis_index("lat") * order_count + jnp.arange(order_count, dtype=jnp.int32)
    exists = row_wavenumber[:, None] >= orders[None, :]
    spectra = jnp.where(exists[:, :, None], control, jnp.zeros((), control.dtype))
    complex_parts = spectra.reshape(row_count, order_count, LEV, 2)
    vertical = jnp.einsum(
        "rmlp,rkl->kpmr", complex_parts, vert_root, preferred_element_type=jnp.float32
    ).astype(jnp.bfloat16)
    stacked = vertical.reshape(2 * LEV, order_count, row_count)
    segment = stacked
    modes_sum = sum_at_owner(
        jnp.einsum("cmr,mrj->cmj", segment, legendre, preferred_element_type=jnp.float32).astype(
            jnp.bfloat16
        ),
        "wave",
        0,
    )
    latitude_modes = modes_sum.astype(jnp.bfloat16)
    lon_local = total_lon // lat_count
    lon_ids = lax.axis_index("lat") * lon_local + jnp.arange(lon_local, dtype=jnp.int32)
    segment = lax.all_gather(latitude_modes, "lat", axis=1, tiled=True)
    order_ids = jnp.arange(segment.shape[1], dtype=jnp.int32)
    basis = dft_basis(order_ids, lon_ids, total_lon, total_orders)
    shaped = segment.reshape(level_local, 2, segment.shape[1], latitudes)
    gridded = jnp.einsum("kpmj,pml->jlk", shaped, basis, preferred_element_type=jnp.float32)
    column_tile = lax.all_to_all(gridded, "wave", split_axis=0, concat_axis=2, tiled=True)
    wind_east = courant_east * (2 * east_flags - 1).astype(jnp.float32)
    wind_north = courant_north * (2 * north_flags - 1).astype(jnp.float32)
    west_edge = passed_along(wind_east[:, -1:], "lat", 1)
    winds_x = jnp.concatenate([west_edge, wind_east], axis=1)
    south_edge = passed_along_2(wind_north[-1:], "wave", 1)
    winds_y = jnp.concatenate([south_edge, wind_north], axis=0)
    tracer = column_tile
    tile_rows = tracer.shape[0]
    tile_lon = tracer.shape[1]
    for repeat in range(STEPS):
        lon_padded = with_halo(tracer.astype(jnp.bfloat16), (("lat", 1),), 2, True).astype(
            tracer.dtype
        )
        row_padded = with_halo(tracer.astype(jnp.bfloat16), (("wave", 0),), 2, False).astype(
            tracer.dtype
        )
        tracer = (
            tracer
            - transport(lon_padded, winds_x, 1, tile_lon)
            - transport(row_padded, winds_y, 0, tile_rows)
        )
    return tracer


def solution(mesh):
    return jax.shard_map(
        per_device,
        mesh=mesh,
        in_specs=(
            P("wave", "lat", None),
            P("wave", None, None),
            P("lat", "wave", None),
            P("wave"),
            P("wave", "lat", None),
            P("wave", "lat", None),
            P("wave", "lat", None),
            P("wave", "lat", None),
        ),
        out_specs=P("wave", "lat", None),
        check_vma=False,
    )
```

profile of v0, /device:TPU:64, one launch (start us, length us, event | category | flops | bytes accessed | tf_op | source)
XLA Modules:
  0.0 311.1 jit_solution(2980356625274923959)
XLA Ops:
  8.8 4.0 %copy.54 = bf16[40,40,256]{1,0,2:T(8,128)(2,1)} copy(bf16[40,40,256]{2,1,0:T(8,128)(2,1)S(1)} %broadcast_select_fusion) | data formatting | bytes 1638400 | tf_op jit(solution)/shard_map/jit(_where)/select_n | solution.py:107
  12.8 2.7 fusion.7
  15.5 5.8 %copy.56 = bf16[128,2,40,40]{3,2,1,0:T(8,128)(2,1)} copy(bf16[128,2,40,40]{0,2,1,3:T(8,128)(2,1)S(1)} %fusion.7) | data formatting | bytes 1638400 | tf_op jit(solution)/shard_map/convert_element_type | solution.py:111
  21.3 3.3 %convolution_convert_fusion = bf16[40,256,256]{2,1,0:T(8,128)(2,1)S(1)} fusion(bf16[40,40,256]{2,1,0:T(8,128)(2,1)S(1)} %copy-done.2, bf16[256,40,40]{2,1,0:T(8,128)(2,1)} %bitcast.36), kind=kOutput, calls=%fused_computation | convolution fusion | flops 212336640 | bytes 6881280 | tf_op jit(solution)/shard_map/cmr,mrj->cmj/dot_general | solution.py:115
  25.1 128.6 %all_to_all.23 = bf16[16,16,40,256]{3,1,2,0:T(8,128)(2,1)} all-to-all(bf16[16,16,40,256]{3,1,2,0:T(8,128)(2,1)S(1)} %copy.58), channel_id=1, replica_groups=mesh['wave'=16,'lat'=16] {'wave'}, dimensions={0} | all-to-all | bytes 10485760 | tf_op jit(solution)/shard_map/all_to_all | solution.py:20
  153.7 4.0 %reduce_sum.12 = bf16[16,40,256]{2,0,1:T(8,128)(2,1)} reduce(bf16[16,16,40,256]{3,1,2,0:T(8,128)(2,1)} %all_to_all.23, bf16[]{:T(256)} %constant.23.clone.1), dimensions={0}, to_apply=%region_0.1 | reduce | flops 2457600 | bytes 5570562 | tf_op jit(solution)/shard_map/reduce_sum | solution.py:21
  158.7 37.5 %all-gather.2.cloned.1.call-done = bf16[16,640,256]{2,0,1:T(8,128)(2,1)} async-done(((bf16[16,40,256]{2,0,1:T(8,128)(2,1)}), bf16[16,640,256]{2,0,1:T(8,128)(2,1)}) %all-gather.2.cloned.1.call-update) | async-done | bytes 5242896 | tf_op jit(solution)/shard_map/all_gather | solution.py:124
  196.2 4.3 %copy.60 = bf16[16,640,256]{2,1,0:T(8,128)(2,1)S(1)} copy(bf16[16,640,256]{2,0,1:T(8,128)(2,1)} %all-gather.2.cloned.1.call-done) | data formatting | bytes 10485760 | tf_op jit(solution)/shard_map/all_gather | solution.py:124
  202.9 9.8 %all-to-all-start.1 = ((f32[256,80,8]{1,2,0:T(8,128)}), f32[256,80,8]{1,2,0:T(8,128)S(1)}, u32[]{:S(2)}, u32[]{:S(2)}) async-start(f32[256,80,8]{1,2,0:T(8,128)} %copy.61), calls=%async_computation.1 | async-start | bytes 2097152 | tf_op jit(solution)/shard_map/all_to_all | solution.py:129
  213.9 4.9 %collective-permute-start.3 = (f32[1,80,128]{2,1,0:T(8,128)S(1)}, f32[1,80,128]{2,1,0:T(8,128)S(1)}, u32[]{:S(2)}, u32[]{:S(2)}) collective-permute-start(f32[1,80,128]{2,1,0:T(8,128)S(1)} %slice.405), channel_id=1, source_target_pairs={{0,16},{16,32},{32,48},{48,64},{64,80},{80,96},{96,112},{112,128},... | collective-permute-start | bytes 122888 | tf_op jit(solution)/shard_map/ppermute | solution.py:33
  220.3 21.5 %all-to-all-done.1 = f32[256,80,8]{1,2,0:T(8,128)S(1)} async-done(((f32[256,80,8]{1,2,0:T(8,128)}), f32[256,80,8]{1,2,0:T(8,128)S(1)}, u32[]{:S(2)}, u32[]{:S(2)}) %all-to-all-start.1) | async-done | bytes 655392 | tf_op jit(solution)/shard_map/all_to_all | solution.py:129
  245.2 1.9 collective-permute-start.5
  247.2 5.4 %collective-permute-start.4 = (bf16[2,80,128]{2,1,0:T(8,128)(2,1)S(1)}, bf16[2,80,128]{2,1,0:T(8,128)(2,1)S(1)}, u32[]{:S(2)}, u32[]{:S(2)}) collective-permute-start(bf16[2,80,128]{2,1,0:T(8,128)(2,1)S(1)} %get-tuple-element.25), channel_id=1, source_target_pairs={{0,16},{16,32},{32,48},{48,64},{64,80},{80,96},{96,112},{112,128},... | collective-permute-start | bytes 122888 | tf_op jit(solution)/shard_map/ppermute | solution.py:43
  253.5 2.1 collective-permute-done.4
  256.4 2.5 collective-permute-start.7
  258.9 3.3 %collective-permute-start.9 = (bf16[2,80,128]{2,1,0:T(8,128)(2,1)S(1)}, bf16[2,80,128]{2,1,0:T(8,128)(2,1)S(1)}, u32[]{:S(2)}, u32[]{:S(2)}) collective-permute-start(bf16[2,80,128]{2,1,0:T(8,128)(2,1)S(1)} %get-tuple-element.22), channel_id=1, source_target_pairs={{16,0},{32,16},{48,32},{64,48},{80,64},{96,80},{112,96},{128,112},... | collective-permute-start | bytes 122888 | tf_op jit(solution)/shard_map/ppermute | solution.py:44
  262.2 4.1 %collective-permute-start.8 = (bf16[2,80,128]{2,1,0:T(8,128)(2,1)S(1)}, bf16[2,80,128]{2,1,0:T(8,128)(2,1)S(1)}, u32[]{:S(2)}, u32[]{:S(2)}) collective-permute-start(bf16[2,80,128]{2,1,0:T(8,128)(2,1)S(1)} %get-tuple-element.21), channel_id=1, source_target_pairs={{0,16},{16,32},{32,48},{48,64},{64,80},{80,96},{96,112},{112,128},... | collective-permute-start | bytes 122888 | tf_op jit(solution)/shard_map/ppermute | solution.py:43
  267.2 3.3 %collective-permute-done.8 = bf16[2,80,128]{2,1,0:T(8,128)(2,1)S(1)} collective-permute-done((bf16[2,80,128]{2,1,0:T(8,128)(2,1)S(1)}, bf16[2,80,128]{2,1,0:T(8,128)(2,1)S(1)}, u32[]{:S(2)}, u32[]{:S(2)}) %collective-permute-start.8) | collective-permute-done | bytes 40992 | tf_op jit(solution)/shard_map/ppermute | solution.py:43
  273.2 4.9 %collective-permute-start.13 = (bf16[2,80,128]{2,1,0:T(8,128)(2,1)S(1)}, bf16[2,80,128]{2,1,0:T(8,128)(2,1)S(1)}, u32[]{:S(2)}, u32[]{:S(2)}) collective-permute-start(bf16[2,80,128]{2,1,0:T(8,128)(2,1)S(1)} %get-tuple-element.18), channel_id=1, source_target_pairs={{16,0},{32,16},{48,32},{64,48},{80,64},{96,80},{112,96},{128,112},... | collective-permute-start | bytes 122888 | tf_op jit(solution)/shard_map/ppermute | solution.py:44
  278.1 2.4 collective-permute-start.12
  281.4 5.0 %collective-permute-done.12 = bf16[2,80,128]{2,1,0:T(8,128)(2,1)S(1)} collective-permute-done((bf16[2,80,128]{2,1,0:T(8,128)(2,1)S(1)}, bf16[2,80,128]{2,1,0:T(8,128)(2,1)S(1)}, u32[]{:S(2)}, u32[]{:S(2)}) %collective-permute-start.12) | collective-permute-done | bytes 40992 | tf_op jit(solution)/shard_map/ppermute | solution.py:43
  289.1 5.3 %collective-permute-start.17 = (bf16[2,80,128]{2,1,0:T(8,128)(2,1)S(1)}, bf16[2,80,128]{2,1,0:T(8,128)(2,1)S(1)}, u32[]{:S(2)}, u32[]{:S(2)}) collective-permute-start(bf16[2,80,128]{2,1,0:T(8,128)(2,1)S(1)} %get-tuple-element.14), channel_id=1, source_target_pairs={{16,0},{32,16},{48,32},{64,48},{80,64},{96,80},{112,96},{128,112},... | collective-permute-start | bytes 122888 | tf_op jit(solution)/shard_map/ppermute | solution.py:44
  294.4 2.0 collective-permute-start.16
  297.3 5.4 %collective-permute-done.16 = bf16[2,80,128]{2,1,0:T(8,128)(2,1)S(1)} collective-permute-done((bf16[2,80,128]{2,1,0:T(8,128)(2,1)S(1)}, bf16[2,80,128]{2,1,0:T(8,128)(2,1)S(1)}, u32[]{:S(2)}, u32[]{:S(2)}) %collective-permute-start.16) | collective-permute-done | bytes 40992 | tf_op jit(solution)/shard_map/ppermute | solution.py:43
  (92 shorter events, 23.1 us)
Async XLA Ops:
  6.5 6.3 %copy-start = (bf16[40,128,128]{2,1,0:T(8,128)(2,1)S(1)}, bf16[40,128,128]{2,1,0:T(8,128)(2,1)}, u32[]{:S(2)}) copy-start(bf16[40,128,128]{2,1,0:T(8,128)(2,1)} %param.9) | copy-start | bytes 3932164
  6.5 189.7 %all-gather.2.cloned.1.call-start = ((), (), s32[]{:S(2)}) async-start(), calls=%async_computation.2 | async-start | bytes 5570560 | tf_op jit(solution)/shard_map/all_gather | solution.py:124
  15.5 5.8 %copy-start.2 = (bf16[40,40,256]{2,1,0:T(8,128)(2,1)S(1)}, bf16[40,40,256]{2,1,0:T(8,128)(2,1)}, u32[]{:S(2)}) copy-start(bf16[40,40,256]{2,1,0:T(8,128)(2,1)} %param.10) | copy-start | bytes 2457604
  201.6 11.1 %copy-start.3 = (f32[16,80,128]{2,1,0:T(8,128)S(1)}, f32[16,80,128]{2,1,0:T(8,128)}, u32[]{:S(2)}) copy-start(f32[16,80,128]{2,1,0:T(8,128)} %param.13) | copy-start | bytes 1966084
  202.9 38.8 %all-to-all-start.1 = ((f32[256,80,8]{1,2,0:T(8,128)}), f32[256,80,8]{1,2,0:T(8,128)S(1)}, u32[]{:S(2)}, u32[]{:S(2)}) async-start(f32[256,80,8]{1,2,0:T(8,128)} %copy.61), calls=%async_computation.1 | async-start | bytes 2097152 | tf_op jit(solution)/shard_map/all_to_all | solution.py:129
  213.9 41.9 %collective-permute-start.3 = (f32[1,80,128]{2,1,0:T(8,128)S(1)}, f32[1,80,128]{2,1,0:T(8,128)S(1)}, u32[]{:S(2)}, u32[]{:S(2)}) collective-permute-start(f32[1,80,128]{2,1,0:T(8,128)S(1)} %slice.405), channel_id=1, source_target_pairs={{0,16},{16,32},{32,48},{48,64},{64,80},{80,96},{96,112},{112,128},... | collective-permute-start | bytes 122888 | tf_op jit(solution)/shard_map/ppermute | solution.py:33
  220.2 32.8 %collective-permute-start = (f32[16,1,128]{2,0,1:T(8,128)S(1)}, f32[16,1,128]{2,0,1:T(8,128)S(1)}, u32[]{:S(2)}, u32[]{:S(2)}) collective-permute-start(f32[16,1,128]{2,0,1:T(8,128)S(1)} %bitcast.43), channel_id=1, source_target_pairs={{0,1},{1,2},{2,3},{3,4},{4,5},{5,6},{6,7},{7,8},{8,9},{9,10},{10,1... | collective-permute-start | bytes 24584 | tf_op jit(solution)/shard_map/ppermute | solution.py:27
  244.5 2.7 collective-permute-start.2
  245.1 7.5 %collective-permute-start.1 = (bf16[16,2,128]{2,1,0:T(2,128)(2,1)S(1)}, bf16[16,2,128]{2,1,0:T(2,128)(2,1)S(1)}, u32[]{:S(2)}, u32[]{:S(2)}) collective-permute-start(bf16[16,2,128]{2,1,0:T(2,128)(2,1)S(1)} %get-tuple-element.23), channel_id=1, source_target_pairs={{0,1},{1,2},{2,3},{3,4},{4,5},{5,6},{6,7},{7,8},{8,9},{9,10},{10,1... | collective-permute-start | bytes 24584 | tf_op jit(solution)/shard_map/ppermute | solution.py:43
  245.2 8.2 %collective-permute-start.5 = (bf16[2,80,128]{2,1,0:T(8,128)(2,1)S(1)}, bf16[2,80,128]{2,1,0:T(8,128)(2,1)S(1)}, u32[]{:S(2)}, u32[]{:S(2)}) collective-permute-start(bf16[2,80,128]{2,1,0:T(8,128)(2,1)S(1)} %get-tuple-element.26), channel_id=1, source_target_pairs={{16,0},{32,16},{48,32},{64,48},{80,64},{96,80},{112,96},{128,112},... | collective-permute-start | bytes 122888 | tf_op jit(solution)/shard_map/ppermute | solution.py:44
  247.2 8.4 %collective-permute-start.4 = (bf16[2,80,128]{2,1,0:T(8,128)(2,1)S(1)}, bf16[2,80,128]{2,1,0:T(8,128)(2,1)S(1)}, u32[]{:S(2)}, u32[]{:S(2)}) collective-permute-start(bf16[2,80,128]{2,1,0:T(8,128)(2,1)S(1)} %get-tuple-element.25), channel_id=1, source_target_pairs={{0,16},{16,32},{32,48},{48,64},{64,80},{80,96},{96,112},{112,128},... | collective-permute-start | bytes 122888 | tf_op jit(solution)/shard_map/ppermute | solution.py:43
  256.4 9.9 %collective-permute-start.7 = (bf16[16,2,128]{2,1,0:T(2,128)(2,1)S(1)}, bf16[16,2,128]{2,1,0:T(2,128)(2,1)S(1)}, u32[]{:S(2)}, u32[]{:S(2)}) collective-permute-start(bf16[16,2,128]{2,1,0:T(2,128)(2,1)S(1)} %get-tuple-element.20), channel_id=1, source_target_pairs={{1,0},{2,1},{3,2},{4,3},{5,4},{6,5},{7,6},{8,7},{9,8},{10,9},{11,1... | collective-permute-start | bytes 24584 | tf_op jit(solution)/shard_map/ppermute | solution.py:44
  258.9 7.4 %collective-permute-start.6 = (bf16[16,2,128]{2,1,0:T(2,128)(2,1)S(1)}, bf16[16,2,128]{2,1,0:T(2,128)(2,1)S(1)}, u32[]{:S(2)}, u32[]{:S(2)}) collective-permute-start(bf16[16,2,128]{2,1,0:T(2,128)(2,1)S(1)} %get-tuple-element.19), channel_id=1, source_target_pairs={{0,1},{1,2},{2,3},{3,4},{4,5},{5,6},{6,7},{7,8},{8,9},{9,10},{10,1... | collective-permute-start | bytes 24584 | tf_op jit(solution)/shard_map/ppermute | solution.py:43
  258.9 8.2 %collective-permute-start.9 = (bf16[2,80,128]{2,1,0:T(8,128)(2,1)S(1)}, bf16[2,80,128]{2,1,0:T(8,128)(2,1)S(1)}, u32[]{:S(2)}, u32[]{:S(2)}) collective-permute-start(bf16[2,80,128]{2,1,0:T(8,128)(2,1)S(1)} %get-tuple-element.22), channel_id=1, source_target_pairs={{16,0},{32,16},{48,32},{64,48},{80,64},{96,80},{112,96},{128,112},... | collective-permute-start | bytes 122888 | tf_op jit(solution)/shard_map/ppermute | solution.py:44
  262.2 8.3 %collective-permute-start.8 = (bf16[2,80,128]{2,1,0:T(8,128)(2,1)S(1)}, bf16[2,80,128]{2,1,0:T(8,128)(2,1)S(1)}, u32[]{:S(2)}, u32[]{:S(2)}) collective-permute-start(bf16[2,80,128]{2,1,0:T(8,128)(2,1)S(1)} %get-tuple-element.21), channel_id=1, source_target_pairs={{0,16},{16,32},{32,48},{48,64},{64,80},{80,96},{96,112},{112,128},... | collective-permute-start | bytes 122888 | tf_op jit(solution)/shard_map/ppermute | solution.py:43
  271.3 9.3 %collective-permute-start.11 = (bf16[16,2,128]{2,1,0:T(2,128)(2,1)S(1)}, bf16[16,2,128]{2,1,0:T(2,128)(2,1)S(1)}, u32[]{:S(2)}, u32[]{:S(2)}) collective-permute-start(bf16[16,2,128]{2,1,0:T(2,128)(2,1)S(1)} %get-tuple-element.16), channel_id=1, source_target_pairs={{1,0},{2,1},{3,2},{4,3},{5,4},{6,5},{7,6},{8,7},{9,8},{10,9},{11,1... | collective-permute-start | bytes 24584 | tf_op jit(solution)/shard_map/ppermute | solution.py:44
  273.2 7.4 %collective-permute-start.10 = (bf16[16,2,128]{2,1,0:T(2,128)(2,1)S(1)}, bf16[16,2,128]{2,1,0:T(2,128)(2,1)S(1)}, u32[]{:S(2)}, u32[]{:S(2)}) collective-permute-start(bf16[16,2,128]{2,1,0:T(2,128)(2,1)S(1)} %get-tuple-element.15), channel_id=1, source_target_pairs={{0,1},{1,2},{2,3},{3,4},{4,5},{5,6},{6,7},{7,8},{8,9},{9,10},{10,1... | collective-permute-start | bytes 24584 | tf_op jit(solution)/shard_map/ppermute | solution.py:43
  273.2 8.2 %collective-permute-start.13 = (bf16[2,80,128]{2,1,0:T(8,128)(2,1)S(1)}, bf16[2,80,128]{2,1,0:T(8,128)(2,1)S(1)}, u32[]{:S(2)}, u32[]{:S(2)}) collective-permute-start(bf16[2,80,128]{2,1,0:T(8,128)(2,1)S(1)} %get-tuple-element.18), channel_id=1, source_target_pairs={{16,0},{32,16},{48,32},{64,48},{80,64},{96,80},{112,96},{128,112},... | collective-permute-start | bytes 122888 | tf_op jit(solution)/shard_map/ppermute | solution.py:44
  278.1 8.3 %collective-permute-start.12 = (bf16[2,80,128]{2,1,0:T(8,128)(2,1)S(1)}, bf16[2,80,128]{2,1,0:T(8,128)(2,1)S(1)}, u32[]{:S(2)}, u32[]{:S(2)}) collective-permute-start(bf16[2,80,128]{2,1,0:T(8,128)(2,1)S(1)} %get-tuple-element.17), channel_id=1, source_target_pairs={{0,16},{16,32},{32,48},{48,64},{64,80},{80,96},{96,112},{112,128},... | collective-permute-start | bytes 122888 | tf_op jit(solution)/shard_map/ppermute | solution.py:43
  287.2 9.3 %collective-permute-start.15 = (bf16[16,2,128]{2,1,0:T(2,128)(2,1)S(1)}, bf16[16,2,128]{2,1,0:T(2,128)(2,1)S(1)}, u32[]{:S(2)}, u32[]{:S(2)}) collective-permute-start(bf16[16,2,128]{2,1,0:T(2,128)(2,1)S(1)} %get-tuple-element.12), channel_id=1, source_target_pairs={{1,0},{2,1},{3,2},{4,3},{5,4},{6,5},{7,6},{8,7},{9,8},{10,9},{11,1... | collective-permute-start | bytes 24584 | tf_op jit(solution)/shard_map/ppermute | solution.py:44
  289.1 7.4 %collective-permute-start.14 = (bf16[16,2,128]{2,1,0:T(2,128)(2,1)S(1)}, bf16[16,2,128]{2,1,0:T(2,128)(2,1)S(1)}, u32[]{:S(2)}, u32[]{:S(2)}) collective-permute-start(bf16[16,2,128]{2,1,0:T(2,128)(2,1)S(1)} %get-tuple-element.11), channel_id=1, source_target_pairs={{0,1},{1,2},{2,3},{3,4},{4,5},{5,6},{6,7},{7,8},{8,9},{9,10},{10,1... | collective-permute-start | bytes 24584 | tf_op jit(solution)/shard_map/ppermute | solution.py:43
  289.1 8.2 %collective-permute-start.17 = (bf16[2,80,128]{2,1,0:T(8,128)(2,1)S(1)}, bf16[2,80,128]{2,1,0:T(8,128)(2,1)S(1)}, u32[]{:S(2)}, u32[]{:S(2)}) collective-permute-start(bf16[2,80,128]{2,1,0:T(8,128)(2,1)S(1)} %get-tuple-element.14), channel_id=1, source_target_pairs={{16,0},{32,16},{48,32},{64,48},{80,64},{96,80},{112,96},{128,112},... | collective-permute-start | bytes 122888 | tf_op jit(solution)/shard_map/ppermute | solution.py:44
  294.4 8.3 %collective-permute-start.16 = (bf16[2,80,128]{2,1,0:T(8,128)(2,1)S(1)}, bf16[2,80,128]{2,1,0:T(8,128)(2,1)S(1)}, u32[]{:S(2)}, u32[]{:S(2)}) collective-permute-start(bf16[2,80,128]{2,1,0:T(8,128)(2,1)S(1)} %get-tuple-element.13), channel_id=1, source_target_pairs={{0,16},{16,32},{32,48},{48,64},{64,80},{80,96},{96,112},{112,128},... | collective-permute-start | bytes 122888 | tf_op jit(solution)/shard_map/ppermute | solution.py:43
  303.0 1.3 copy-start.1
Sparse Core Ops, SparseCore 0:
  157.9 38.2 all-gather.1
where the time goes:
time: 312 us; the launch traced here: 311 us
  blocking collectives  129 us (41%)
  waiting for transfers between devices  74.9 us (24%)
  starting transfers between devices  51.2 us (16%)
  local copies, waits for them, and re-layouts  18.7 us (6%)
  other arithmetic  16.8 us (5%)
  between operations  14 us (4%)
  matrix products  6.99 us (2%)
    all_to_all x1, blocking collectives, sum_at_owner(): lax.all_to_all(cut_along(array, dim, length), axis, 0, 0, tiled=True)  129 us
    all_gather x1, waiting for transfers between devices, per_device(): segment = lax.all_gather(latitude_modes, 'lat', axis=1, tiled=True)  37.5 us
    ppermute x8, starting transfers between devices, with_halo(): after = lax.ppermute(leading, axis, down)  22.4 us
    all_to_all x1, waiting for transfers between devices, per_device(): lax.all_to_all(gridded, 'wave', split_axis=0, concat_axis=2, tiled=True)  21.5 us
    ppermute x8, waiting for transfers between devices, with_halo(): before = lax.ppermute(last, axis, up)  15.9 us
    ppermute x8, starting transfers between devices, with_halo(): before = lax.ppermute(last, axis, up)  14.1 us
    all_to_all x1, starting transfers between devices, per_device(): lax.all_to_all(gridded, 'wave', split_axis=0, concat_axis=2, tiled=True)  9.8 us
  transfers between devices with their start and end apart: 20, of which 6 were waited for; matrix products, arithmetic and copies ran while one was open for 3% of the time, Pallas kernels for 0%

commit v1 on v0

v1 whole, which is shorter than its diff:
```python
import math

import jax
import jax.numpy as jnp
import numpy as np
from jax import lax
from jax.experimental import pallas as pl
from jax.experimental.pallas import tpu as pltpu
from jax.sharding import PartitionSpec as P

NW = 640
LEV = 128
STEPS = 4
NLON = 2 * NW
WAVE = 16
LAT = 16
ROWS = NW // WAVE
ORDERS = NW // LAT
LATS = 256
TILE_R = LATS // WAVE
TILE_X = NLON // LAT
HALO = 2 * STEPS
EXT_X = TILE_X + 2 * HALO
EXT_R = TILE_R + 2 * HALO
PAIRS = 5
SLOTS = 8
GROUP = 5
PAIR_OF = (((0, 0), (0, 1), (1, 0), (1, 1), (2, 0)), ((4, 0), (4, 1), (3, 0), (3, 1), (2, 1)))
ORDER_OF = ((0, 1, 2), (4, 3, 2))
ORDER_SLOT = (0, 0, 1, 1, 2)
R_STEP = 8


def vertical_kernel(info, control, vert, pick, out, scratch):
    step = pl.program_id(0)
    parts = jnp.dot(control[...], pick[...], preferred_element_type=jnp.float32)
    orders = info[ROWS] + lax.broadcasted_iota(jnp.int32, (ORDERS, 2 * LEV), 0)
    for i in range(R_STEP):
        r = step * R_STEP + i
        rows = jnp.where(info[r] >= orders, parts[i * ORDERS : (i + 1) * ORDERS], 0.0)
        both = jnp.concatenate([rows[:, :LEV], rows[:, LEV:]], axis=0).astype(jnp.bfloat16)
        mixed = lax.dot_general(
            both, vert[i], (((1,), (1,)), ((), ())), preferred_element_type=jnp.float32
        )
        for p in range(2):
            scratch[p, pl.ds(r, ORDERS, stride=ROWS), :] = mixed[p * ORDERS : (p + 1) * ORDERS]

    @pl.when(step == pl.num_programs(0) - 1)
    def _():
        for w in range(WAVE):
            for b in range(PAIRS):
                m, p = PAIR_OF[w % 2][b]
                m += GROUP * (w // 2)
                out[w, b] = scratch[p, m * ROWS : (m + 1) * ROWS, :].astype(jnp.bfloat16)


def vertical_parts(control, vert_root, row_wavenumber, first_order):
    info = jnp.concatenate([row_wavenumber, first_order[None]])
    pick = np.zeros((2 * LEV, 2 * LEV), np.float32)
    pick[np.arange(2 * LEV), np.arange(2 * LEV) % 2 * LEV + np.arange(2 * LEV) // 2] = 1.0
    return pl.pallas_call(
        vertical_kernel,
        grid=(ROWS // R_STEP,),
        in_specs=[
            pl.BlockSpec(memory_space=pltpu.SMEM),
            pl.BlockSpec((R_STEP * ORDERS, 2 * LEV), lambda i: (i, 0)),
            pl.BlockSpec((R_STEP, LEV, LEV), lambda i: (i, 0, 0)),
            pl.BlockSpec((2 * LEV, 2 * LEV), lambda i: (0, 0)),
        ],
        out_specs=pl.BlockSpec((WAVE, PAIRS, ROWS, LEV), lambda i: (0, 0, 0, 0)),
        out_shape=jax.ShapeDtypeStruct((WAVE, PAIRS, ROWS, LEV), jnp.bfloat16),
        scratch_shapes=[pltpu.VMEM((2, ORDERS * ROWS, LEV), jnp.float32)],
    )(info, control.reshape(ROWS * ORDERS, 2 * LEV), vert_root, jnp.asarray(pick, jnp.bfloat16))


def modes_kernel(vertical, legendre, out, left, right, result):
    result[...] = jnp.zeros(result.shape, jnp.float32)
    for slot in range(3):
        pairs = [b for b in range(PAIRS) if ORDER_SLOT[b] == slot]
        for s in range(WAVE):
            left[s * ROWS : (s + 1) * ROWS, :] = legendre[s, slot].astype(jnp.float32)
            for i, b in enumerate(pairs):
                right[s * ROWS : (s + 1) * ROWS, i * LEV : (i + 1) * LEV] = vertical[s, b].astype(
                    jnp.float32
                )
        width = len(pairs) * LEV
        total = lax.dot_general(
            left[...].astype(jnp.bfloat16),
            right[:, :width].astype(jnp.bfloat16),
            (((0,), (0,)), ((), ())),
            preferred_element_type=jnp.float32,
        )
        for i, b in enumerate(pairs):
            result[pl.ds(b, LATS, stride=SLOTS), :] = total[:, i * LEV : (i + 1) * LEV]
    out[...] = result[...].astype(jnp.bfloat16)


def modes_of(vertical, legendre):
    return pl.pallas_call(
        modes_kernel,
        out_shape=jax.ShapeDtypeStruct((LATS * SLOTS, LEV), jnp.bfloat16),
        scratch_shapes=[
            pltpu.VMEM((NW, LATS), jnp.float32),
            pltpu.VMEM((NW, 2 * LEV), jnp.float32),
            pltpu.VMEM((LATS * SLOTS, LEV), jnp.float32),
        ],
    )(vertical, legendre)


def fourier_basis():
    order = np.zeros((WAVE, LAT, SLOTS), np.int32)
    part = np.zeros((WAVE, LAT, SLOTS), np.int32)
    used = np.zeros((WAVE, LAT, SLOTS), np.float32)
    for w in range(WAVE):
        for b, (m, p) in enumerate(PAIR_OF[w % 2]):
            order[w, :, b] = np.arange(LAT) * ORDERS + GROUP * (w // 2) + m
            part[w, :, b] = p
            used[w, :, b] = 1.0
    order, part, used = (jnp.asarray(a.reshape(-1)) for a in (order, part, used))
    weight = used * jnp.where(order == 0, 1.0, 2.0).astype(jnp.float32) / math.sqrt(NLON)

    def turn(steps):
        return (steps % NLON).astype(jnp.float32) * (2.0 * math.pi / NLON)

    local = jnp.arange(EXT_X, dtype=jnp.int32) - HALO + NLON
    near = turn(order[None, :] * local[:, None] + part[None, :] * (NLON // 4))
    far = turn(order[None, :] * (TILE_X * jnp.arange(LAT, dtype=jnp.int32))[:, None])
    near_cos, near_sin = weight * jnp.cos(near), weight * jnp.sin(near)
    far_cos, far_sin = jnp.cos(far), jnp.sin(far)
    basis = far_cos[:, None, :] * near_cos[None] - far_sin[:, None, :] * near_sin[None]
    return basis.astype(jnp.bfloat16).reshape(LAT * EXT_X, -1)


def minmod(a, b):
    return jnp.maximum(0.0, jnp.minimum(a, b)) + jnp.minimum(0.0, jnp.maximum(a, b))


def shifted(array, amount):
    return pltpu.roll(array, amount % array.shape[0], 0)


def flux(wind, gain, low, high, low_slope, high_slope):
    forward = wind > 0.0
    return wind * jnp.where(forward, low, high) + gain * jnp.where(forward, low_slope, high_slope)


def advect_kernel(
    where, middle, south, north, ce, cn, ef, nf, west, east, wind_s, wind_n, out, qa, qb, us, gs
):
    band = where[0]
    qa[0:HALO] = south[...].astype(jnp.float32)
    qa[HALO : HALO + TILE_R] = middle[...].astype(jnp.float32)
    qa[HALO + TILE_R :] = north[...].astype(jnp.float32)
    qb[0:HALO] = jnp.zeros((HALO, EXT_X, LEV), jnp.float32)
    qb[HALO + TILE_R :] = jnp.zeros((HALO, EXT_X, LEV), jnp.float32)
    inner = slice(HALO, HALO + TILE_R)
    for d, (size, flag) in enumerate(((ce, ef), (cn, nf))):
        us[d, 0:HALO] = wind_s[d].astype(jnp.float32)
        us[d, HALO + TILE_R :] = wind_n[d].astype(jnp.float32)
        us[d, inner, 0:HALO] = west[d].astype(jnp.float32)
        us[d, inner, HALO + TILE_X :] = east[d].astype(jnp.float32)
        us[d, inner, HALO : HALO + TILE_X] = jnp.where(flag[...] > 0, size[...], -size[...])

    def gains(r, carry):
        for d in range(2):
            speed = jnp.abs(us[d, r])
            gs[d, r] = 0.5 * speed * (1.0 - speed)
        return carry

    lax.fori_loop(0, EXT_R, gains, 0)
    for t in range(1, STEPS + 1):
        old, new = (qa, qb) if t % 2 else (qb, qa)
        low = jnp.where(band == 0, HALO, 2 * t)
        high = jnp.where(band == WAVE - 1, HALO + TILE_R, EXT_R - 2 * t)

        def slope(r):
            here = old[r]
            return minmod(old[r + 1] - here, here - old[r - 1])

        def face(r, low_slope, high_slope):
            return flux(us[1, r], gs[1, r], old[r], old[r + 1], low_slope, high_slope)

        def row(r, carry):
            here_slope, below = carry
            here = old[r]
            next_slope = slope(r + 1)
            above = face(r, here_slope, next_slope)
            right = shifted(here, -1)
            jump = right - here
            steep = minmod(jump, shifted(jump, 1))
            east_face = flux(us[0, r], gs[0, r], here, right, steep, shifted(steep, -1))
            fresh = here - (east_face - shifted(east_face, 1)) - (above - below)
            if t == STEPS:
                out[r - HALO] = fresh[HALO : HALO + TILE_X]
            else:
                new[r] = fresh
            return next_slope, above

        first = slope(low)
        lax.fori_loop(low, high, row, (first, face(low - 1, slope(low - 1), first)))


def advected(band, middle, south, north, winds, halos):
    return pl.pallas_call(
        advect_kernel,
        in_specs=[pl.BlockSpec(memory_space=pltpu.SMEM)]
        + [pl.BlockSpec(memory_space=pltpu.VMEM)] * 11,
        out_shape=jax.ShapeDtypeStruct((TILE_R, TILE_X, LEV), jnp.float32),
        scratch_shapes=[
            pltpu.VMEM((EXT_R, EXT_X, LEV), jnp.float32),
            pltpu.VMEM((EXT_R, EXT_X, LEV), jnp.float32),
            pltpu.VMEM((2, EXT_R, EXT_X, LEV), jnp.float32),
            pltpu.VMEM((2, EXT_R, EXT_X, LEV), jnp.float32),
        ],
    )(band[None], middle, south, north, *winds, *halos)


def from_below(block, axis, wrap):
    pairs = [(i, (i + 1) % 16) for i in range(16 if wrap else 15)]
    return lax.ppermute(block, axis, pairs)


def from_above(block, axis, wrap):
    pairs = [((i + 1) % 16, i) for i in range(16 if wrap else 15)]
    return lax.ppermute(block, axis, pairs)


def per_device(
    control,
    vert_root,
    legendre,
    row_wavenumber,
    courant_east,
    courant_north,
    east_flags,
    north_flags,
):
    lat = lax.axis_index("lat").astype(jnp.int32)
    wave = lax.axis_index("wave").astype(jnp.int32)
    groups = legendre.reshape(WAVE // 2, GROUP, ROWS, LATS)
    legendre_out = jnp.stack(
        [jnp.stack([groups[:, m] for m in orders], axis=1) for orders in ORDER_OF], axis=1
    ).reshape(WAVE, 3, ROWS, LATS)
    legendre_in = lax.all_to_all(legendre_out, "wave", 0, 0, tiled=True)
    vertical_out = vertical_parts(control, vert_root, row_wavenumber, lat * ORDERS)
    vertical_in = lax.all_to_all(vertical_out, "wave", 0, 0, tiled=True)

    winds = jnp.stack(
        [
            jnp.where(flag > 0, size, -size).astype(jnp.bfloat16)
            for size, flag in ((courant_east, east_flags), (courant_north, north_flags))
        ]
    )
    west = from_below(winds[:, :, -HALO:], "lat", True)
    east = from_above(winds[:, :, :HALO], "lat", True)
    wide = jnp.concatenate([west, winds, east], axis=2)

    modes = modes_of(vertical_in, legendre_in).reshape(LATS, SLOTS, LEV)
    modes = lax.all_to_all(modes, ("wave", "lat"), 0, 0, tiled=True)
    wind_s = from_below(wide[:, -HALO:], "wave", False)
    wind_n = from_above(wide[:, :HALO], "wave", False)
    row = jnp.dot(
        fourier_basis(), modes.reshape(LATS * SLOTS, LEV), preferred_element_type=jnp.float32
    ).astype(jnp.bfloat16)
    middle = lax.all_to_all(row.reshape(LAT, EXT_X, LEV), "lat", 0, 0, tiled=True)
    south = from_below(middle[-HALO:], "wave", False)
    north = from_above(middle[:HALO], "wave", False)
    return advected(
        wave,
        middle,
        south,
        north,
        (courant_east, courant_north, east_flags, north_flags),
        (west, east, wind_s, wind_n),
    )


def solution(mesh):
    return jax.shard_map(
        per_device,
        mesh=mesh,
        in_specs=(
            P("wave", "lat", None),
            P("wave", None, None),
            P("lat", "wave", None),
            P("wave"),
            P("wave", "lat", None),
            P("wave", "lat", None),
            P("wave", "lat", None),
            P("wave", "lat", None),
        ),
        out_specs=P("wave", "lat", None),
        check_vma=False,
    )
```

time: 312 us -> 160 us (0.51)
  blocking collectives: 129 us -> 0 us
  Pallas kernels: 0 us -> 18.5 us
  local copies, waits for them, and re-layouts: 18.7 us -> 2.85 us
  between operations: 14 us -> 0.26 us
  waiting for transfers between devices: 74.9 us -> 65.9 us
    all_to_all x1 -> x0, blocking collectives: 129 us -> none  [sum_at_owner(): lax.all_to_all(cut_along(array, dim, length), axis, 0, 0, tiled=True)]
    all_gather x1 -> x0, waiting for transfers between devices: 37.5 us -> none  [per_device(): segment = lax.all_gather(latitude_modes, 'lat', axis=1, tiled=True)]
    all_to_all x1 -> x4, waiting for transfers between devices: 21.5 us -> 49.6 us  [the longest x1 19.8 us: per_device(): vertical_in = lax.all_to_all(vertical_out, 'wave', 0, 0, tiled=True)]
    ppermute x18 -> x6, starting transfers between devices: 41.4 us -> 20.3 us  [the longest x3 14.6 us: from_above(): return lax.ppermute(block, axis, pairs)]
    all_to_all x1 -> x4, starting transfers between devices: 9.8 us -> 30.1 us  [the longest x1 10.9 us: per_device(): vertical_in = lax.all_to_all(vertical_out, 'wave', 0, 0, tiled=True)]
    pallas_call x0 -> x3, Pallas kernels: none -> 18.5 us  [the longest x1 10.2 us: advected(): pl.pallas_call(advect_kernel, in_specs=[pl.BlockSpec(memory_space=pltpu.S...]
    convert_element_type x1 -> x0, local copies, waits for them, and re-layouts: 5.77 us -> none  [per_device(): vertical = jnp.einsum('rmlp,rkl->kpmr', complex_parts, vert_root, preferr...]
    all_gather x1 -> x0, local copies, waits for them, and re-layouts: 4.34 us -> none  [per_device(): segment = lax.all_gather(latitude_modes, 'lat', axis=1, tiled=True)]
  transfers between devices with their start and end apart: 20 -> 10, of which waited for: 6 -> 8; matrix products, arithmetic and copies ran while one was open for 3% -> 12% of each run, Pallas kernels for 0% -> 2%
where the time goes in v1:
time: 160 us; the launch traced here: 158 us
  waiting for transfers between devices  65.9 us (41%)
  starting transfers between devices  50.4 us (32%)
  Pallas kernels  18.5 us (12%)
  other arithmetic  14.5 us (9%)
  matrix products  5.4 us (3%)
  local copies, waits for them, and re-layouts  2.85 us (2%)
    all_to_all x1, waiting for transfers between devices, per_device(): vertical_in = lax.all_to_all(vertical_out, 'wave', 0, 0, tiled=True)  19.8 us
    all_to_all x1, waiting for transfers between devices, per_device(): legendre_in = lax.all_to_all(legendre_out, 'wave', 0, 0, tiled=True)  16.3 us
    ppermute x3, starting transfers between devices, from_above(): return lax.ppermute(block, axis, pairs)  14.6 us
    all_to_all x1, waiting for transfers between devices, per_device(): modes = lax.all_to_all(modes, ('wave', 'lat'), 0, 0, tiled=True)  12.9 us
    ppermute x3, waiting for transfers between devices, from_below(): return lax.ppermute(block, axis, pairs)  12.4 us
    all_to_all x1, starting transfers between devices, per_device(): vertical_in = lax.all_to_all(vertical_out, 'wave', 0, 0, tiled=True)  10.9 us
    pallas_call x1, Pallas kernels, advected(): pl.pallas_call(advect_kernel, in_specs=[pl.BlockSpec(memory_space=pltpu.S...  10.2 us
    all_to_all x1, starting transfers between devices, per_device(): modes = lax.all_to_all(modes, ('wave', 'lat'), 0, 0, tiled=True)  9.85 us
  transfers between devices with their start and end apart: 10, of which 8 were waited for; matrix products, arithmetic and copies ran while one was open for 12% of the time, Pallas kernels for 2%

profile of v1, /device:TPU:64, one launch (start us, length us, event | category | flops | bytes accessed | tf_op | source)
XLA Modules:
  0.0 157.8 jit_solution(15717445615686675189)
XLA Ops:
  0.0 1.4 pad_add_fusion.info
  1.4 5.5 %shard_map.118 = bf16[16,5,40,128]{3,2,1,0:T(8,128)(2,1)} custom-call(s32[41]{0:T(128)} %pad_add_fusion.info, bf16[1600,256]{1,0:T(8,128)(2,1)} %bitcast.26, bf16[40,128,128]{2,1,0:T(8,128)(2,1)} %vert.1, bf16[256,256]{1,0:T(8,128)(2,1)} %constant.56.clone.pick), custom_call_target="tpu_custom_call" | custom-call | tf_op jit(solution)/shard_map/pallas_call | solution.py:61
  6.9 10.9 %all-to-all-start = ((bf16[16,5,40,128]{3,2,1,0:T(8,128)(2,1)}), bf16[16,5,40,128]{3,2,1,0:T(8,128)(2,1)S(1)}, u32[]{:S(2)}, u32[]{:S(2)}) async-start(bf16[16,5,40,128]{3,2,1,0:T(8,128)(2,1)} %shard_map.118), calls=%async_computation | async-start | bytes 1638400 | tf_op jit(solution)/shard_map/all_to_all | solution.py:246
  21.1 19.8 %all-to-all-done.vertical = bf16[16,5,40,128]{3,2,1,0:T(8,128)(2,1)S(1)} async-done(((bf16[16,5,40,128]{3,2,1,0:T(8,128)(2,1)}), bf16[16,5,40,128]{3,2,1,0:T(8,128)(2,1)S(1)}, u32[]{:S(2)}, u32[]{:S(2)}) %all-to-all-start) | async-done | bytes 819232 | tf_op jit(solution)/shard_map/all_to_all | solution.py:246
  40.9 5.7 %all-to-all-start.1 = ((bf16[16,3,40,256]{3,2,1,0:T(8,128)(2,1)}), bf16[16,3,40,256]{3,2,1,0:T(8,128)(2,1)S(1)}, u32[]{:S(2)}, u32[]{:S(2)}) async-start(bf16[16,3,40,256]{3,2,1,0:T(8,128)(2,1)} %bitcast.8), calls=%async_computation.1 | async-start | bytes 1966080 | tf_op jit(solution)/shard_map/all_to_all | solution.py:244
  46.7 1.5 fusion.8
  48.9 3.9 %collective-permute-start.3 = (bf16[2,16,8,128]{3,2,1,0:T(8,128)(2,1)}, bf16[2,16,8,128]{3,2,1,0:T(8,128)(2,1)S(1)}, u32[]{:S(2)}, u32[]{:S(2)}) collective-permute-start(bf16[2,16,8,128]{3,2,1,0:T(8,128)(2,1)} %get-tuple-element.10), channel_id=1, source_target_pairs={{1,0},{2,1},{3,2},{4,3},{5,4},{6,5},{7,6},{8,7},{9,8},{10,9},{11,1... | collective-permute-start | bytes 196616 | tf_op jit(solution)/shard_map/ppermute | solution.py:225
  52.8 3.3 %cosine_multiply_fusion = (f32[96,2048]{1,0:T(8,128)S(1)}, f32[96,2048]{1,0:T(8,128)S(1)}) fusion(s32[2048]{0:T(1024)S(1)} %copy-done.17, s32[96]{0:T(128)S(1)} %iota_add_fusion, s32[2048]{0:T(1024)S(1)} %copy-done.15, f32[2048]{0:T(1024)S(1)} %copy-done.16), kind=kLoop, calls=%fused_computation.10 | loop fusion | flops 2359296 | bytes 1597824 | tf_op jit(solution)/shard_map/mul | solution.py:128
  56.1 16.3 %all-to-all-done.1.legendre = bf16[16,3,40,256]{3,2,1,0:T(8,128)(2,1)S(1)} async-done(((bf16[16,3,40,256]{3,2,1,0:T(8,128)(2,1)}), bf16[16,3,40,256]{3,2,1,0:T(8,128)(2,1)S(1)}, u32[]{:S(2)}, u32[]{:S(2)}) %all-to-all-start.1) | async-done | bytes 983072 | tf_op jit(solution)/shard_map/all_to_all | solution.py:244
  73.3 2.8 %shard_map.119 = bf16[2048,128]{1,0:T(8,128)(2,1)} custom-call(bf16[16,5,40,128]{3,2,1,0:T(8,128)(2,1)} %copy-done.2, bf16[16,3,40,256]{3,2,1,0:T(8,128)(2,1)} %copy-done), custom_call_target="tpu_custom_call" | custom-call | tf_op jit(solution)/shard_map/pallas_call | solution.py:99
  76.1 9.9 %all-to-all-start.2 = ((bf16[256,8,128]{2,1,0:T(8,128)(2,1)}), bf16[256,8,128]{2,1,0:T(8,128)(2,1)}, u32[]{:S(2)}, u32[]{:S(2)}) async-start(bf16[256,8,128]{2,1,0:T(8,128)(2,1)} %bitcast.23), calls=%async_computation.2 | async-start | bytes 1048576 | tf_op jit(solution)/shard_map/all_to_all | solution.py:259
  86.6 4.8 %subtract_convert_fusion = bf16[16,96,2048]{2,1,0:T(8,128)(2,1)} fusion(f32[96,2048]{1,0:T(8,128)S(1)} %get-tuple-element.15, f32[16,2048]{1,0:T(8,128)S(1)} %get-tuple-element.17, f32[96,2048]{1,0:T(8,128)S(1)} %get-tuple-element.14, f32[16,2048]{1,0:T(8,128)S(1)} %get-tuple-element.16), kind=kLoop, calls=%fused_computation | loop fusion | flops 12582912 | bytes 8126464 | tf_op jit(solution)/shard_map/convert_element_type | solution.py:131
  91.4 12.9 %all-to-all-done.2 = bf16[256,8,128]{2,1,0:T(8,128)(2,1)} async-done(((bf16[256,8,128]{2,1,0:T(8,128)(2,1)}), bf16[256,8,128]{2,1,0:T(8,128)(2,1)}, u32[]{:S(2)}, u32[]{:S(2)}) %all-to-all-start.2) | async-done | bytes 524320 | tf_op jit(solution)/shard_map/all_to_all | solution.py:259
  104.3 5.4 %convolution_convert_fusion = bf16[1536,128]{1,0:T(8,128)(2,1)} fusion(bf16[1536,2048]{1,0:T(8,128)(2,1)} %bitcast.22, bf16[256,8,128]{2,1,0:T(8,128)(2,1)} %all-to-all-done.2), kind=kOutput, calls=%fused_computation.1 | convolution fusion | flops 805502976 | bytes 7208960 | tf_op jit(solution)/shard_map/dot_general | solution.py:262
  109.7 3.6 %all-to-all-start.3 = ((bf16[16,96,128]{2,1,0:T(8,128)(2,1)}), bf16[16,96,128]{2,1,0:T(8,128)(2,1)S(1)}, u32[]{:S(2)}, u32[]{:S(2)}) async-start(bf16[16,96,128]{2,1,0:T(8,128)(2,1)} %bitcast.11), calls=%async_computation.3 | async-start | bytes 786432 | tf_op jit(solution)/shard_map/all_to_all | solution.py:265
  113.4 2.7 %collective-permute-start.4 = (bf16[2,8,96,128]{3,2,1,0:T(8,128)(2,1)S(1)}, bf16[2,8,96,128]{3,2,1,0:T(8,128)(2,1)S(1)}, u32[]{:S(2)}, u32[]{:S(2)}) collective-permute-start(bf16[2,8,96,128]{3,2,1,0:T(8,128)(2,1)S(1)} %get-tuple-element.9), channel_id=1, source_target_pairs={{0,16},{16,32},{32,48},{48,64},{64,80},{80,96},{96,112},{112,128},... | collective-permute-start | bytes 1179656 | tf_op jit(solution)/shard_map/ppermute | solution.py:220
  116.2 5.5 %collective-permute-start.5 = (bf16[2,8,96,128]{3,2,1,0:T(8,128)(2,1)S(1)}, bf16[2,8,96,128]{3,2,1,0:T(8,128)(2,1)S(1)}, u32[]{:S(2)}, u32[]{:S(2)}) collective-permute-start(bf16[2,8,96,128]{3,2,1,0:T(8,128)(2,1)S(1)} %get-tuple-element.8), channel_id=1, source_target_pairs={{16,0},{32,16},{48,32},{64,48},{80,64},{96,80},{112,96},{128,112},... | collective-permute-start | bytes 1179656 | tf_op jit(solution)/shard_map/ppermute | solution.py:225
  122.4 3.0 %collective-permute-start = (bf16[8,96,128]{2,1,0:T(8,128)(2,1)S(1)}, bf16[8,96,128]{2,1,0:T(8,128)(2,1)S(1)}, u32[]{:S(2)}, u32[]{:S(2)}) collective-permute-start(bf16[8,96,128]{2,1,0:T(8,128)(2,1)S(1)} %get-tuple-element.13), channel_id=1, source_target_pairs={{0,16},{16,32},{32,48},{48,64},{64,80},{80,96},{96,112},{112,128},... | collective-permute-start | bytes 589832 | tf_op jit(solution)/shard_map/ppermute | solution.py:220
  125.4 5.2 %collective-permute-start.1 = (bf16[8,96,128]{2,1,0:T(8,128)(2,1)S(1)}, bf16[8,96,128]{2,1,0:T(8,128)(2,1)S(1)}, u32[]{:S(2)}, u32[]{:S(2)}) collective-permute-start(bf16[8,96,128]{2,1,0:T(8,128)(2,1)S(1)} %get-tuple-element.12), channel_id=1, source_target_pairs={{16,0},{32,16},{48,32},{64,48},{80,64},{96,80},{112,96},{128,112},... | collective-permute-start | bytes 589832 | tf_op jit(solution)/shard_map/ppermute | solution.py:225
  130.6 10.3 %collective-permute-done.4.wind_s = bf16[2,8,96,128]{3,2,1,0:T(8,128)(2,1)S(1)} collective-permute-done((bf16[2,8,96,128]{3,2,1,0:T(8,128)(2,1)S(1)}, bf16[2,8,96,128]{3,2,1,0:T(8,128)(2,1)S(1)}, u32[]{:S(2)}, u32[]{:S(2)}) %collective-permute-start.4) | collective-permute-done | bytes 393248 | tf_op jit(solution)/shard_map/ppermute | solution.py:220
  141.0 1.8 %collective-permute-done.5.wind_n = bf16[2,8,96,128]{3,2,1,0:T(8,128)(2,1)S(1)} collective-permute-done((bf16[2,8,96,128]{3,2,1,0:T(8,128)(2,1)S(1)}, bf16[2,8,96,128]{3,2,1,0:T(8,128)(2,1)S(1)}, u32[]{:S(2)}, u32[]{:S(2)}) %collective-permute-start.5) | collective-permute-done | bytes 393248 | tf_op jit(solution)/shard_map/ppermute | solution.py:225
  142.8 2.1 %collective-permute-done.south = bf16[8,96,128]{2,1,0:T(8,128)(2,1)S(1)} collective-permute-done((bf16[8,96,128]{2,1,0:T(8,128)(2,1)S(1)}, bf16[8,96,128]{2,1,0:T(8,128)(2,1)S(1)}, u32[]{:S(2)}, u32[]{:S(2)}) %collective-permute-start) | collective-permute-done | bytes 196640 | tf_op jit(solution)/shard_map/ppermute | solution.py:220
  144.9 2.1 %collective-permute-done.1.north = bf16[8,96,128]{2,1,0:T(8,128)(2,1)S(1)} collective-permute-done((bf16[8,96,128]{2,1,0:T(8,128)(2,1)S(1)}, bf16[8,96,128]{2,1,0:T(8,128)(2,1)S(1)}, u32[]{:S(2)}, u32[]{:S(2)}) %collective-permute-start.1) | collective-permute-done | bytes 196640 | tf_op jit(solution)/shard_map/ppermute | solution.py:225
  147.6 10.2 %shard_map.120 = f32[16,80,128]{2,1,0:T(8,128)} custom-call(s32[1]{0:T(128)} %bitcast.where, bf16[16,96,128]{2,1,0:T(8,128)(2,1)} %copy-done.1, bf16[8,96,128]{2,1,0:T(8,128)(2,1)} %copy-done.13, bf16[8,96,128]{2,1,0:T(8,128)(2,1)} %copy-done.14, f32[16,80,128]{2,1,0:T(8,128)} %ce.1, f32[16,80,128]{2,1,0:T(8,128)} %cn.1, s32[16,80,128]{2,1,0:T(8,128)} %ef.1, ...), custom_call_target="tpu_custom_call" | custom-call | tf_op jit(solution)/shard_map/pallas_call | solution.py:204
  (50 shorter events, 7.1 us)
Async XLA Ops:
  0.0 46.6 %copy-start.7 = (f32[16,80,128]{2,1,0:T(8,128)S(1)}, f32[16,80,128]{2,1,0:T(8,128)}, u32[]{:S(2)}) copy-start(f32[16,80,128]{2,1,0:T(8,128)} %ce.1) | copy-start | bytes 1966084
  0.0 46.6 %copy-start.8 = (f32[16,80,128]{2,1,0:T(8,128)S(1)}, f32[16,80,128]{2,1,0:T(8,128)}, u32[]{:S(2)}) copy-start(f32[16,80,128]{2,1,0:T(8,128)} %cn.1) | copy-start | bytes 1966084
  6.9 45.9 %copy-start.15 = (s32[2048]{0:T(1024)S(1)}, s32[2048]{0:T(1024)}, u32[]{:S(2)}) copy-start(s32[2048]{0:T(1024)} %constant.57.clone) | copy-start | bytes 24580
  6.9 45.9 %copy-start.16 = (f32[2048]{0:T(1024)S(1)}, f32[2048]{0:T(1024)}, u32[]{:S(2)}) copy-start(f32[2048]{0:T(1024)} %constant.67) | copy-start | bytes 24580
  6.9 45.9 %copy-start.17 = (s32[2048]{0:T(1024)S(1)}, s32[2048]{0:T(1024)}, u32[]{:S(2)}) copy-start(s32[2048]{0:T(1024)} %constant.68) | copy-start | bytes 24580
  6.9 34.0 %all-to-all-start = ((bf16[16,5,40,128]{3,2,1,0:T(8,128)(2,1)}), bf16[16,5,40,128]{3,2,1,0:T(8,128)(2,1)S(1)}, u32[]{:S(2)}, u32[]{:S(2)}) async-start(bf16[16,5,40,128]{3,2,1,0:T(8,128)(2,1)} %shard_map.118), calls=%async_computation | async-start | bytes 1638400 | tf_op jit(solution)/shard_map/all_to_all | solution.py:246
  40.9 31.5 %copy-start.2 = (bf16[16,5,40,128]{3,2,1,0:T(8,128)(2,1)}, bf16[16,5,40,128]{3,2,1,0:T(8,128)(2,1)S(1)}, u32[]{:S(2)}) copy-start(bf16[16,5,40,128]{3,2,1,0:T(8,128)(2,1)S(1)} %all-to-all-done.vertical) | copy-start | bytes 2457604
  40.9 31.5 %all-to-all-start.1 = ((bf16[16,3,40,256]{3,2,1,0:T(8,128)(2,1)}), bf16[16,3,40,256]{3,2,1,0:T(8,128)(2,1)S(1)}, u32[]{:S(2)}, u32[]{:S(2)}) async-start(bf16[16,3,40,256]{3,2,1,0:T(8,128)(2,1)} %bitcast.8), calls=%async_computation.1 | async-start | bytes 1966080 | tf_op jit(solution)/shard_map/all_to_all | solution.py:244
  48.1 4.6 %copy-start.3 = (bf16[1,16,80,128]{3,2,1,0:T(8,128)(2,1)}, bf16[1,16,80,128]{3,2,1,0:T(8,128)(2,1)S(1)}, u32[]{:S(2)}) copy-start(bf16[1,16,80,128]{3,2,1,0:T(8,128)(2,1)S(1)} %get-tuple-element.20) | copy-start | bytes 983044
  48.1 4.6 %copy-start.5 = (bf16[1,16,80,128]{3,2,1,0:T(8,128)(2,1)}, bf16[1,16,80,128]{3,2,1,0:T(8,128)(2,1)S(1)}, u32[]{:S(2)}) copy-start(bf16[1,16,80,128]{3,2,1,0:T(8,128)(2,1)S(1)} %get-tuple-element.21) | copy-start | bytes 983044
  48.9 64.4 %collective-permute-start.2 = (bf16[2,16,8,128]{3,2,1,0:T(8,128)(2,1)}, bf16[2,16,8,128]{3,2,1,0:T(8,128)(2,1)S(1)}, u32[]{:S(2)}, u32[]{:S(2)}) collective-permute-start(bf16[2,16,8,128]{3,2,1,0:T(8,128)(2,1)} %get-tuple-element.11), channel_id=1, source_target_pairs={{0,1},{1,2},{2,3},{3,4},{4,5},{5,6},{6,7},{7,8},{8,9},{9,10},{10,1... | collective-permute-start | bytes 196616 | tf_op jit(solution)/shard_map/ppermute | solution.py:220
  48.9 64.4 %collective-permute-start.3 = (bf16[2,16,8,128]{3,2,1,0:T(8,128)(2,1)}, bf16[2,16,8,128]{3,2,1,0:T(8,128)(2,1)S(1)}, u32[]{:S(2)}, u32[]{:S(2)}) collective-permute-start(bf16[2,16,8,128]{3,2,1,0:T(8,128)(2,1)} %get-tuple-element.10), channel_id=1, source_target_pairs={{1,0},{2,1},{3,2},{4,3},{5,4},{6,5},{7,6},{8,7},{9,8},{10,9},{11,1... | collective-permute-start | bytes 196616 | tf_op jit(solution)/shard_map/ppermute | solution.py:225
  76.1 28.2 %all-to-all-start.2 = ((bf16[256,8,128]{2,1,0:T(8,128)(2,1)}), bf16[256,8,128]{2,1,0:T(8,128)(2,1)}, u32[]{:S(2)}, u32[]{:S(2)}) async-start(bf16[256,8,128]{2,1,0:T(8,128)(2,1)} %bitcast.23), calls=%async_computation.2 | async-start | bytes 1048576 | tf_op jit(solution)/shard_map/all_to_all | solution.py:259
  86.6 26.7 %copy-start.4 = (bf16[1,16,80,128]{3,2,1,0:T(8,128)(2,1)S(1)}, bf16[1,16,80,128]{3,2,1,0:T(8,128)(2,1)}, u32[]{:S(2)}) copy-start(bf16[1,16,80,128]{3,2,1,0:T(8,128)(2,1)} %copy-done.3) | copy-start | bytes 983044
  86.6 26.7 %copy-start.6 = (bf16[1,16,80,128]{3,2,1,0:T(8,128)(2,1)S(1)}, bf16[1,16,80,128]{3,2,1,0:T(8,128)(2,1)}, u32[]{:S(2)}) copy-start(bf16[1,16,80,128]{3,2,1,0:T(8,128)(2,1)} %copy-done.5) | copy-start | bytes 983044
  109.7 12.6 %all-to-all-start.3 = ((bf16[16,96,128]{2,1,0:T(8,128)(2,1)}), bf16[16,96,128]{2,1,0:T(8,128)(2,1)S(1)}, u32[]{:S(2)}, u32[]{:S(2)}) async-start(bf16[16,96,128]{2,1,0:T(8,128)(2,1)} %bitcast.11), calls=%async_computation.3 | async-start | bytes 786432 | tf_op jit(solution)/shard_map/all_to_all | solution.py:265
  113.3 33.7 %copy-start.11 = (bf16[2,16,8,128]{3,2,1,0:T(8,128)(2,1)}, bf16[2,16,8,128]{3,2,1,0:T(8,128)(2,1)S(1)}, u32[]{:S(2)}) copy-start(bf16[2,16,8,128]{3,2,1,0:T(8,128)(2,1)S(1)} %collective-permute-done.2.west) | copy-start | bytes 196612
  113.3 33.6 %copy-start.12 = (bf16[2,16,8,128]{3,2,1,0:T(8,128)(2,1)}, bf16[2,16,8,128]{3,2,1,0:T(8,128)(2,1)S(1)}, u32[]{:S(2)}) copy-start(bf16[2,16,8,128]{3,2,1,0:T(8,128)(2,1)S(1)} %collective-permute-done.3.east) | copy-start | bytes 196612
  113.4 27.5 %collective-permute-start.4 = (bf16[2,8,96,128]{3,2,1,0:T(8,128)(2,1)S(1)}, bf16[2,8,96,128]{3,2,1,0:T(8,128)(2,1)S(1)}, u32[]{:S(2)}, u32[]{:S(2)}) collective-permute-start(bf16[2,8,96,128]{3,2,1,0:T(8,128)(2,1)S(1)} %get-tuple-element.9), channel_id=1, source_target_pairs={{0,16},{16,32},{32,48},{48,64},{64,80},{80,96},{96,112},{112,128},... | collective-permute-start | bytes 1179656 | tf_op jit(solution)/shard_map/ppermute | solution.py:220
  116.2 26.6 %collective-permute-start.5 = (bf16[2,8,96,128]{3,2,1,0:T(8,128)(2,1)S(1)}, bf16[2,8,96,128]{3,2,1,0:T(8,128)(2,1)S(1)}, u32[]{:S(2)}, u32[]{:S(2)}) collective-permute-start(bf16[2,8,96,128]{3,2,1,0:T(8,128)(2,1)S(1)} %get-tuple-element.8), channel_id=1, source_target_pairs={{16,0},{32,16},{48,32},{64,48},{80,64},{96,80},{112,96},{128,112},... | collective-permute-start | bytes 1179656 | tf_op jit(solution)/shard_map/ppermute | solution.py:225
  122.3 24.6 %copy-start.1 = (bf16[16,96,128]{2,1,0:T(8,128)(2,1)}, bf16[16,96,128]{2,1,0:T(8,128)(2,1)S(1)}, u32[]{:S(2)}) copy-start(bf16[16,96,128]{2,1,0:T(8,128)(2,1)S(1)} %all-to-all-done.3.middle) | copy-start | bytes 1179652
  122.4 22.5 %collective-permute-start = (bf16[8,96,128]{2,1,0:T(8,128)(2,1)S(1)}, bf16[8,96,128]{2,1,0:T(8,128)(2,1)S(1)}, u32[]{:S(2)}, u32[]{:S(2)}) collective-permute-start(bf16[8,96,128]{2,1,0:T(8,128)(2,1)S(1)} %get-tuple-element.13), channel_id=1, source_target_pairs={{0,16},{16,32},{32,48},{48,64},{64,80},{80,96},{96,112},{112,128},... | collective-permute-start | bytes 589832 | tf_op jit(solution)/shard_map/ppermute | solution.py:220
  125.4 21.5 %collective-permute-start.1 = (bf16[8,96,128]{2,1,0:T(8,128)(2,1)S(1)}, bf16[8,96,128]{2,1,0:T(8,128)(2,1)S(1)}, u32[]{:S(2)}, u32[]{:S(2)}) collective-permute-start(bf16[8,96,128]{2,1,0:T(8,128)(2,1)S(1)} %get-tuple-element.12), channel_id=1, source_target_pairs={{16,0},{32,16},{48,32},{64,48},{80,64},{96,80},{112,96},{128,112},... | collective-permute-start | bytes 589832 | tf_op jit(solution)/shard_map/ppermute | solution.py:225
  140.9 6.0 %copy-start.9 = (bf16[2,8,96,128]{3,2,1,0:T(8,128)(2,1)}, bf16[2,8,96,128]{3,2,1,0:T(8,128)(2,1)S(1)}, u32[]{:S(2)}) copy-start(bf16[2,8,96,128]{3,2,1,0:T(8,128)(2,1)S(1)} %collective-permute-done.4.wind_s) | copy-start | bytes 1179652
  (4 other events, 7.9 us)

commit v2 on v1

--- a/solution.py
+++ b/solution.py
@@ -26,18 +26,34 @@
 SLOTS = 8
 GROUP = 5
 PAIR_OF = (((0, 0), (0, 1), (1, 0), (1, 1), (2, 0)), ((4, 0), (4, 1), (3, 0), (3, 1), (2, 1)))
-ORDER_OF = ((0, 1, 2), (4, 3, 2))
 ORDER_SLOT = (0, 0, 1, 1, 2)
 R_STEP = 8
-
-
-def vertical_kernel(info, control, vert, pick, out, scratch):
+BLOCKS = PAIRS + 6
+PARAMS = pltpu.CompilerParams(vmem_limit_bytes=24 * 1024 * 1024)
+
+
+def packing_kernel(wavenumber, first, control, vert, pick, legendre, out, scratch):
     step = pl.program_id(0)
+    for i in range(R_STEP):
+        m = step * R_STEP + i
+        z = m // GROUP
+        place = m - GROUP * z
+        late = place > 2
+        w = 2 * z + jnp.where(late, 1, 0)
+        slot = PAIRS + 2 * jnp.where(late, GROUP - 1 - place, place)
+        for h in range(2):
+            half = legendre[i, :, h * LEV : (h + 1) * LEV]
+            out[w, slot + h] = half
+
+            @pl.when(place == 2)
+            def _():
+                out[w + 1, slot + h] = half
+
     parts = jnp.dot(control[...], pick[...], preferred_element_type=jnp.float32)
-    orders = info[ROWS] + lax.broadcasted_iota(jnp.int32, (ORDERS, 2 * LEV), 0)
+    orders = first[0] + lax.broadcasted_iota(jnp.int32, (ORDERS, 2 * LEV), 0)
     for i in range(R_STEP):
         r = step * R_STEP + i
-        rows = jnp.where(info[r] >= orders, parts[i * ORDERS : (i + 1) * ORDERS], 0.0)
+        rows = jnp.where(wavenumber[r] >= orders, parts[i * ORDERS : (i + 1) * ORDERS], 0.0)
         both = jnp.concatenate([rows[:, :LEV], rows[:, LEV:]], axis=0).astype(jnp.bfloat16)
         mixed = lax.dot_general(
             both, vert[i], (((1,), (1,)), ((), ())), preferred_element_type=jnp.float32
@@ -54,35 +70,44 @@
                 out[w, b] = scratch[p, m * ROWS : (m + 1) * ROWS, :].astype(jnp.bfloat16)
 
 
-def vertical_parts(control, vert_root, row_wavenumber, first_order):
-    info = jnp.concatenate([row_wavenumber, first_order[None]])
+def packed_inputs(control, vert_root, legendre, row_wavenumber, first_order):
     pick = np.zeros((2 * LEV, 2 * LEV), np.float32)
     pick[np.arange(2 * LEV), np.arange(2 * LEV) % 2 * LEV + np.arange(2 * LEV) // 2] = 1.0
     return pl.pallas_call(
-        vertical_kernel,
+        packing_kernel,
         grid=(ROWS // R_STEP,),
         in_specs=[
+            pl.BlockSpec(memory_space=pltpu.SMEM),
             pl.BlockSpec(memory_space=pltpu.SMEM),
             pl.BlockSpec((R_STEP * ORDERS, 2 * LEV), lambda i: (i, 0)),
             pl.BlockSpec((R_STEP, LEV, LEV), lambda i: (i, 0, 0)),
             pl.BlockSpec((2 * LEV, 2 * LEV), lambda i: (0, 0)),
+            pl.BlockSpec((R_STEP, ROWS, LATS), lambda i: (i, 0, 0)),
         ],
-        out_specs=pl.BlockSpec((WAVE, PAIRS, ROWS, LEV), lambda i: (0, 0, 0, 0)),
-        out_shape=jax.ShapeDtypeStruct((WAVE, PAIRS, ROWS, LEV), jnp.bfloat16),
+        out_specs=pl.BlockSpec((WAVE, BLOCKS, ROWS, LEV), lambda i: (0, 0, 0, 0)),
+        out_shape=jax.ShapeDtypeStruct((WAVE, BLOCKS, ROWS, LEV), jnp.bfloat16),
         scratch_shapes=[pltpu.VMEM((2, ORDERS * ROWS, LEV), jnp.float32)],
-    )(info, control.reshape(ROWS * ORDERS, 2 * LEV), vert_root, jnp.asarray(pick, jnp.bfloat16))
-
-
-def modes_kernel(vertical, legendre, out, left, right, result):
+    )(
+        row_wavenumber,
+        first_order[None],
+        control.reshape(ROWS * ORDERS, 2 * LEV),
+        vert_root,
+        jnp.asarray(pick, jnp.bfloat16),
+        legendre,
+    )
+
+
+def modes_kernel(packed, out, left, right, result):
     result[...] = jnp.zeros(result.shape, jnp.float32)
     for slot in range(3):
         pairs = [b for b in range(PAIRS) if ORDER_SLOT[b] == slot]
         for s in range(WAVE):
-            left[s * ROWS : (s + 1) * ROWS, :] = legendre[s, slot].astype(jnp.float32)
+            rows = slice(s * ROWS, (s + 1) * ROWS)
+            for h in range(2):
+                half = packed[s, PAIRS + 2 * slot + h]
+                left[rows, h * LEV : (h + 1) * LEV] = half.astype(jnp.float32)
             for i, b in enumerate(pairs):
-                right[s * ROWS : (s + 1) * ROWS, i * LEV : (i + 1) * LEV] = vertical[s, b].astype(
-                    jnp.float32
-                )
+                right[rows, i * LEV : (i + 1) * LEV] = packed[s, b].astype(jnp.float32)
         width = len(pairs) * LEV
         total = lax.dot_general(
             left[...].astype(jnp.bfloat16),
@@ -95,7 +120,7 @@
     out[...] = result[...].astype(jnp.bfloat16)
 
 
-def modes_of(vertical, legendre):
+def modes_of(packed):
     return pl.pallas_call(
         modes_kernel,
         out_shape=jax.ShapeDtypeStruct((LATS * SLOTS, LEV), jnp.bfloat16),
@@ -104,35 +129,60 @@
             pltpu.VMEM((NW, 2 * LEV), jnp.float32),
             pltpu.VMEM((LATS * SLOTS, LEV), jnp.float32),
         ],
-    )(vertical, legendre)
-
-
-def fourier_basis():
-    order = np.zeros((WAVE, LAT, SLOTS), np.int32)
-    part = np.zeros((WAVE, LAT, SLOTS), np.int32)
-    used = np.zeros((WAVE, LAT, SLOTS), np.float32)
+        compiler_params=PARAMS,
+    )(packed)
+
+
+def angle_tables():
+    order = np.zeros((PAIRS, WAVE, LAT), np.int32)
+    part = np.zeros((PAIRS, WAVE, LAT), np.int32)
     for w in range(WAVE):
         for b, (m, p) in enumerate(PAIR_OF[w % 2]):
-            order[w, :, b] = np.arange(LAT) * ORDERS + GROUP * (w // 2) + m
-            part[w, :, b] = p
-            used[w, :, b] = 1.0
-    order, part, used = (jnp.asarray(a.reshape(-1)) for a in (order, part, used))
-    weight = used * jnp.where(order == 0, 1.0, 2.0).astype(jnp.float32) / math.sqrt(NLON)
+            order[b, w] = np.arange(LAT) * ORDERS + GROUP * (w // 2) + m
+            part[b, w] = p
+    order, part = (jnp.asarray(a.reshape(-1)) for a in (order, part))
+    weight = jnp.where(order == 0, 1.0, 2.0).astype(jnp.float32) * (1.0 / math.sqrt(NLON))
 
     def turn(steps):
         return (steps % NLON).astype(jnp.float32) * (2.0 * math.pi / NLON)
 
     local = jnp.arange(EXT_X, dtype=jnp.int32) - HALO + NLON
     near = turn(order[None, :] * local[:, None] + part[None, :] * (NLON // 4))
-    far = turn(order[None, :] * (TILE_X * jnp.arange(LAT, dtype=jnp.int32))[:, None])
-    near_cos, near_sin = weight * jnp.cos(near), weight * jnp.sin(near)
-    far_cos, far_sin = jnp.cos(far), jnp.sin(far)
-    basis = far_cos[:, None, :] * near_cos[None] - far_sin[:, None, :] * near_sin[None]
-    return basis.astype(jnp.bfloat16).reshape(LAT * EXT_X, -1)
+    far = turn(order[None, :] * (TILE_X * jnp.arange(LAT // 2 + 1, dtype=jnp.int32))[:, None])
+    return weight * jnp.cos(near), weight * jnp.sin(near), jnp.cos(far), jnp.sin(far)
+
+
+def fourier_kernel(modes, near_cos, near_sin, far_cos, far_sin, out, wide, rhs):
+    wide[...] = modes[...].astype(jnp.float32)
+    for b in range(PAIRS):
+        rhs[b * LATS : (b + 1) * LATS] = wide[pl.ds(b, LATS, stride=SLOTS), :].astype(jnp.bfloat16)
+
+    def put(band, basis):
+        total = jnp.dot(basis.astype(jnp.bfloat16), rhs[...], preferred_element_type=jnp.float32)
+        out[band] = total.astype(jnp.bfloat16)
+
+    for b in range(LAT // 2 + 1):
+        even = far_cos[b : b + 1, :] * near_cos[...]
+        odd = far_sin[b : b + 1, :] * near_sin[...]
+        put(b, even - odd)
+        if 0 < b < LAT // 2:
+            put(LAT - b, even + odd)
+
+
+def latitude_row(modes):
+    return pl.pallas_call(
+        fourier_kernel,
+        out_shape=jax.ShapeDtypeStruct((LAT, EXT_X, LEV), jnp.bfloat16),
+        scratch_shapes=[
+            pltpu.VMEM((LATS * SLOTS, LEV), jnp.float32),
+            pltpu.VMEM((LATS * PAIRS, LEV), jnp.bfloat16),
+        ],
+        compiler_params=PARAMS,
+    )(modes, *angle_tables())
 
 
 def minmod(a, b):
-    return jnp.maximum(0.0, jnp.minimum(a, b)) + jnp.minimum(0.0, jnp.maximum(a, b))
+    return jnp.maximum(jnp.minimum(a, b), jnp.minimum(jnp.maximum(a, b), 0.0))
 
 
 def shifted(array, amount):
@@ -212,6 +262,7 @@
             pltpu.VMEM((2, EXT_R, EXT_X, LEV), jnp.float32),
             pltpu.VMEM((2, EXT_R, EXT_X, LEV), jnp.float32),
         ],
+        compiler_params=PARAMS,
     )(band[None], middle, south, north, *winds, *halos)
 
 
@@ -237,14 +288,7 @@
 ):
     lat = lax.axis_index("lat").astype(jnp.int32)
     wave = lax.axis_index("wave").astype(jnp.int32)
-    groups = legendre.reshape(WAVE // 2, GROUP, ROWS, LATS)
-    legendre_out = jnp.stack(
-        [jnp.stack([groups[:, m] for m in orders], axis=1) for orders in ORDER_OF], axis=1
-    ).reshape(WAVE, 3, ROWS, LATS)
-    legendre_in = lax.all_to_all(legendre_out, "wave", 0, 0, tiled=True)
-    vertical_out = vertical_parts(control, vert_root, row_wavenumber, lat * ORDERS)
-    vertical_in = lax.all_to_all(vertical_out, "wave", 0, 0, tiled=True)
-
+    packed = packed_inputs(control, vert_root, legendre, row_wavenumber, lat * ORDERS)
     winds = jnp.stack(
         [
             jnp.where(flag > 0, size, -size).astype(jnp.bfloat16)
@@ -254,15 +298,16 @@
     west = from_below(winds[:, :, -HALO:], "lat", True)
     east = from_above(winds[:, :, :HALO], "lat", True)
     wide = jnp.concatenate([west, winds, east], axis=2)
-
-    modes = modes_of(vertical_in, legendre_in).reshape(LATS, SLOTS, LEV)
-    modes = lax.all_to_all(modes, ("wave", "lat"), 0, 0, tiled=True)
+    packed = lax.all_to_all(packed, "wave", 0, 0, tiled=True)
+    packed, wide = lax.optimization_barrier((packed, wide))
+    modes = modes_of(packed)
+    modes, wide = lax.optimization_barrier((modes, wide))
     wind_s = from_below(wide[:, -HALO:], "wave", False)
     wind_n = from_above(wide[:, :HALO], "wave", False)
-    row = jnp.dot(
-        fourier_basis(), modes.reshape(LATS * SLOTS, LEV), preferred_element_type=jnp.float32
-    ).astype(jnp.bfloat16)
-    middle = lax.all_to_all(row.reshape(LAT, EXT_X, LEV), "lat", 0, 0, tiled=True)
+    modes = lax.all_to_all(modes.reshape(LATS, SLOTS, LEV), ("wave", "lat"), 0, 0, tiled=True)
+    modes, wind_s, wind_n = lax.optimization_barrier((modes, wind_s, wind_n))
+    row = latitude_row(modes.reshape(LATS * SLOTS, LEV))
+    middle = lax.all_to_all(row, "lat", 0, 0, tiled=True)
     south = from_below(middle[-HALO:], "wave", False)
     north = from_above(middle[:HALO], "wave", False)
     return advected(

time: 160 us -> 150 us (0.938)
  blocking collectives: 0 us -> 12.9 us
  starting transfers between devices: 50.4 us -> 37.8 us
  other arithmetic: 14.5 us -> 6.76 us
  local copies, waits for them, and re-layouts: 2.85 us -> 8.46 us
  matrix products: 5.4 us -> 0 us
  waiting for transfers between devices: 65.9 us -> 64 us
    all_to_all x4 -> x2, waiting for transfers between devices: 49.6 us -> 32.8 us  [the longest x1 32.8 us: per_device(): packed = lax.all_to_all(packed, 'wave', 0, 0, tiled=True)]
    all_to_all x0 -> x1, blocking collectives: none -> 12.9 us  [per_device(): middle = lax.all_to_all(row, 'lat', 0, 0, tiled=True)]
    all_to_all x4 -> x2, starting transfers between devices: 30.1 us -> 19.5 us  [the longest x1 10.9 us: per_device(): packed = lax.all_to_all(packed, 'wave', 0, 0, tiled=True)]
    ppermute x3, waiting for transfers between devices: 12.4 us -> 21.8 us  [from_below(): return lax.ppermute(block, axis, pairs)]
    unnamed x36 -> x38, local copies, waits for them, and re-layouts: 1.66 us -> 7.64 us
    ppermute x3, waiting for transfers between devices: 3.9 us -> 9.41 us  [from_above(): return lax.ppermute(block, axis, pairs)]
    dot_general x1 -> x0, matrix products: 5.4 us -> none  [per_device(): jnp.dot(fourier_basis(), modes.reshape(LATS * SLOTS, LEV), preferred_elem...]
    convert_element_type x1 -> x0, other arithmetic: 4.76 us -> none  [fourier_basis(): return basis.astype(jnp.bfloat16).reshape(LAT * EXT_X, -1)]
  transfers between devices with their start and end apart: 10 -> 8, of which waited for: 8 -> 7; matrix products, arithmetic and copies ran while one was open for 12% -> 5% of each run, Pallas kernels for 2% -> 0%
where the time goes in v2:
time: 150 us; the launch traced here: 147 us
  waiting for transfers between devices  64 us (43%)
  starting transfers between devices  37.8 us (25%)
  Pallas kernels  17.4 us (12%)
  blocking collectives  12.9 us (9%)
  local copies, waits for them, and re-layouts  8.46 us (6%)
  other arithmetic  6.76 us (5%)
    all_to_all x1, waiting for transfers between devices, per_device(): packed = lax.all_to_all(packed, 'wave', 0, 0, tiled=True)  32.8 us
    ppermute x3, waiting for transfers between devices, from_below(): return lax.ppermute(block, axis, pairs)  21.8 us
    all_to_all x1, blocking collectives, per_device(): middle = lax.all_to_all(row, 'lat', 0, 0, tiled=True)  12.9 us
    all_to_all x1, starting transfers between devices, per_device(): packed = lax.all_to_all(packed, 'wave', 0, 0, tiled=True)  10.9 us
    ppermute x3, starting transfers between devices, from_above(): return lax.ppermute(block, axis, pairs)  9.93 us
    ppermute x3, waiting for transfers between devices, from_above(): return lax.ppermute(block, axis, pairs)  9.41 us
    pallas_call x1, Pallas kernels, advected(): pl.pallas_call(advect_kernel, in_specs=[pl.BlockSpec(memory_space=pltpu.S...  8.67 us
    all_to_all x1, starting transfers between devices, per_device(): lax.all_to_all(modes.reshape(LATS, SLOTS, LEV), ('wave', 'lat'), 0, 0, ti...  8.56 us
  transfers between devices with their start and end apart: 8, of which 7 were waited for; matrix products, arithmetic and copies ran while one was open for 5% of the time, Pallas kernels for 0%

profile of v2, /device:TPU:64, one launch (start us, length us, event | category | flops | bytes accessed | tf_op | source)
XLA Modules:
  0.0 147.5 jit_solution(16460242900363674749)
XLA Ops:
  0.0 6.7 %shard_map.109 = bf16[16,11,40,128]{3,2,1,0:T(8,128)(2,1)} custom-call(s32[40]{0:T(128)} %wavenumber.1, s32[1]{0:T(128)} %bitcast.1.first, bf16[1600,256]{1,0:T(8,128)(2,1)} %bitcast.11, bf16[40,128,128]{2,1,0:T(8,128)(2,1)} %vert.1, bf16[256,256]{1,0:T(8,128)(2,1)} %constant.53.clone.pick, bf16[40,40,256]{2,1,0:T(8,128)(2,1)} %legendre.1), custom_call_target="tpu_custom_call" | custom-call | tf_op jit(solution)/shard_map/pallas_call | solution.py:76
  6.7 10.9 %all-to-all-start = ((bf16[16,11,40,128]{3,2,1,0:T(8,128)(2,1)}), bf16[16,11,40,128]{3,2,1,0:T(8,128)(2,1)S(1)}, u32[]{:S(2)}, u32[]{:S(2)}) async-start(bf16[16,11,40,128]{3,2,1,0:T(8,128)(2,1)} %shard_map.109), calls=%async_computation | async-start | bytes 3604480 | tf_op jit(solution)/shard_map/all_to_all | solution.py:301
  17.6 1.5 fusion.7
  19.1 1.8 %collective-permute-start.1 = (bf16[2,16,8,128]{3,2,1,0:T(8,128)(2,1)S(1)}, bf16[2,16,8,128]{3,2,1,0:T(8,128)(2,1)S(1)}, u32[]{:S(2)}, u32[]{:S(2)}) collective-permute-start(bf16[2,16,8,128]{3,2,1,0:T(8,128)(2,1)S(1)} %get-tuple-element.22), channel_id=1, source_target_pairs={{1,0},{2,1},{3,2},{4,3},{5,4},{6,5},{7,6},{8,7},{9,8},{10,9},{11,1... | collective-permute-start | bytes 196616 | tf_op jit(solution)/shard_map/ppermute | solution.py:276
  20.9 1.9 %collective-permute-done.1.east = bf16[2,16,8,128]{3,2,1,0:T(8,128)(2,1)S(1)} collective-permute-done((bf16[2,16,8,128]{3,2,1,0:T(8,128)(2,1)S(1)}, bf16[2,16,8,128]{3,2,1,0:T(8,128)(2,1)S(1)}, u32[]{:S(2)}, u32[]{:S(2)}) %collective-permute-start.1) | collective-permute-done | bytes 65568 | tf_op jit(solution)/shard_map/ppermute | solution.py:276
  22.8 3.9 %collective-permute-done.west = bf16[2,16,8,128]{3,2,1,0:T(8,128)(2,1)S(1)} collective-permute-done((bf16[2,16,8,128]{3,2,1,0:T(8,128)(2,1)S(1)}, bf16[2,16,8,128]{3,2,1,0:T(8,128)(2,1)S(1)}, u32[]{:S(2)}, u32[]{:S(2)}) %collective-permute-start) | collective-permute-done | bytes 65568 | tf_op jit(solution)/shard_map/ppermute | solution.py:271
  29.0 32.8 %all-to-all-done.packed = bf16[16,11,40,128]{3,2,1,0:T(8,128)(2,1)S(1)} async-done(((bf16[16,11,40,128]{3,2,1,0:T(8,128)(2,1)}), bf16[16,11,40,128]{3,2,1,0:T(8,128)(2,1)S(1)}, u32[]{:S(2)}, u32[]{:S(2)}) %all-to-all-start) | async-done | bytes 1802272 | tf_op jit(solution)/shard_map/all_to_all | solution.py:301
  63.1 8.6 %all-to-all-start.1 = ((bf16[256,8,128]{2,1,0:T(8,128)(2,1)}), bf16[256,8,128]{2,1,0:T(8,128)(2,1)S(1)}, u32[]{:S(2)}, u32[]{:S(2)}) async-start(bf16[256,8,128]{2,1,0:T(8,128)(2,1)} %bitcast.10), calls=%async_computation.1 | async-start | bytes 1048576 | tf_op jit(solution)/shard_map/all_to_all | solution.py:307
  71.7 3.2 %sine_multiply_fusion = (f32[96,1280]{1,0:T(8,128)}, f32[96,1280]{1,0:T(8,128)}) fusion(s32[1280]{0:T(1024)S(1)} %copy-done.17, s32[96]{0:T(128)S(1)} %iota_add_fusion, s32[1280]{0:T(1024)S(1)} %copy-done.16, f32[1280]{0:T(1024)S(1)} %copy-done.18), kind=kLoop, calls=%fused_computation.8 | loop fusion | flops 1474560 | bytes 998784 | tf_op jit(solution)/shard_map/mul | solution.py:152
  75.0 5.0 %collective-permute-start.2 = (bf16[2,8,96,128]{3,2,1,0:T(8,128)(2,1)S(1)}, bf16[2,8,96,128]{3,2,1,0:T(8,128)(2,1)S(1)}, u32[]{:S(2)}, u32[]{:S(2)}) collective-permute-start(bf16[2,8,96,128]{3,2,1,0:T(8,128)(2,1)S(1)} %get-tuple-element.20), channel_id=1, source_target_pairs={{0,16},{16,32},{32,48},{48,64},{64,80},{80,96},{96,112},{112,128},... | collective-permute-start | bytes 1179656 | tf_op jit(solution)/shard_map/ppermute | solution.py:271
  80.0 3.2 %collective-permute-start.3 = (bf16[2,8,96,128]{3,2,1,0:T(8,128)(2,1)S(1)}, bf16[2,8,96,128]{3,2,1,0:T(8,128)(2,1)S(1)}, u32[]{:S(2)}, u32[]{:S(2)}) collective-permute-start(bf16[2,8,96,128]{3,2,1,0:T(8,128)(2,1)S(1)} %get-tuple-element.19), channel_id=1, source_target_pairs={{16,0},{32,16},{48,32},{64,48},{80,64},{96,80},{112,96},{128,112},... | collective-permute-start | bytes 1179656 | tf_op jit(solution)/shard_map/ppermute | solution.py:276
  83.2 1.1 fusion.13
  84.3 14.7 %collective-permute-done.2.wind_s = bf16[2,8,96,128]{3,2,1,0:T(8,128)(2,1)S(1)} collective-permute-done((bf16[2,8,96,128]{3,2,1,0:T(8,128)(2,1)S(1)}, bf16[2,8,96,128]{3,2,1,0:T(8,128)(2,1)S(1)}, u32[]{:S(2)}, u32[]{:S(2)}) %collective-permute-start.2) | collective-permute-done | bytes 393248 | tf_op jit(solution)/shard_map/ppermute | solution.py:271
  99.0 3.4 %collective-permute-done.3.wind_n = bf16[2,8,96,128]{3,2,1,0:T(8,128)(2,1)S(1)} collective-permute-done((bf16[2,8,96,128]{3,2,1,0:T(8,128)(2,1)S(1)}, bf16[2,8,96,128]{3,2,1,0:T(8,128)(2,1)S(1)}, u32[]{:S(2)}, u32[]{:S(2)}) %collective-permute-start.3) | collective-permute-done | bytes 393248 | tf_op jit(solution)/shard_map/ppermute | solution.py:276
  103.2 1.0 copy-done.5
  104.2 1.0 copy-done.6
  107.0 1.5 %shard_map.111 = bf16[16,96,128]{2,1,0:T(8,128)(2,1)S(1)} custom-call(bf16[2048,128]{1,0:T(8,128)(2,1)S(1)} %bitcast.9, f32[96,1280]{1,0:T(8,128)S(1)} %copy-done.6, f32[96,1280]{1,0:T(8,128)S(1)} %copy-done.5, f32[9,1280]{1,0:T(8,128)S(1)} %copy-done.10, f32[9,1280]{1,0:T(8,128)S(1)} %copy-done.9), custom_call_target="tpu_custom_call" | custom-call | tf_op jit(solution)/shard_map/pallas_call | solution.py:173
  108.6 12.9 %all_to_all.15.middle = bf16[16,96,128]{2,1,0:T(8,128)(2,1)S(1)} all-to-all(bf16[16,96,128]{2,1,0:T(8,128)(2,1)S(1)} %shard_map.111), channel_id=1, replica_groups=mesh['wave'=16,'lat'=16] {'lat'}, dimensions={0} | all-to-all | bytes 786432 | tf_op jit(solution)/shard_map/all_to_all | solution.py:310
  122.2 3.4 %collective-permute-start.4 = (bf16[8,96,128]{2,1,0:T(8,128)(2,1)}, bf16[8,96,128]{2,1,0:T(8,128)(2,1)}, u32[]{:S(2)}, u32[]{:S(2)}) collective-permute-start(bf16[8,96,128]{2,1,0:T(8,128)(2,1)} %get-tuple-element.24), channel_id=1, source_target_pairs={{0,16},{16,32},{32,48},{48,64},{64,80},{80,96},{96,112},{112,128},... | collective-permute-start | bytes 589832 | tf_op jit(solution)/shard_map/ppermute | solution.py:271
  125.6 4.9 %collective-permute-start.5 = (bf16[8,96,128]{2,1,0:T(8,128)(2,1)}, bf16[8,96,128]{2,1,0:T(8,128)(2,1)}, u32[]{:S(2)}, u32[]{:S(2)}) collective-permute-start(bf16[8,96,128]{2,1,0:T(8,128)(2,1)} %get-tuple-element.23), channel_id=1, source_target_pairs={{16,0},{32,16},{48,32},{64,48},{80,64},{96,80},{112,96},{128,112},... | collective-permute-start | bytes 589832 | tf_op jit(solution)/shard_map/ppermute | solution.py:276
  130.5 3.2 %collective-permute-done.4.south = bf16[8,96,128]{2,1,0:T(8,128)(2,1)} collective-permute-done((bf16[8,96,128]{2,1,0:T(8,128)(2,1)}, bf16[8,96,128]{2,1,0:T(8,128)(2,1)}, u32[]{:S(2)}, u32[]{:S(2)}) %collective-permute-start.4) | collective-permute-done | bytes 196640 | tf_op jit(solution)/shard_map/ppermute | solution.py:271
  133.7 4.1 %collective-permute-done.5.north = bf16[8,96,128]{2,1,0:T(8,128)(2,1)} collective-permute-done((bf16[8,96,128]{2,1,0:T(8,128)(2,1)}, bf16[8,96,128]{2,1,0:T(8,128)(2,1)}, u32[]{:S(2)}, u32[]{:S(2)}) %collective-permute-start.5) | collective-permute-done | bytes 196640 | tf_op jit(solution)/shard_map/ppermute | solution.py:276
  137.8 1.0 copy-done.8
  138.8 8.7 %shard_map.112 = f32[16,80,128]{2,1,0:T(8,128)} custom-call(s32[1]{0:T(128)} %bitcast.where, bf16[16,96,128]{2,1,0:T(8,128)(2,1)S(1)} %all_to_all.15.middle, bf16[8,96,128]{2,1,0:T(8,128)(2,1)} %collective-permute-done.4.south, bf16[8,96,128]{2,1,0:T(8,128)(2,1)} %collective-permute-done.5.north, f32[16,80,128]{2,1,0:T(8,128)S(1)} %copy-done, ...), custom_call_target="tpu_custom_call" | custom-call | tf_op jit(solution)/shard_map/pallas_call | solution.py:254
  (44 shorter events, 7.0 us)
Async XLA Ops:
  6.7 10.9 %copy-start = (f32[16,80,128]{2,1,0:T(8,128)S(1)}, f32[16,80,128]{2,1,0:T(8,128)}, u32[]{:S(2)}) copy-start(f32[16,80,128]{2,1,0:T(8,128)} %ce.1) | copy-start | bytes 1966084
  6.7 10.9 %copy-start.1 = (f32[16,80,128]{2,1,0:T(8,128)S(1)}, f32[16,80,128]{2,1,0:T(8,128)}, u32[]{:S(2)}) copy-start(f32[16,80,128]{2,1,0:T(8,128)} %cn.1) | copy-start | bytes 1966084
  6.7 55.1 %all-to-all-start = ((bf16[16,11,40,128]{3,2,1,0:T(8,128)(2,1)}), bf16[16,11,40,128]{3,2,1,0:T(8,128)(2,1)S(1)}, u32[]{:S(2)}, u32[]{:S(2)}) async-start(bf16[16,11,40,128]{3,2,1,0:T(8,128)(2,1)} %shard_map.109), calls=%async_computation | async-start | bytes 3604480 | tf_op jit(solution)/shard_map/all_to_all | solution.py:301
  19.1 3.7 %collective-permute-start.1 = (bf16[2,16,8,128]{3,2,1,0:T(8,128)(2,1)S(1)}, bf16[2,16,8,128]{3,2,1,0:T(8,128)(2,1)S(1)}, u32[]{:S(2)}, u32[]{:S(2)}) collective-permute-start(bf16[2,16,8,128]{3,2,1,0:T(8,128)(2,1)S(1)} %get-tuple-element.22), channel_id=1, source_target_pairs={{1,0},{2,1},{3,2},{4,3},{5,4},{6,5},{7,6},{8,7},{9,8},{10,9},{11,1... | collective-permute-start | bytes 196616 | tf_op jit(solution)/shard_map/ppermute | solution.py:276
  20.9 5.8 %collective-permute-start = (bf16[2,16,8,128]{3,2,1,0:T(8,128)(2,1)S(1)}, bf16[2,16,8,128]{3,2,1,0:T(8,128)(2,1)S(1)}, u32[]{:S(2)}, u32[]{:S(2)}) collective-permute-start(bf16[2,16,8,128]{3,2,1,0:T(8,128)(2,1)S(1)} %get-tuple-element.21), channel_id=1, source_target_pairs={{0,1},{1,2},{2,3},{3,4},{4,5},{5,6},{6,7},{7,8},{8,9},{9,10},{10,1... | collective-permute-start | bytes 196616 | tf_op jit(solution)/shard_map/ppermute | solution.py:271
  28.9 42.7 %copy-start.16 = (s32[1280]{0:T(1024)S(1)}, s32[1280]{0:T(1024)}, u32[]{:S(2)}) copy-start(s32[1280]{0:T(1024)} %constant.54.clone) | copy-start | bytes 15364
  28.9 42.7 %copy-start.17 = (s32[1280]{0:T(1024)S(1)}, s32[1280]{0:T(1024)}, u32[]{:S(2)}) copy-start(s32[1280]{0:T(1024)} %constant.63) | copy-start | bytes 15364
  29.0 42.7 %copy-start.18 = (f32[1280]{0:T(1024)S(1)}, f32[1280]{0:T(1024)}, u32[]{:S(2)}) copy-start(f32[1280]{0:T(1024)} %constant.62) | copy-start | bytes 15364
  62.3 0.8 copy-start.4
  63.1 11.8 %copy-start.15 = (bf16[2,16,96,128]{3,2,1,0:T(8,128)(2,1)S(1)}, bf16[2,16,96,128]{3,2,1,0:T(8,128)(2,1)}, u32[]{:S(2)}) copy-start(bf16[2,16,96,128]{3,2,1,0:T(8,128)(2,1)} %pad_maximum_fusion) | copy-start | bytes 2359300
  63.1 40.1 %all-to-all-start.1 = ((bf16[256,8,128]{2,1,0:T(8,128)(2,1)}), bf16[256,8,128]{2,1,0:T(8,128)(2,1)S(1)}, u32[]{:S(2)}, u32[]{:S(2)}) async-start(bf16[256,8,128]{2,1,0:T(8,128)(2,1)} %bitcast.10), calls=%async_computation.1 | async-start | bytes 1048576 | tf_op jit(solution)/shard_map/all_to_all | solution.py:307
  75.0 24.0 %collective-permute-start.2 = (bf16[2,8,96,128]{3,2,1,0:T(8,128)(2,1)S(1)}, bf16[2,8,96,128]{3,2,1,0:T(8,128)(2,1)S(1)}, u32[]{:S(2)}, u32[]{:S(2)}) collective-permute-start(bf16[2,8,96,128]{3,2,1,0:T(8,128)(2,1)S(1)} %get-tuple-element.20), channel_id=1, source_target_pairs={{0,16},{16,32},{32,48},{48,64},{64,80},{80,96},{96,112},{112,128},... | collective-permute-start | bytes 1179656 | tf_op jit(solution)/shard_map/ppermute | solution.py:271
  80.0 22.4 %collective-permute-start.3 = (bf16[2,8,96,128]{3,2,1,0:T(8,128)(2,1)S(1)}, bf16[2,8,96,128]{3,2,1,0:T(8,128)(2,1)S(1)}, u32[]{:S(2)}, u32[]{:S(2)}) collective-permute-start(bf16[2,8,96,128]{3,2,1,0:T(8,128)(2,1)S(1)} %get-tuple-element.19), channel_id=1, source_target_pairs={{16,0},{32,16},{48,32},{64,48},{80,64},{96,80},{112,96},{128,112},... | collective-permute-start | bytes 1179656 | tf_op jit(solution)/shard_map/ppermute | solution.py:276
  103.2 1.0 copy-start.5
  104.2 1.0 copy-start.6
  105.2 0.9 copy-start.9
  106.1 0.9 copy-start.10
  107.0 30.8 %copy-start.2 = (s32[16,80,128]{2,1,0:T(8,128)S(1)}, s32[16,80,128]{2,1,0:T(8,128)}, u32[]{:S(2)}) copy-start(s32[16,80,128]{2,1,0:T(8,128)} %ef.1) | copy-start | bytes 1966084
  107.0 30.8 %copy-start.3 = (s32[16,80,128]{2,1,0:T(8,128)S(1)}, s32[16,80,128]{2,1,0:T(8,128)}, u32[]{:S(2)}) copy-start(s32[16,80,128]{2,1,0:T(8,128)} %nf.1) | copy-start | bytes 1966084
  108.5 29.2 %copy-start.12 = (bf16[2,16,8,128]{3,2,1,0:T(8,128)(2,1)S(1)}, bf16[2,16,8,128]{3,2,1,0:T(8,128)(2,1)}, u32[]{:S(2)}) copy-start(bf16[2,16,8,128]{3,2,1,0:T(8,128)(2,1)} %copy-done.11) | copy-start | bytes 196612
  108.6 29.2 %copy-start.14 = (bf16[2,16,8,128]{3,2,1,0:T(8,128)(2,1)S(1)}, bf16[2,16,8,128]{3,2,1,0:T(8,128)(2,1)}, u32[]{:S(2)}) copy-start(bf16[2,16,8,128]{3,2,1,0:T(8,128)(2,1)} %copy-done.13) | copy-start | bytes 196612
  122.2 11.4 %collective-permute-start.4 = (bf16[8,96,128]{2,1,0:T(8,128)(2,1)}, bf16[8,96,128]{2,1,0:T(8,128)(2,1)}, u32[]{:S(2)}, u32[]{:S(2)}) collective-permute-start(bf16[8,96,128]{2,1,0:T(8,128)(2,1)} %get-tuple-element.24), channel_id=1, source_target_pairs={{0,16},{16,32},{32,48},{48,64},{64,80},{80,96},{96,112},{112,128},... | collective-permute-start | bytes 589832 | tf_op jit(solution)/shard_map/ppermute | solution.py:271
  125.6 12.2 %collective-permute-start.5 = (bf16[8,96,128]{2,1,0:T(8,128)(2,1)}, bf16[8,96,128]{2,1,0:T(8,128)(2,1)}, u32[]{:S(2)}, u32[]{:S(2)}) collective-permute-start(bf16[8,96,128]{2,1,0:T(8,128)(2,1)} %get-tuple-element.23), channel_id=1, source_target_pairs={{16,0},{32,16},{48,32},{64,48},{80,64},{96,80},{112,96},{128,112},... | collective-permute-start | bytes 589832 | tf_op jit(solution)/shard_map/ppermute | solution.py:276
  137.8 1.0 copy-start.8
  (3 other events, 2.0 us)

commit v3 on v2

--- a/solution.py
+++ b/solution.py
@@ -28,6 +28,7 @@
 PAIR_OF = (((0, 0), (0, 1), (1, 0), (1, 1), (2, 0)), ((4, 0), (4, 1), (3, 0), (3, 1), (2, 1)))
 ORDER_SLOT = (0, 0, 1, 1, 2)
 R_STEP = 8
+FAR = 16
 BLOCKS = PAIRS + 6
 PARAMS = pltpu.CompilerParams(vmem_limit_bytes=24 * 1024 * 1024)
 
@@ -148,11 +149,17 @@
 
     local = jnp.arange(EXT_X, dtype=jnp.int32) - HALO + NLON
     near = turn(order[None, :] * local[:, None] + part[None, :] * (NLON // 4))
-    far = turn(order[None, :] * (TILE_X * jnp.arange(LAT // 2 + 1, dtype=jnp.int32))[:, None])
-    return weight * jnp.cos(near), weight * jnp.sin(near), jnp.cos(far), jnp.sin(far)
-
-
-def fourier_kernel(modes, near_cos, near_sin, far_cos, far_sin, out, wide, rhs):
+    far = turn(order[None, :] * (TILE_X * jnp.arange(FAR, dtype=jnp.int32))[:, None])
+    return jnp.concatenate(
+        [weight * jnp.cos(near), weight * jnp.sin(near), jnp.cos(far), jnp.sin(far)]
+    )
+
+
+def fourier_kernel(modes, tables, out, wide, rhs):
+    near_cos = tables.at[0:EXT_X]
+    near_sin = tables.at[EXT_X : 2 * EXT_X]
+    far_cos = tables.at[2 * EXT_X : 2 * EXT_X + FAR]
+    far_sin = tables.at[2 * EXT_X + FAR : 2 * EXT_X + 2 * FAR]
     wide[...] = modes[...].astype(jnp.float32)
     for b in range(PAIRS):
         rhs[b * LATS : (b + 1) * LATS] = wide[pl.ds(b, LATS, stride=SLOTS), :].astype(jnp.bfloat16)
@@ -169,7 +176,7 @@
             put(LAT - b, even + odd)
 
 
-def latitude_row(modes):
+def latitude_row(modes, tables):
     return pl.pallas_call(
         fourier_kernel,
         out_shape=jax.ShapeDtypeStruct((LAT, EXT_X, LEV), jnp.bfloat16),
@@ -177,8 +184,7 @@
             pltpu.VMEM((LATS * SLOTS, LEV), jnp.float32),
             pltpu.VMEM((LATS * PAIRS, LEV), jnp.bfloat16),
         ],
-        compiler_params=PARAMS,
-    )(modes, *angle_tables())
+    )(modes, tables)
 
 
 def minmod(a, b):
@@ -195,12 +201,12 @@
 
 
 def advect_kernel(
-    where, middle, south, north, ce, cn, ef, nf, west, east, wind_s, wind_n, out, qa, qb, us, gs
+    where, middle, halo, ce, cn, ef, nf, west, east, wind_s, wind_n, out, qa, qb, us, gs
 ):
     band = where[0]
-    qa[0:HALO] = south[...].astype(jnp.float32)
+    qa[0:HALO] = halo[HALO:].astype(jnp.float32)
     qa[HALO : HALO + TILE_R] = middle[...].astype(jnp.float32)
-    qa[HALO + TILE_R :] = north[...].astype(jnp.float32)
+    qa[HALO + TILE_R :] = halo[:HALO].astype(jnp.float32)
     qb[0:HALO] = jnp.zeros((HALO, EXT_X, LEV), jnp.float32)
     qb[HALO + TILE_R :] = jnp.zeros((HALO, EXT_X, LEV), jnp.float32)
     inner = slice(HALO, HALO + TILE_R)
@@ -250,11 +256,11 @@
         lax.fori_loop(low, high, row, (first, face(low - 1, slope(low - 1), first)))
 
 
-def advected(band, middle, south, north, winds, halos):
+def advected(band, middle, halo, winds, halos):
     return pl.pallas_call(
         advect_kernel,
         in_specs=[pl.BlockSpec(memory_space=pltpu.SMEM)]
-        + [pl.BlockSpec(memory_space=pltpu.VMEM)] * 11,
+        + [pl.BlockSpec(memory_space=pltpu.VMEM)] * 10,
         out_shape=jax.ShapeDtypeStruct((TILE_R, TILE_X, LEV), jnp.float32),
         scratch_shapes=[
             pltpu.VMEM((EXT_R, EXT_X, LEV), jnp.float32),
@@ -263,7 +269,7 @@
             pltpu.VMEM((2, EXT_R, EXT_X, LEV), jnp.float32),
         ],
         compiler_params=PARAMS,
-    )(band[None], middle, south, north, *winds, *halos)
+    )(band[None], middle, halo, *winds, *halos)
 
 
 def from_below(block, axis, wrap):
@@ -298,23 +304,28 @@
     west = from_below(winds[:, :, -HALO:], "lat", True)
     east = from_above(winds[:, :, :HALO], "lat", True)
     wide = jnp.concatenate([west, winds, east], axis=2)
+    tables = angle_tables()
     packed = lax.all_to_all(packed, "wave", 0, 0, tiled=True)
-    packed, wide = lax.optimization_barrier((packed, wide))
+    packed, wide, tables = lax.optimization_barrier((packed, wide, tables))
     modes = modes_of(packed)
     modes, wide = lax.optimization_barrier((modes, wide))
     wind_s = from_below(wide[:, -HALO:], "wave", False)
     wind_n = from_above(wide[:, :HALO], "wave", False)
     modes = lax.all_to_all(modes.reshape(LATS, SLOTS, LEV), ("wave", "lat"), 0, 0, tiled=True)
-    modes, wind_s, wind_n = lax.optimization_barrier((modes, wind_s, wind_n))
-    row = latitude_row(modes.reshape(LATS * SLOTS, LEV))
+    row = latitude_row(modes.reshape(LATS * SLOTS, LEV), tables)
+    pairs = []
+    for w in range(WAVE):
+        for l in range(LAT):
+            to = w - 1 if l < HALO else w + 1
+            if 0 <= to < WAVE:
+                pairs.append((w * LAT + l, to * LAT + l))
+    next_row = lax.ppermute(row, ("wave", "lat"), pairs)
     middle = lax.all_to_all(row, "lat", 0, 0, tiled=True)
-    south = from_below(middle[-HALO:], "wave", False)
-    north = from_above(middle[:HALO], "wave", False)
+    halo = lax.all_to_all(next_row, "lat", 0, 0, tiled=True)
     return advected(
         wave,
         middle,
-        south,
-        north,
+        halo,
         (courant_east, courant_north, east_flags, north_flags),
         (west, east, wind_s, wind_n),
     )

time: 150 us -> 145 us (0.967)
  blocking collectives: 12.9 us -> 27.7 us
  waiting for transfers between devices: 64 us -> 54.8 us
  local copies, waits for them, and re-layouts: 8.46 us -> 2.12 us
  starting transfers between devices: 37.8 us -> 32 us
  Pallas kernels: 17.4 us -> 19.7 us
    ppermute x3 -> x2, waiting for transfers between devices: 21.8 us -> 5.45 us  [from_below(): return lax.ppermute(block, axis, pairs)]
    all_to_all x1, blocking collectives: 12.9 us -> 27.7 us  [per_device(): lax.all_to_all(modes.reshape(LATS, SLOTS, LEV), ('wave', 'lat'), 0, 0, ti...]
    ppermute x0 -> x1, waiting for transfers between devices: none -> 8.81 us  [per_device(): next_row = lax.ppermute(row, ('wave', 'lat'), pairs)]
    unnamed x38 -> x14, local copies, waits for them, and re-layouts: 7.64 us -> 0.04 us
    ppermute x3 -> x2, waiting for transfers between devices: 9.41 us -> 2.65 us  [from_above(): return lax.ppermute(block, axis, pairs)]
    ppermute x3 -> x2, starting transfers between devices: 8.38 us -> 3.57 us  [from_below(): return lax.ppermute(block, axis, pairs)]
    all_to_all x1 -> x2, waiting for transfers between devices: 0.01 us -> 3.9 us  [the longest x1 3.11 us: per_device(): halo = lax.all_to_all(next_row, 'lat', 0, 0, tiled=True)]
    ppermute x0 -> x1, starting transfers between devices: none -> 3.89 us  [per_device(): next_row = lax.ppermute(row, ('wave', 'lat'), pairs)]
  transfers between devices with their start and end apart: 8 -> 8, of which waited for: 7 -> 7; matrix products, arithmetic and copies ran while one was open for 5% -> 6% of each run, Pallas kernels for 0% -> 0%
where the time goes in v3:
time: 145 us; the launch traced here: 143 us
  waiting for transfers between devices  54.8 us (38%)
  starting transfers between devices  32 us (22%)
  blocking collectives  27.7 us (19%)
  Pallas kernels  19.7 us (14%)
  other arithmetic  6.07 us (4%)
  local copies, waits for them, and re-layouts  2.12 us (1%)
    all_to_all x1, waiting for transfers between devices, per_device(): packed = lax.all_to_all(packed, 'wave', 0, 0, tiled=True)  34 us
    all_to_all x1, blocking collectives, per_device(): lax.all_to_all(modes.reshape(LATS, SLOTS, LEV), ('wave', 'lat'), 0, 0, ti...  27.7 us
    all_to_all x1, starting transfers between devices, per_device(): packed = lax.all_to_all(packed, 'wave', 0, 0, tiled=True)  10.9 us
    ppermute x1, waiting for transfers between devices, per_device(): next_row = lax.ppermute(row, ('wave', 'lat'), pairs)  8.81 us
    pallas_call x1, Pallas kernels, advected(): pl.pallas_call(advect_kernel, in_specs=[pl.BlockSpec(memory_space=pltpu.S...  8.76 us
    pallas_call x1, Pallas kernels, packed_inputs(): pl.pallas_call(packing_kernel, grid=(ROWS // R_STEP,), in_specs=[pl.Block...  6.68 us
    ppermute x2, starting transfers between devices, from_above(): return lax.ppermute(block, axis, pairs)  6.5 us
    ppermute x2, waiting for transfers between devices, from_below(): return lax.ppermute(block, axis, pairs)  5.45 us
  transfers between devices with their start and end apart: 8, of which 7 were waited for; matrix products, arithmetic and copies ran while one was open for 6% of the time, Pallas kernels for 0%

profile of v3, /device:TPU:64, one launch (start us, length us, event | category | flops | bytes accessed | tf_op | source)
XLA Modules:
  0.0 142.5 jit_solution(14789066815934494354)
XLA Ops:
  0.0 6.7 %shard_map.109 = bf16[16,11,40,128]{3,2,1,0:T(8,128)(2,1)} custom-call(s32[40]{0:T(128)} %wavenumber.1, s32[1]{0:T(128)} %bitcast.1.first, bf16[1600,256]{1,0:T(8,128)(2,1)} %bitcast.11, bf16[40,128,128]{2,1,0:T(8,128)(2,1)} %vert.1, bf16[256,256]{1,0:T(8,128)(2,1)} %constant.53.clone.pick, bf16[40,40,256]{2,1,0:T(8,128)(2,1)} %legendre.1), custom_call_target="tpu_custom_call" | custom-call | tf_op jit(solution)/shard_map/pallas_call | solution.py:77
  6.7 10.9 %all-to-all-start = ((bf16[16,11,40,128]{3,2,1,0:T(8,128)(2,1)}), bf16[16,11,40,128]{3,2,1,0:T(8,128)(2,1)S(1)}, u32[]{:S(2)}, u32[]{:S(2)}) async-start(bf16[16,11,40,128]{3,2,1,0:T(8,128)(2,1)} %shard_map.109), calls=%async_computation | async-start | bytes 3604480 | tf_op jit(solution)/shard_map/all_to_all | solution.py:308
  17.6 1.5 %fusion.7 = (bf16[1,16,80,128]{3,2,1,0:T(8,128)(2,1)S(1)}, bf16[1,16,80,128]{3,2,1,0:T(8,128)(2,1)S(1)}) fusion(f32[16,80,128]{2,1,0:T(8,128)S(1)} %copy-done.1, s32[16,80,128]{2,1,0:T(8,128)} %nf.1, f32[16,80,128]{2,1,0:T(8,128)S(1)} %copy-done, s32[16,80,128]{2,1,0:T(8,128)} %ef.1), kind=kLoop, calls=%fused_computation.15 | loop fusion | flops 1310720 | bytes 3276800 | tf_op jit(solution)/shard_map/stack | solution.py:298
  19.1 1.8 %collective-permute-start.1 = (bf16[2,16,8,128]{3,2,1,0:T(8,128)(2,1)S(1)}, bf16[2,16,8,128]{3,2,1,0:T(8,128)(2,1)S(1)}, u32[]{:S(2)}, u32[]{:S(2)}) collective-permute-start(bf16[2,16,8,128]{3,2,1,0:T(8,128)(2,1)S(1)} %get-tuple-element.18), channel_id=1, source_target_pairs={{1,0},{2,1},{3,2},{4,3},{5,4},{6,5},{7,6},{8,7},{9,8},{10,9},{11,1... | collective-permute-start | bytes 196616 | tf_op jit(solution)/shard_map/ppermute | solution.py:282
  21.4 2.1 %cosine_multiply_fusion = (f32[96,1280]{1,0:T(8,128)S(1)}, f32[96,1280]{1,0:T(8,128)S(1)}) fusion(s32[1280]{0:T(1024)S(1)} %copy-done.5, s32[96]{0:T(128)S(1)} %iota_add_fusion, s32[1280]{0:T(1024)S(1)} %copy-done.4, f32[1280]{0:T(1024)S(1)} %copy-done.6), kind=kLoop, calls=%fused_computation.10 | loop fusion | flops 1474560 | bytes 998784 | tf_op jit(solution)/shard_map/mul | solution.py:154
  23.5 1.1 pad_maximum_fusion.tables
  24.6 2.1 %collective-permute-done.west = bf16[2,16,8,128]{3,2,1,0:T(8,128)(2,1)S(1)} collective-permute-done((bf16[2,16,8,128]{3,2,1,0:T(8,128)(2,1)S(1)}, bf16[2,16,8,128]{3,2,1,0:T(8,128)(2,1)S(1)}, u32[]{:S(2)}, u32[]{:S(2)}) %collective-permute-start) | collective-permute-done | bytes 65568 | tf_op jit(solution)/shard_map/ppermute | solution.py:277
  26.8 1.0 pad_maximum_fusion.1
  27.7 34.0 %all-to-all-done.packed = bf16[16,11,40,128]{3,2,1,0:T(8,128)(2,1)S(1)} async-done(((bf16[16,11,40,128]{3,2,1,0:T(8,128)(2,1)}), bf16[16,11,40,128]{3,2,1,0:T(8,128)(2,1)S(1)}, u32[]{:S(2)}, u32[]{:S(2)}) %all-to-all-start) | async-done | bytes 1802272 | tf_op jit(solution)/shard_map/all_to_all | solution.py:308
  61.8 0.5 shard_map.110
  62.3 27.7 %all_to_all.20 = bf16[256,8,128]{2,1,0:T(8,128)(2,1)} all-to-all(bf16[256,8,128]{2,1,0:T(8,128)(2,1)S(1)} %bitcast.9), channel_id=1, replica_groups=mesh['wave'=16,'lat'=16] {'wave','lat'}, dimensions={0} | all-to-all | bytes 1048576 | tf_op jit(solution)/shard_map/all_to_all | solution.py:314
  90.0 3.7 %shard_map.111 = bf16[16,96,128]{2,1,0:T(8,128)(2,1)} custom-call(bf16[2048,128]{1,0:T(8,128)(2,1)} %bitcast.10, f32[224,1280]{1,0:T(8,128)} %pad_maximum_fusion.tables), custom_call_target="tpu_custom_call" | custom-call | tf_op jit(solution)/shard_map/pallas_call | solution.py:180
  93.7 3.9 %collective-permute-start.2 = (bf16[16,96,128]{2,1,0:T(8,128)(2,1)}, bf16[16,96,128]{2,1,0:T(8,128)(2,1)}, u32[]{:S(2)}, u32[]{:S(2)}) collective-permute-start(bf16[16,96,128]{2,1,0:T(8,128)(2,1)} %shard_map.111), channel_id=1, source_target_pairs={{8,24},{9,25},{10,26},{11,27},{12,28},{13,29},{14,30},{15,31},{16,... | collective-permute-start | bytes 1179656 | tf_op jit(solution)/shard_map/ppermute | solution.py:322
  97.6 3.6 %all-to-all-start.2 = ((bf16[16,96,128]{2,1,0:T(8,128)(2,1)}), bf16[16,96,128]{2,1,0:T(8,128)(2,1)S(1)}, u32[]{:S(2)}, u32[]{:S(2)}) async-start(bf16[16,96,128]{2,1,0:T(8,128)(2,1)} %shard_map.111), calls=%async_computation.2 | async-start | bytes 786432 | tf_op jit(solution)/shard_map/all_to_all | solution.py:323
  101.2 2.1 %fusion.16 = (bf16[2,8,96,128]{3,2,1,0:T(8,128)(2,1)}, bf16[2,8,96,128]{3,2,1,0:T(8,128)(2,1)}) fusion(bf16[2,16,96,128]{3,2,1,0:T(8,128)(2,1)} %pad_maximum_fusion.1), kind=kLoop, calls=%fused_computation.30 | loop fusion | bytes 1572864 | tf_op jit(solution)/shard_map/slice | solution.py:313
  103.3 3.6 %collective-permute-start.3 = (bf16[2,8,96,128]{3,2,1,0:T(8,128)(2,1)}, bf16[2,8,96,128]{3,2,1,0:T(8,128)(2,1)}, u32[]{:S(2)}, u32[]{:S(2)}) collective-permute-start(bf16[2,8,96,128]{3,2,1,0:T(8,128)(2,1)} %get-tuple-element.16), channel_id=1, source_target_pairs={{0,16},{16,32},{32,48},{48,64},{64,80},{80,96},{96,112},{112,128},... | collective-permute-start | bytes 1179656 | tf_op jit(solution)/shard_map/ppermute | solution.py:277
  106.8 4.7 %collective-permute-start.4 = (bf16[2,8,96,128]{3,2,1,0:T(8,128)(2,1)}, bf16[2,8,96,128]{3,2,1,0:T(8,128)(2,1)}, u32[]{:S(2)}, u32[]{:S(2)}) collective-permute-start(bf16[2,8,96,128]{3,2,1,0:T(8,128)(2,1)} %get-tuple-element.15), channel_id=1, source_target_pairs={{16,0},{32,16},{48,32},{64,48},{80,64},{96,80},{112,96},{128,112},... | collective-permute-start | bytes 1179656 | tf_op jit(solution)/shard_map/ppermute | solution.py:282
  111.5 0.8 all-to-all-done.2.middle
  112.3 8.8 %collective-permute-done.2 = bf16[16,96,128]{2,1,0:T(8,128)(2,1)} collective-permute-done((bf16[16,96,128]{2,1,0:T(8,128)(2,1)}, bf16[16,96,128]{2,1,0:T(8,128)(2,1)}, u32[]{:S(2)}, u32[]{:S(2)}) %collective-permute-start.2) | collective-permute-done | bytes 393248 | tf_op jit(solution)/shard_map/ppermute | solution.py:322
  121.1 3.6 %all-to-all-start.3 = ((bf16[16,96,128]{2,1,0:T(8,128)(2,1)}), bf16[16,96,128]{2,1,0:T(8,128)(2,1)S(1)}, u32[]{:S(2)}, u32[]{:S(2)}) async-start(bf16[16,96,128]{2,1,0:T(8,128)(2,1)} %collective-permute-done.2), calls=%async_computation.3 | async-start | bytes 786432 | tf_op jit(solution)/shard_map/all_to_all | solution.py:324
  124.7 3.3 %collective-permute-done.3.wind_s = bf16[2,8,96,128]{3,2,1,0:T(8,128)(2,1)} collective-permute-done((bf16[2,8,96,128]{3,2,1,0:T(8,128)(2,1)}, bf16[2,8,96,128]{3,2,1,0:T(8,128)(2,1)}, u32[]{:S(2)}, u32[]{:S(2)}) %collective-permute-start.3) | collective-permute-done | bytes 393248 | tf_op jit(solution)/shard_map/ppermute | solution.py:277
  128.0 2.6 %collective-permute-done.4.wind_n = bf16[2,8,96,128]{3,2,1,0:T(8,128)(2,1)} collective-permute-done((bf16[2,8,96,128]{3,2,1,0:T(8,128)(2,1)}, bf16[2,8,96,128]{3,2,1,0:T(8,128)(2,1)}, u32[]{:S(2)}, u32[]{:S(2)}) %collective-permute-start.4) | collective-permute-done | bytes 393248 | tf_op jit(solution)/shard_map/ppermute | solution.py:282
  130.6 3.1 %all-to-all-done.3.halo = bf16[16,96,128]{2,1,0:T(8,128)(2,1)S(1)} async-done(((bf16[16,96,128]{2,1,0:T(8,128)(2,1)}), bf16[16,96,128]{2,1,0:T(8,128)(2,1)S(1)}, u32[]{:S(2)}, u32[]{:S(2)}) %all-to-all-start.3) | async-done | bytes 393248 | tf_op jit(solution)/shard_map/all_to_all | solution.py:324
  133.8 8.8 %shard_map.112 = f32[16,80,128]{2,1,0:T(8,128)} custom-call(s32[1]{0:T(128)} %bitcast.where, bf16[16,96,128]{2,1,0:T(8,128)(2,1)S(1)} %all-to-all-done.2.middle, bf16[16,96,128]{2,1,0:T(8,128)(2,1)S(1)} %all-to-all-done.3.halo, f32[16,80,128]{2,1,0:T(8,128)S(1)} %copy-done, f32[16,80,128]{2,1,0:T(8,128)S(1)} %copy-done.1, s32[16,80,128]{2,1,0:T(8,128)S(1)} %copy-done.2, ...), custom_call_target="tpu_custom_call" | custom-call | tf_op jit(solution)/shard_map/pallas_call | solution.py:260
  (20 shorter events, 0.5 us)
Async XLA Ops:
  6.7 10.9 %copy-start = (f32[16,80,128]{2,1,0:T(8,128)S(1)}, f32[16,80,128]{2,1,0:T(8,128)}, u32[]{:S(2)}) copy-start(f32[16,80,128]{2,1,0:T(8,128)} %ce.1) | copy-start | bytes 1966084
  6.7 10.9 %copy-start.1 = (f32[16,80,128]{2,1,0:T(8,128)S(1)}, f32[16,80,128]{2,1,0:T(8,128)}, u32[]{:S(2)}) copy-start(f32[16,80,128]{2,1,0:T(8,128)} %cn.1) | copy-start | bytes 1966084
  6.7 55.1 %all-to-all-start = ((bf16[16,11,40,128]{3,2,1,0:T(8,128)(2,1)}), bf16[16,11,40,128]{3,2,1,0:T(8,128)(2,1)S(1)}, u32[]{:S(2)}, u32[]{:S(2)}) async-start(bf16[16,11,40,128]{3,2,1,0:T(8,128)(2,1)} %shard_map.109), calls=%async_computation | async-start | bytes 3604480 | tf_op jit(solution)/shard_map/all_to_all | solution.py:308
  17.6 3.4 %copy-start.4 = (s32[1280]{0:T(1024)S(1)}, s32[1280]{0:T(1024)}, u32[]{:S(2)}) copy-start(s32[1280]{0:T(1024)} %constant.54.clone) | copy-start | bytes 15364
  17.6 3.8 %copy-start.5 = (s32[1280]{0:T(1024)S(1)}, s32[1280]{0:T(1024)}, u32[]{:S(2)}) copy-start(s32[1280]{0:T(1024)} %constant.63) | copy-start | bytes 15364
  17.6 3.8 %copy-start.6 = (f32[1280]{0:T(1024)S(1)}, f32[1280]{0:T(1024)}, u32[]{:S(2)}) copy-start(f32[1280]{0:T(1024)} %constant.62) | copy-start | bytes 15364
  19.1 5.5 %collective-permute-start.1 = (bf16[2,16,8,128]{3,2,1,0:T(8,128)(2,1)S(1)}, bf16[2,16,8,128]{3,2,1,0:T(8,128)(2,1)S(1)}, u32[]{:S(2)}, u32[]{:S(2)}) collective-permute-start(bf16[2,16,8,128]{3,2,1,0:T(8,128)(2,1)S(1)} %get-tuple-element.18), channel_id=1, source_target_pairs={{1,0},{2,1},{3,2},{4,3},{5,4},{6,5},{7,6},{8,7},{9,8},{10,9},{11,1... | collective-permute-start | bytes 196616 | tf_op jit(solution)/shard_map/ppermute | solution.py:282
  21.0 5.8 %collective-permute-start = (bf16[2,16,8,128]{3,2,1,0:T(8,128)(2,1)S(1)}, bf16[2,16,8,128]{3,2,1,0:T(8,128)(2,1)S(1)}, u32[]{:S(2)}, u32[]{:S(2)}) collective-permute-start(bf16[2,16,8,128]{3,2,1,0:T(8,128)(2,1)S(1)} %get-tuple-element.17), channel_id=1, source_target_pairs={{0,1},{1,2},{2,3},{3,4},{4,5},{5,6},{6,7},{7,8},{8,9},{9,10},{10,1... | collective-permute-start | bytes 196616 | tf_op jit(solution)/shard_map/ppermute | solution.py:277
  93.7 40.1 %copy-start.2 = (s32[16,80,128]{2,1,0:T(8,128)S(1)}, s32[16,80,128]{2,1,0:T(8,128)}, u32[]{:S(2)}) copy-start(s32[16,80,128]{2,1,0:T(8,128)} %ef.1) | copy-start | bytes 1966084
  93.7 40.1 %copy-start.3 = (s32[16,80,128]{2,1,0:T(8,128)S(1)}, s32[16,80,128]{2,1,0:T(8,128)}, u32[]{:S(2)}) copy-start(s32[16,80,128]{2,1,0:T(8,128)} %nf.1) | copy-start | bytes 1966084
  93.7 27.4 %collective-permute-start.2 = (bf16[16,96,128]{2,1,0:T(8,128)(2,1)}, bf16[16,96,128]{2,1,0:T(8,128)(2,1)}, u32[]{:S(2)}, u32[]{:S(2)}) collective-permute-start(bf16[16,96,128]{2,1,0:T(8,128)(2,1)} %shard_map.111), channel_id=1, source_target_pairs={{8,24},{9,25},{10,26},{11,27},{12,28},{13,29},{14,30},{15,31},{16,... | collective-permute-start | bytes 1179656 | tf_op jit(solution)/shard_map/ppermute | solution.py:322
  97.6 14.7 %all-to-all-start.2 = ((bf16[16,96,128]{2,1,0:T(8,128)(2,1)}), bf16[16,96,128]{2,1,0:T(8,128)(2,1)S(1)}, u32[]{:S(2)}, u32[]{:S(2)}) async-start(bf16[16,96,128]{2,1,0:T(8,128)(2,1)} %shard_map.111), calls=%async_computation.2 | async-start | bytes 786432 | tf_op jit(solution)/shard_map/all_to_all | solution.py:323
  103.3 24.7 %collective-permute-start.3 = (bf16[2,8,96,128]{3,2,1,0:T(8,128)(2,1)}, bf16[2,8,96,128]{3,2,1,0:T(8,128)(2,1)}, u32[]{:S(2)}, u32[]{:S(2)}) collective-permute-start(bf16[2,8,96,128]{3,2,1,0:T(8,128)(2,1)} %get-tuple-element.16), channel_id=1, source_target_pairs={{0,16},{16,32},{32,48},{48,64},{64,80},{80,96},{96,112},{112,128},... | collective-permute-start | bytes 1179656 | tf_op jit(solution)/shard_map/ppermute | solution.py:277
  106.8 23.8 %collective-permute-start.4 = (bf16[2,8,96,128]{3,2,1,0:T(8,128)(2,1)}, bf16[2,8,96,128]{3,2,1,0:T(8,128)(2,1)}, u32[]{:S(2)}, u32[]{:S(2)}) collective-permute-start(bf16[2,8,96,128]{3,2,1,0:T(8,128)(2,1)} %get-tuple-element.15), channel_id=1, source_target_pairs={{16,0},{32,16},{48,32},{64,48},{80,64},{96,80},{112,96},{128,112},... | collective-permute-start | bytes 1179656 | tf_op jit(solution)/shard_map/ppermute | solution.py:282
  121.1 12.6 %all-to-all-start.3 = ((bf16[16,96,128]{2,1,0:T(8,128)(2,1)}), bf16[16,96,128]{2,1,0:T(8,128)(2,1)S(1)}, u32[]{:S(2)}, u32[]{:S(2)}) async-start(bf16[16,96,128]{2,1,0:T(8,128)(2,1)} %collective-permute-done.2), calls=%async_computation.3 | async-start | bytes 786432 | tf_op jit(solution)/shard_map/all_to_all | solution.py:324

commit v4 on v3

--- a/solution.py
+++ b/solution.py
@@ -22,78 +22,124 @@
 HALO = 2 * STEPS
 EXT_X = TILE_X + 2 * HALO
 EXT_R = TILE_R + 2 * HALO
-PAIRS = 5
+GROUP = 5
 SLOTS = 8
-GROUP = 5
-PAIR_OF = (((0, 0), (0, 1), (1, 0), (1, 1), (2, 0)), ((4, 0), (4, 1), (3, 0), (3, 1), (2, 1)))
-ORDER_SLOT = (0, 0, 1, 1, 2)
-R_STEP = 8
+ORDER_OF = ((0, 1, 2), (4, 3, 2))
+SHARE = 24
+SIZE_OF = (ROWS, ROWS, SHARE)
+START_OF = (0, ROWS, 2 * ROWS)
+PART_ROWS = 2 * ROWS + SHARE
+CHUNK = 8
+CHUNKS = ROWS // CHUNK
 FAR = 16
-BLOCKS = PAIRS + 6
+COLUMNS = 3 * LATS
+SOUTH_ROWS = HALO - 1
+NORTH_ROWS = HALO - 2
 PARAMS = pltpu.CompilerParams(vmem_limit_bytes=24 * 1024 * 1024)
 
 
-def packing_kernel(wavenumber, first, control, vert, pick, legendre, out, scratch):
-    step = pl.program_id(0)
-    for i in range(R_STEP):
-        m = step * R_STEP + i
-        z = m // GROUP
-        place = m - GROUP * z
-        late = place > 2
-        w = 2 * z + jnp.where(late, 1, 0)
-        slot = PAIRS + 2 * jnp.where(late, GROUP - 1 - place, place)
-        for h in range(2):
-            half = legendre[i, :, h * LEV : (h + 1) * LEV]
-            out[w, slot + h] = half
-
-            @pl.when(place == 2)
-            def _():
-                out[w + 1, slot + h] = half
-
-    parts = jnp.dot(control[...], pick[...], preferred_element_type=jnp.float32)
+def owned(w, slot):
+    order = GROUP * (w // 2) + ORDER_OF[w % 2][slot]
+    return order, ROWS - SHARE if slot == 2 and w % 2 else 0, SIZE_OF[slot]
+
+
+def packing_kernel(
+    wavenumber, first, control, vert, legendre, out, cbuf, vbuf, scratch, whole, share, isem, osem
+):
+    loads = []
+    for i in range(CHUNKS):
+        rows = pl.ds(i * CHUNK * ORDERS, CHUNK * ORDERS)
+        mats = pl.ds(i * CHUNK, CHUNK)
+        loads.append(
+            (
+                pltpu.make_async_copy(control.at[rows], cbuf.at[rows], isem.at[0, i]),
+                pltpu.make_async_copy(vert.at[mats], vbuf.at[mats], isem.at[1, i]),
+            )
+        )
+    for pair in loads:
+        for load in pair:
+            load.start()
+    sends = []
+    for w in range(WAVE):
+        for slot in range(3):
+            order, start, size = owned(w, slot)
+            sends.append(
+                pltpu.make_async_copy(
+                    legendre.at[order, pl.ds(start, size)],
+                    out.at[w, pl.ds(PART_ROWS + START_OF[slot], size)],
+                    osem.at[0, w, slot],
+                )
+            )
+            sends[-1].start()
+    row_id = lax.broadcasted_iota(jnp.int32, (2 * LEV, 2 * LEV), 0)
+    column = lax.broadcasted_iota(jnp.int32, (2 * LEV, 2 * LEV), 1)
+    chosen = column == (row_id & 1) * LEV + (row_id >> 1)
+    pick = jnp.where(chosen, 1.0, 0.0).astype(jnp.bfloat16)
     orders = first[0] + lax.broadcasted_iota(jnp.int32, (ORDERS, 2 * LEV), 0)
-    for i in range(R_STEP):
-        r = step * R_STEP + i
-        rows = jnp.where(wavenumber[r] >= orders, parts[i * ORDERS : (i + 1) * ORDERS], 0.0)
-        both = jnp.concatenate([rows[:, :LEV], rows[:, LEV:]], axis=0).astype(jnp.bfloat16)
-        mixed = lax.dot_general(
-            both, vert[i], (((1,), (1,)), ((), ())), preferred_element_type=jnp.float32
+    for i in range(CHUNKS):
+        for load in loads[i]:
+            load.wait()
+        parts = jnp.dot(
+            cbuf[i * CHUNK * ORDERS : (i + 1) * CHUNK * ORDERS],
+            pick,
+            preferred_element_type=jnp.float32,
         )
-        for p in range(2):
-            scratch[p, pl.ds(r, ORDERS, stride=ROWS), :] = mixed[p * ORDERS : (p + 1) * ORDERS]
-
-    @pl.when(step == pl.num_programs(0) - 1)
-    def _():
-        for w in range(WAVE):
-            for b in range(PAIRS):
-                m, p = PAIR_OF[w % 2][b]
-                m += GROUP * (w // 2)
-                out[w, b] = scratch[p, m * ROWS : (m + 1) * ROWS, :].astype(jnp.bfloat16)
+        for k in range(CHUNK):
+            r = i * CHUNK + k
+            rows = jnp.where(wavenumber[r] >= orders, parts[k * ORDERS : (k + 1) * ORDERS], 0.0)
+            both = jnp.concatenate([rows[:, :LEV], rows[:, LEV:]], axis=0).astype(jnp.bfloat16)
+            mixed = lax.dot_general(
+                both, vbuf[r], (((1,), (1,)), ((), ())), preferred_element_type=jnp.float32
+            )
+            for p in range(2):
+                scratch[p, pl.ds(r, ORDERS, stride=ROWS), :] = mixed[p * ORDERS : (p + 1) * ORDERS]
+    for w in range(WAVE):
+        for slot in range(3):
+            order, start, size = owned(w, slot)
+            base = order * ROWS + start
+            values = jnp.concatenate(
+                [scratch[0, base : base + size], scratch[1, base : base + size]], axis=1
+            )
+            if slot < 2:
+                kept = whole.at[w, slot]
+            else:
+                kept = share.at[w]
+                if w % 2:
+                    own = lax.broadcasted_iota(jnp.int32, values.shape, 0) >= 2 * SHARE - ROWS
+                    values = jnp.where(own, values, 0.0)
+            kept[...] = values.astype(jnp.bfloat16)
+            sends.append(
+                pltpu.make_async_copy(
+                    kept, out.at[w, pl.ds(START_OF[slot], size)], osem.at[1, w, slot]
+                )
+            )
+            sends[-1].start()
+    for send in sends:
+        send.wait()
 
 
 def packed_inputs(control, vert_root, legendre, row_wavenumber, first_order):
-    pick = np.zeros((2 * LEV, 2 * LEV), np.float32)
-    pick[np.arange(2 * LEV), np.arange(2 * LEV) % 2 * LEV + np.arange(2 * LEV) // 2] = 1.0
+    smem = pl.BlockSpec(memory_space=pltpu.SMEM)
+    far = pl.BlockSpec(memory_space=pltpu.HBM)
     return pl.pallas_call(
         packing_kernel,
-        grid=(ROWS // R_STEP,),
-        in_specs=[
-            pl.BlockSpec(memory_space=pltpu.SMEM),
-            pl.BlockSpec(memory_space=pltpu.SMEM),
-            pl.BlockSpec((R_STEP * ORDERS, 2 * LEV), lambda i: (i, 0)),
-            pl.BlockSpec((R_STEP, LEV, LEV), lambda i: (i, 0, 0)),
-            pl.BlockSpec((2 * LEV, 2 * LEV), lambda i: (0, 0)),
-            pl.BlockSpec((R_STEP, ROWS, LATS), lambda i: (i, 0, 0)),
+        in_specs=[smem, smem, far, far, far],
+        out_specs=far,
+        out_shape=jax.ShapeDtypeStruct((WAVE, 2 * PART_ROWS, 2 * LEV), jnp.bfloat16),
+        scratch_shapes=[
+            pltpu.VMEM((ROWS * ORDERS, 2 * LEV), jnp.bfloat16),
+            pltpu.VMEM((ROWS, LEV, LEV), jnp.bfloat16),
+            pltpu.VMEM((2, ORDERS * ROWS, LEV), jnp.float32),
+            pltpu.VMEM((WAVE, 2, ROWS, 2 * LEV), jnp.bfloat16),
+            pltpu.VMEM((WAVE, SHARE, 2 * LEV), jnp.bfloat16),
+            pltpu.SemaphoreType.DMA((2, CHUNKS)),
+            pltpu.SemaphoreType.DMA((2, WAVE, 3)),
         ],
-        out_specs=pl.BlockSpec((WAVE, BLOCKS, ROWS, LEV), lambda i: (0, 0, 0, 0)),
-        out_shape=jax.ShapeDtypeStruct((WAVE, BLOCKS, ROWS, LEV), jnp.bfloat16),
-        scratch_shapes=[pltpu.VMEM((2, ORDERS * ROWS, LEV), jnp.float32)],
     )(
         row_wavenumber,
         first_order[None],
         control.reshape(ROWS * ORDERS, 2 * LEV),
         vert_root,
-        jnp.asarray(pick, jnp.bfloat16),
         legendre,
     )
 
@@ -101,23 +147,20 @@
 def modes_kernel(packed, out, left, right, result):
     result[...] = jnp.zeros(result.shape, jnp.float32)
     for slot in range(3):
-        pairs = [b for b in range(PAIRS) if ORDER_SLOT[b] == slot]
+        size = SIZE_OF[slot]
         for s in range(WAVE):
-            rows = slice(s * ROWS, (s + 1) * ROWS)
-            for h in range(2):
-                half = packed[s, PAIRS + 2 * slot + h]
-                left[rows, h * LEV : (h + 1) * LEV] = half.astype(jnp.float32)
-            for i, b in enumerate(pairs):
-                right[rows, i * LEV : (i + 1) * LEV] = packed[s, b].astype(jnp.float32)
-        width = len(pairs) * LEV
+            rows = slice(s * size, (s + 1) * size)
+            for start, side in ((START_OF[slot], right), (PART_ROWS + START_OF[slot], left)):
+                block = packed[s, start // 8 : (start + size) // 8].astype(jnp.float32)
+                side[rows, :] = block.reshape(size, 2 * LEV)
         total = lax.dot_general(
-            left[...].astype(jnp.bfloat16),
-            right[:, :width].astype(jnp.bfloat16),
+            left[0 : WAVE * size].astype(jnp.bfloat16),
+            right[0 : WAVE * size].astype(jnp.bfloat16),
             (((0,), (0,)), ((), ())),
             preferred_element_type=jnp.float32,
         )
-        for i, b in enumerate(pairs):
-            result[pl.ds(b, LATS, stride=SLOTS), :] = total[:, i * LEV : (i + 1) * LEV]
+        for p in range(2):
+            result[pl.ds(2 * slot + p, LATS, stride=SLOTS), :] = total[:, p * LEV : (p + 1) * LEV]
     out[...] = result[...].astype(jnp.bfloat16)
 
 
@@ -131,49 +174,52 @@
             pltpu.VMEM((LATS * SLOTS, LEV), jnp.float32),
         ],
         compiler_params=PARAMS,
-    )(packed)
+    )(packed.reshape(WAVE, PART_ROWS // 4, 8, 2 * LEV))
 
 
 def angle_tables():
-    order = np.zeros((PAIRS, WAVE, LAT), np.int32)
-    part = np.zeros((PAIRS, WAVE, LAT), np.int32)
+    order = np.zeros((3, WAVE, LAT), np.int32)
     for w in range(WAVE):
-        for b, (m, p) in enumerate(PAIR_OF[w % 2]):
-            order[b, w] = np.arange(LAT) * ORDERS + GROUP * (w // 2) + m
-            part[b, w] = p
-    order, part = (jnp.asarray(a.reshape(-1)) for a in (order, part))
+        for slot in range(3):
+            order[slot, w] = np.arange(LAT) * ORDERS + owned(w, slot)[0]
+    order = jnp.asarray(order.reshape(-1))
     weight = jnp.where(order == 0, 1.0, 2.0).astype(jnp.float32) * (1.0 / math.sqrt(NLON))
 
     def turn(steps):
         return (steps % NLON).astype(jnp.float32) * (2.0 * math.pi / NLON)
 
     local = jnp.arange(EXT_X, dtype=jnp.int32) - HALO + NLON
-    near = turn(order[None, :] * local[:, None] + part[None, :] * (NLON // 4))
+    near = turn(order[None, :] * local[:, None])
     far = turn(order[None, :] * (TILE_X * jnp.arange(FAR, dtype=jnp.int32))[:, None])
     return jnp.concatenate(
-        [weight * jnp.cos(near), weight * jnp.sin(near), jnp.cos(far), jnp.sin(far)]
-    )
-
-
-def fourier_kernel(modes, tables, out, wide, rhs):
-    near_cos = tables.at[0:EXT_X]
-    near_sin = tables.at[EXT_X : 2 * EXT_X]
-    far_cos = tables.at[2 * EXT_X : 2 * EXT_X + FAR]
-    far_sin = tables.at[2 * EXT_X + FAR : 2 * EXT_X + 2 * FAR]
+        [weight * jnp.cos(near), -weight * jnp.sin(near), jnp.cos(far), jnp.sin(far)]
+    )
+
+
+def fourier_kernel(modes, local, out, wide, rhs):
     wide[...] = modes[...].astype(jnp.float32)
-    for b in range(PAIRS):
-        rhs[b * LATS : (b + 1) * LATS] = wide[pl.ds(b, LATS, stride=SLOTS), :].astype(jnp.bfloat16)
-
-    def put(band, basis):
-        total = jnp.dot(basis.astype(jnp.bfloat16), rhs[...], preferred_element_type=jnp.float32)
+    for p in range(2):
+        for slot in range(3):
+            rows = wide[pl.ds(2 * slot + p, LATS, stride=SLOTS), :]
+            start = p * COLUMNS + slot * LATS
+            rhs[start : start + LATS] = rows.astype(jnp.bfloat16)
+
+    def put(band, real, imaginary):
+        basis = jnp.concatenate(
+            [real.astype(jnp.bfloat16), imaginary.astype(jnp.bfloat16)], axis=1
+        )
+        total = jnp.dot(basis, rhs[...], preferred_element_type=jnp.float32)
         out[band] = total.astype(jnp.bfloat16)
 
     for b in range(LAT // 2 + 1):
-        even = far_cos[b : b + 1, :] * near_cos[...]
-        odd = far_sin[b : b + 1, :] * near_sin[...]
-        put(b, even - odd)
+        far_cos = local[2 * EXT_X + b : 2 * EXT_X + b + 1, :]
+        far_sin = local[2 * EXT_X + FAR + b : 2 * EXT_X + FAR + b + 1, :]
+        near_cos, near_sin = local[0:EXT_X], local[EXT_X : 2 * EXT_X]
+        cc, ss = far_cos * near_cos, far_sin * near_sin
+        cs, sc = far_cos * near_sin, far_sin * near_cos
+        put(b, cc + ss, cs - sc)
         if 0 < b < LAT // 2:
-            put(LAT - b, even + odd)
+            put(LAT - b, cc - ss, cs + sc)
 
 
 def latitude_row(modes, tables):
@@ -182,7 +228,7 @@
         out_shape=jax.ShapeDtypeStruct((LAT, EXT_X, LEV), jnp.bfloat16),
         scratch_shapes=[
             pltpu.VMEM((LATS * SLOTS, LEV), jnp.float32),
-            pltpu.VMEM((LATS * PAIRS, LEV), jnp.bfloat16),
+            pltpu.VMEM((2 * COLUMNS, LEV), jnp.bfloat16),
         ],
     )(modes, tables)
 
@@ -211,8 +257,8 @@
     qb[HALO + TILE_R :] = jnp.zeros((HALO, EXT_X, LEV), jnp.float32)
     inner = slice(HALO, HALO + TILE_R)
     for d, (size, flag) in enumerate(((ce, ef), (cn, nf))):
-        us[d, 0:HALO] = wind_s[d].astype(jnp.float32)
-        us[d, HALO + TILE_R :] = wind_n[d].astype(jnp.float32)
+        us[d, HALO - SOUTH_ROWS : HALO] = wind_s[d].astype(jnp.float32)
+        us[d, HALO + TILE_R : HALO + TILE_R + NORTH_ROWS] = wind_n[d].astype(jnp.float32)
         us[d, inner, 0:HALO] = west[d].astype(jnp.float32)
         us[d, inner, HALO + TILE_X :] = east[d].astype(jnp.float32)
         us[d, inner, HALO : HALO + TILE_X] = jnp.where(flag[...] > 0, size[...], -size[...])
@@ -223,7 +269,7 @@
             gs[d, r] = 0.5 * speed * (1.0 - speed)
         return carry
 
-    lax.fori_loop(0, EXT_R, gains, 0)
+    lax.fori_loop(HALO - SOUTH_ROWS, HALO + TILE_R + NORTH_ROWS, gains, 0)
     for t in range(1, STEPS + 1):
         old, new = (qa, qb) if t % 2 else (qb, qa)
         low = jnp.where(band == 0, HALO, 2 * t)
@@ -309,8 +355,8 @@
     packed, wide, tables = lax.optimization_barrier((packed, wide, tables))
     modes = modes_of(packed)
     modes, wide = lax.optimization_barrier((modes, wide))
-    wind_s = from_below(wide[:, -HALO:], "wave", False)
-    wind_n = from_above(wide[:, :HALO], "wave", False)
+    wind_s = from_below(wide[:, -SOUTH_ROWS:], "wave", False)
+    wind_n = from_above(wide[:, :NORTH_ROWS], "wave", False)
     modes = lax.all_to_all(modes.reshape(LATS, SLOTS, LEV), ("wave", "lat"), 0, 0, tiled=True)
     row = latitude_row(modes.reshape(LATS * SLOTS, LEV), tables)
     pairs = []

time: 145 us -> 170 us (1.17)
  Pallas kernels: 19.7 us -> 41.7 us
  blocking collectives: 27.7 us -> 42.4 us
  waiting for transfers between devices: 54.8 us -> 46.7 us
  starting transfers between devices: 32 us -> 28.4 us
    pallas_call x1, Pallas kernels: 6.68 us -> 28.6 us  [packed_inputs(): pl.pallas_call(packing_kernel, in_specs=[smem, smem, far, far, far], out_...]
    all_to_all x0 -> x1, blocking collectives: none -> 14.7 us  [per_device(): middle = lax.all_to_all(row, 'lat', 0, 0, tiled=True)]
    ppermute x2, waiting for transfers between devices: 2.65 us -> 11.5 us  [from_above(): return lax.ppermute(block, axis, pairs)]
    ppermute x1, waiting for transfers between devices: 8.81 us -> 0.01 us  [per_device(): next_row = lax.ppermute(row, ('wave', 'lat'), pairs)]
    all_to_all x1 -> x0, starting transfers between devices: 3.57 us -> none  [per_device(): middle = lax.all_to_all(row, 'lat', 0, 0, tiled=True)]
    all_to_all x1, waiting for transfers between devices: 3.11 us -> 0.01 us  [per_device(): halo = lax.all_to_all(next_row, 'lat', 0, 0, tiled=True)]
    all_to_all x1, waiting for transfers between devices: 34 us -> 31.9 us  [per_device(): packed = lax.all_to_all(packed, 'wave', 0, 0, tiled=True)]
    ppermute x2, waiting for transfers between devices: 5.45 us -> 3.29 us  [from_below(): return lax.ppermute(block, axis, pairs)]
  transfers between devices with their start and end apart: 8 -> 7, of which waited for: 7 -> 3; matrix products, arithmetic and copies ran while one was open for 6% -> 5% of each run, Pallas kernels for 0% -> 0%
where the time goes in v4:
time: 170 us; the launch traced here: 168 us
  waiting for transfers between devices  46.7 us (27%)
  blocking collectives  42.4 us (25%)
  Pallas kernels  41.7 us (25%)
  starting transfers between devices  28.4 us (17%)
  other arithmetic  4.93 us (3%)
  local copies, waits for them, and re-layouts  3.49 us (2%)
    all_to_all x1, waiting for transfers between devices, per_device(): packed = lax.all_to_all(packed, 'wave', 0, 0, tiled=True)  31.9 us
    pallas_call x1, Pallas kernels, packed_inputs(): pl.pallas_call(packing_kernel, in_specs=[smem, smem, far, far, far], out_...  28.6 us
    all_to_all x1, blocking collectives, per_device(): lax.all_to_all(modes.reshape(LATS, SLOTS, LEV), ('wave', 'lat'), 0, 0, ti...  27.8 us
    all_to_all x1, blocking collectives, per_device(): middle = lax.all_to_all(row, 'lat', 0, 0, tiled=True)  14.7 us
    ppermute x2, waiting for transfers between devices, from_above(): return lax.ppermute(block, axis, pairs)  11.5 us
    all_to_all x1, starting transfers between devices, per_device(): packed = lax.all_to_all(packed, 'wave', 0, 0, tiled=True)  10.9 us
    pallas_call x1, Pallas kernels, advected(): pl.pallas_call(advect_kernel, in_specs=[pl.BlockSpec(memory_space=pltpu.S...  8.64 us
    ppermute x2, starting transfers between devices, from_above(): return lax.ppermute(block, axis, pairs)  6.63 us
  transfers between devices with their start and end apart: 7, of which 3 were waited for; matrix products, arithmetic and copies ran while one was open for 5% of the time, Pallas kernels for 0%

profile of v4, /device:TPU:64, one launch (start us, length us, event | category | flops | bytes accessed | tf_op | source)
XLA Modules:
  0.0 167.9 jit_solution(9940875362844806854)
XLA Ops:
  0.0 28.6 %shard_map.91 = bf16[16,208,256]{2,1,0:T(8,128)(2,1)} custom-call(s32[40]{0:T(128)} %wavenumber.1, s32[1]{0:T(128)} %bitcast.1.first, bf16[1600,256]{1,0:T(8,128)(2,1)} %bitcast.13, bf16[40,128,128]{2,1,0:T(8,128)(2,1)} %vert.1, bf16[40,40,256]{2,1,0:T(8,128)(2,1)} %legendre.1), custom_call_target="tpu_custom_call" | custom-call | tf_op jit(solution)/shard_map/pallas_call | solution.py:124
  28.6 10.9 %all-to-all-start = ((bf16[16,208,256]{2,1,0:T(8,128)(2,1)}), bf16[16,208,256]{2,1,0:T(8,128)(2,1)S(1)}, u32[]{:S(2)}, u32[]{:S(2)}) async-start(bf16[16,208,256]{2,1,0:T(8,128)(2,1)} %shard_map.91), calls=%async_computation | async-start | bytes 3407872 | tf_op jit(solution)/shard_map/all_to_all | solution.py:354
  39.6 0.0 copy-start.4
  39.6 0.0 copy-start.5
  39.6 1.5 fusion.2
  41.1 1.8 %collective-permute-start.1 = (bf16[2,16,8,128]{3,2,1,0:T(8,128)(2,1)S(1)}, bf16[2,16,8,128]{3,2,1,0:T(8,128)(2,1)S(1)}, u32[]{:S(2)}, u32[]{:S(2)}) collective-permute-start(bf16[2,16,8,128]{3,2,1,0:T(8,128)(2,1)S(1)} %get-tuple-element.16), channel_id=1, source_target_pairs={{1,0},{2,1},{3,2},{4,3},{5,4},{6,5},{7,6},{8,7},{9,8},{10,9},{11,1... | collective-permute-start | bytes 196616 | tf_op jit(solution)/shard_map/ppermute | solution.py:328
  43.0 0.3 fusion.14
  43.3 1.3 cosine_multiply_fusion
  44.6 0.9 pad_maximum_fusion.1.local
  45.5 3.3 %collective-permute-done.west = bf16[2,16,8,128]{3,2,1,0:T(8,128)(2,1)S(1)} collective-permute-done((bf16[2,16,8,128]{3,2,1,0:T(8,128)(2,1)S(1)}, bf16[2,16,8,128]{3,2,1,0:T(8,128)(2,1)S(1)}, u32[]{:S(2)}, u32[]{:S(2)}) %collective-permute-start) | collective-permute-done | bytes 65568 | tf_op jit(solution)/shard_map/ppermute | solution.py:323
  48.7 1.0 pad_maximum_fusion
  49.7 31.9 %all-to-all-done = bf16[16,208,256]{2,1,0:T(8,128)(2,1)S(1)} async-done(((bf16[16,208,256]{2,1,0:T(8,128)(2,1)}), bf16[16,208,256]{2,1,0:T(8,128)(2,1)S(1)}, u32[]{:S(2)}, u32[]{:S(2)}) %all-to-all-start) | async-done | bytes 1703968 | tf_op jit(solution)/shard_map/all_to_all | solution.py:354
  81.6 0.6 shard_map.92
  82.2 27.8 %all_to_all.20 = bf16[256,8,128]{2,1,0:T(8,128)(2,1)} all-to-all(bf16[256,8,128]{2,1,0:T(8,128)(2,1)S(1)} %bitcast.11), channel_id=1, replica_groups=mesh['wave'=16,'lat'=16] {'wave','lat'}, dimensions={0} | all-to-all | bytes 1048576 | tf_op jit(solution)/shard_map/all_to_all | solution.py:360
  109.9 3.9 %shard_map.93 = bf16[16,96,128]{2,1,0:T(8,128)(2,1)} custom-call(bf16[2048,128]{1,0:T(8,128)(2,1)} %bitcast.12, f32[224,768]{1,0:T(8,128)} %pad_maximum_fusion.1.local), custom_call_target="tpu_custom_call" | custom-call | tf_op jit(solution)/shard_map/pallas_call | solution.py:226
  113.8 3.9 %collective-permute-start.2 = (bf16[16,96,128]{2,1,0:T(8,128)(2,1)}, bf16[16,96,128]{2,1,0:T(8,128)(2,1)}, u32[]{:S(2)}, u32[]{:S(2)}) collective-permute-start(bf16[16,96,128]{2,1,0:T(8,128)(2,1)} %shard_map.93), channel_id=1, source_target_pairs={{8,24},{9,25},{10,26},{11,27},{12,28},{13,29},{14,30},{15,31},{16,... | collective-permute-start | bytes 1179656 | tf_op jit(solution)/shard_map/ppermute | solution.py:368
  117.7 14.7 %all_to_all.21.middle = bf16[16,96,128]{2,1,0:T(8,128)(2,1)S(1)} all-to-all(bf16[16,96,128]{2,1,0:T(8,128)(2,1)} %shard_map.93), channel_id=1, replica_groups=mesh['wave'=16,'lat'=16] {'lat'}, dimensions={0} | all-to-all | bytes 786432 | tf_op jit(solution)/shard_map/all_to_all | solution.py:369
  132.4 3.6 %all-to-all-start.3 = ((bf16[16,96,128]{2,1,0:T(8,128)(2,1)}), bf16[16,96,128]{2,1,0:T(8,128)(2,1)S(1)}, u32[]{:S(2)}, u32[]{:S(2)}) async-start(bf16[16,96,128]{2,1,0:T(8,128)(2,1)} %collective-permute-done.2), calls=%async_computation.3 | async-start | bytes 786432 | tf_op jit(solution)/shard_map/all_to_all | solution.py:370
  136.0 1.7 %slice.14 = bf16[2,7,96,128]{3,2,1,0:T(8,128)(2,1)} slice(bf16[2,16,96,128]{3,2,1,0:T(8,128)(2,1)} %pad_maximum_fusion), slice={[0:2], [9:16], [0:96], [0:128]} | slice | bytes 688128 | tf_op jit(solution)/shard_map/slice | solution.py:358
  137.7 3.4 %collective-permute-start.3 = (bf16[2,7,96,128]{3,2,1,0:T(8,128)(2,1)}, bf16[2,7,96,128]{3,2,1,0:T(8,128)(2,1)}, u32[]{:S(2)}, u32[]{:S(2)}) collective-permute-start(bf16[2,7,96,128]{3,2,1,0:T(8,128)(2,1)} %slice.14), channel_id=1, source_target_pairs={{0,16},{16,32},{32,48},{48,64},{64,80},{80,96},{96,112},{112,128},... | collective-permute-start | bytes 1032200 | tf_op jit(solution)/shard_map/ppermute | solution.py:323
  141.1 1.7 %slice.15 = bf16[2,6,96,128]{3,2,1,0:T(8,128)(2,1)} slice(bf16[2,16,96,128]{3,2,1,0:T(8,128)(2,1)} %pad_maximum_fusion), slice={[0:2], [0:6], [0:96], [0:128]} | slice | bytes 589824 | tf_op jit(solution)/shard_map/slice | solution.py:359
  142.9 4.8 %collective-permute-start.4 = (bf16[2,6,96,128]{3,2,1,0:T(8,128)(2,1)}, bf16[2,6,96,128]{3,2,1,0:T(8,128)(2,1)}, u32[]{:S(2)}, u32[]{:S(2)}) collective-permute-start(bf16[2,6,96,128]{3,2,1,0:T(8,128)(2,1)} %slice.15), channel_id=1, source_target_pairs={{16,0},{32,16},{48,32},{64,48},{80,64},{96,80},{112,96},{128,112},... | collective-permute-start | bytes 884744 | tf_op jit(solution)/shard_map/ppermute | solution.py:328
  147.7 11.5 %collective-permute-done.4.wind_n = bf16[2,6,96,128]{3,2,1,0:T(8,128)(2,1)} collective-permute-done((bf16[2,6,96,128]{3,2,1,0:T(8,128)(2,1)}, bf16[2,6,96,128]{3,2,1,0:T(8,128)(2,1)}, u32[]{:S(2)}, u32[]{:S(2)}) %collective-permute-start.4) | collective-permute-done | bytes 294944 | tf_op jit(solution)/shard_map/ppermute | solution.py:328
  159.2 8.6 %shard_map.94 = f32[16,80,128]{2,1,0:T(8,128)} custom-call(s32[1]{0:T(128)} %bitcast.where, bf16[16,96,128]{2,1,0:T(8,128)(2,1)S(1)} %all_to_all.21.middle, bf16[16,96,128]{2,1,0:T(8,128)(2,1)S(1)} %all-to-all-done.3.halo, f32[16,80,128]{2,1,0:T(8,128)S(1)} %copy-done, f32[16,80,128]{2,1,0:T(8,128)S(1)} %copy-done.1, s32[16,80,128]{2,1,0:T(8,128)S(1)} %copy-done.2, ...), custom_call_target="tpu_custom_call" | custom-call | tf_op jit(solution)/shard_map/pallas_call | solution.py:306
  (20 shorter events, 0.1 us)
Async XLA Ops:
  28.6 10.9 %copy-start = (f32[16,80,128]{2,1,0:T(8,128)S(1)}, f32[16,80,128]{2,1,0:T(8,128)}, u32[]{:S(2)}) copy-start(f32[16,80,128]{2,1,0:T(8,128)} %ce.1) | copy-start | bytes 1966084
  28.6 10.9 %copy-start.1 = (f32[16,80,128]{2,1,0:T(8,128)S(1)}, f32[16,80,128]{2,1,0:T(8,128)}, u32[]{:S(2)}) copy-start(f32[16,80,128]{2,1,0:T(8,128)} %cn.1) | copy-start | bytes 1966084
  28.6 52.9 %all-to-all-start = ((bf16[16,208,256]{2,1,0:T(8,128)(2,1)}), bf16[16,208,256]{2,1,0:T(8,128)(2,1)S(1)}, u32[]{:S(2)}, u32[]{:S(2)}) async-start(bf16[16,208,256]{2,1,0:T(8,128)(2,1)} %shard_map.91), calls=%async_computation | async-start | bytes 3407872 | tf_op jit(solution)/shard_map/all_to_all | solution.py:354
  39.6 3.4 %copy-start.4 = (s32[768]{0:T(1024)S(1)}, s32[768]{0:T(1024)}, u32[]{:S(2)}) copy-start(s32[768]{0:T(1024)} %constant.47.clone) | copy-start | bytes 9220
  39.6 3.7 %copy-start.5 = (f32[768]{0:T(1024)S(1)}, f32[768]{0:T(1024)}, u32[]{:S(2)}) copy-start(f32[768]{0:T(1024)} %constant.54) | copy-start | bytes 9220
  39.6 3.7 %copy-start.6 = (f32[768]{0:T(1024)S(1)}, f32[768]{0:T(1024)}, u32[]{:S(2)}) copy-start(f32[768]{0:T(1024)} %constant.55) | copy-start | bytes 9220
  41.1 4.3 %collective-permute-start.1 = (bf16[2,16,8,128]{3,2,1,0:T(8,128)(2,1)S(1)}, bf16[2,16,8,128]{3,2,1,0:T(8,128)(2,1)S(1)}, u32[]{:S(2)}, u32[]{:S(2)}) collective-permute-start(bf16[2,16,8,128]{3,2,1,0:T(8,128)(2,1)S(1)} %get-tuple-element.16), channel_id=1, source_target_pairs={{1,0},{2,1},{3,2},{4,3},{5,4},{6,5},{7,6},{8,7},{9,8},{10,9},{11,1... | collective-permute-start | bytes 196616 | tf_op jit(solution)/shard_map/ppermute | solution.py:328
  42.9 5.8 %collective-permute-start = (bf16[2,16,8,128]{3,2,1,0:T(8,128)(2,1)S(1)}, bf16[2,16,8,128]{3,2,1,0:T(8,128)(2,1)S(1)}, u32[]{:S(2)}, u32[]{:S(2)}) collective-permute-start(bf16[2,16,8,128]{3,2,1,0:T(8,128)(2,1)S(1)} %get-tuple-element.15), channel_id=1, source_target_pairs={{0,1},{1,2},{2,3},{3,4},{4,5},{5,6},{6,7},{7,8},{8,9},{9,10},{10,1... | collective-permute-start | bytes 196616 | tf_op jit(solution)/shard_map/ppermute | solution.py:323
  113.8 45.4 %copy-start.2 = (s32[16,80,128]{2,1,0:T(8,128)S(1)}, s32[16,80,128]{2,1,0:T(8,128)}, u32[]{:S(2)}) copy-start(s32[16,80,128]{2,1,0:T(8,128)} %ef.1) | copy-start | bytes 1966084
  113.8 45.4 %copy-start.3 = (s32[16,80,128]{2,1,0:T(8,128)S(1)}, s32[16,80,128]{2,1,0:T(8,128)}, u32[]{:S(2)}) copy-start(s32[16,80,128]{2,1,0:T(8,128)} %nf.1) | copy-start | bytes 1966084
  113.8 18.6 %collective-permute-start.2 = (bf16[16,96,128]{2,1,0:T(8,128)(2,1)}, bf16[16,96,128]{2,1,0:T(8,128)(2,1)}, u32[]{:S(2)}, u32[]{:S(2)}) collective-permute-start(bf16[16,96,128]{2,1,0:T(8,128)(2,1)} %shard_map.93), channel_id=1, source_target_pairs={{8,24},{9,25},{10,26},{11,27},{12,28},{13,29},{14,30},{15,31},{16,... | collective-permute-start | bytes 1179656 | tf_op jit(solution)/shard_map/ppermute | solution.py:368
  132.4 26.8 %all-to-all-start.3 = ((bf16[16,96,128]{2,1,0:T(8,128)(2,1)}), bf16[16,96,128]{2,1,0:T(8,128)(2,1)S(1)}, u32[]{:S(2)}, u32[]{:S(2)}) async-start(bf16[16,96,128]{2,1,0:T(8,128)(2,1)} %collective-permute-done.2), calls=%async_computation.3 | async-start | bytes 786432 | tf_op jit(solution)/shard_map/all_to_all | solution.py:370
  137.7 21.5 %collective-permute-start.3 = (bf16[2,7,96,128]{3,2,1,0:T(8,128)(2,1)}, bf16[2,7,96,128]{3,2,1,0:T(8,128)(2,1)}, u32[]{:S(2)}, u32[]{:S(2)}) collective-permute-start(bf16[2,7,96,128]{3,2,1,0:T(8,128)(2,1)} %slice.14), channel_id=1, source_target_pairs={{0,16},{16,32},{32,48},{48,64},{64,80},{80,96},{96,112},{112,128},... | collective-permute-start | bytes 1032200 | tf_op jit(solution)/shard_map/ppermute | solution.py:323
  142.9 16.3 %collective-permute-start.4 = (bf16[2,6,96,128]{3,2,1,0:T(8,128)(2,1)}, bf16[2,6,96,128]{3,2,1,0:T(8,128)(2,1)}, u32[]{:S(2)}, u32[]{:S(2)}) collective-permute-start(bf16[2,6,96,128]{3,2,1,0:T(8,128)(2,1)} %slice.15), channel_id=1, source_target_pairs={{16,0},{32,16},{48,32},{64,48},{80,64},{96,80},{112,96},{128,112},... | collective-permute-start | bytes 884744 | tf_op jit(solution)/shard_map/ppermute | solution.py:328

commit v5 on v4

--- a/solution.py
+++ b/solution.py
@@ -44,7 +44,7 @@
 
 
 def packing_kernel(
-    wavenumber, first, control, vert, legendre, out, cbuf, vbuf, scratch, whole, share, isem, osem
+    wavenumber, first, control, vert, legendre, out, cbuf, vbuf, lbuf, scratch, whole, share, isem, osem
 ):
     loads = []
     for i in range(CHUNKS):
@@ -52,32 +52,24 @@
         mats = pl.ds(i * CHUNK, CHUNK)
         loads.append(
             (
+                pltpu.make_async_copy(legendre.at[mats], lbuf.at[mats], isem.at[2, i]),
                 pltpu.make_async_copy(control.at[rows], cbuf.at[rows], isem.at[0, i]),
                 pltpu.make_async_copy(vert.at[mats], vbuf.at[mats], isem.at[1, i]),
             )
         )
-    for pair in loads:
-        for load in pair:
+    for several in loads:
+        for load in several[1:]:
             load.start()
+    for several in loads:
+        several[0].start()
     sends = []
-    for w in range(WAVE):
-        for slot in range(3):
-            order, start, size = owned(w, slot)
-            sends.append(
-                pltpu.make_async_copy(
-                    legendre.at[order, pl.ds(start, size)],
-                    out.at[w, pl.ds(PART_ROWS + START_OF[slot], size)],
-                    osem.at[0, w, slot],
-                )
-            )
-            sends[-1].start()
     row_id = lax.broadcasted_iota(jnp.int32, (2 * LEV, 2 * LEV), 0)
     column = lax.broadcasted_iota(jnp.int32, (2 * LEV, 2 * LEV), 1)
     chosen = column == (row_id & 1) * LEV + (row_id >> 1)
     pick = jnp.where(chosen, 1.0, 0.0).astype(jnp.bfloat16)
     orders = first[0] + lax.broadcasted_iota(jnp.int32, (ORDERS, 2 * LEV), 0)
     for i in range(CHUNKS):
-        for load in loads[i]:
+        for load in loads[i][1:]:
             load.wait()
         parts = jnp.dot(
             cbuf[i * CHUNK * ORDERS : (i + 1) * CHUNK * ORDERS],
@@ -93,6 +85,19 @@
             )
             for p in range(2):
                 scratch[p, pl.ds(r, ORDERS, stride=ROWS), :] = mixed[p * ORDERS : (p + 1) * ORDERS]
+    for several in loads:
+        several[0].wait()
+    for w in range(WAVE):
+        for slot in range(3):
+            order, start, size = owned(w, slot)
+            sends.append(
+                pltpu.make_async_copy(
+                    lbuf.at[order, pl.ds(start, size)],
+                    out.at[w, pl.ds(PART_ROWS + START_OF[slot], size)],
+                    osem.at[0, w, slot],
+                )
+            )
+            sends[-1].start()
     for w in range(WAVE):
         for slot in range(3):
             order, start, size = owned(w, slot)
@@ -129,10 +134,11 @@
         scratch_shapes=[
             pltpu.VMEM((ROWS * ORDERS, 2 * LEV), jnp.bfloat16),
             pltpu.VMEM((ROWS, LEV, LEV), jnp.bfloat16),
+            pltpu.VMEM((ORDERS, ROWS, LATS), jnp.bfloat16),
             pltpu.VMEM((2, ORDERS * ROWS, LEV), jnp.float32),
             pltpu.VMEM((WAVE, 2, ROWS, 2 * LEV), jnp.bfloat16),
             pltpu.VMEM((WAVE, SHARE, 2 * LEV), jnp.bfloat16),
-            pltpu.SemaphoreType.DMA((2, CHUNKS)),
+            pltpu.SemaphoreType.DMA((3, CHUNKS)),
             pltpu.SemaphoreType.DMA((2, WAVE, 3)),
         ],
     )(
@@ -196,20 +202,29 @@
     )
 
 
-def fourier_kernel(modes, local, out, wide, rhs):
-    wide[...] = modes[...].astype(jnp.float32)
+def fourier_kernel(modes, tables, out, held, local, wide, rhs, bands, isem, osem):
+    load_modes = pltpu.make_async_copy(modes, held, isem.at[0])
+    load_tables = pltpu.make_async_copy(tables, local, isem.at[1])
+    load_modes.start()
+    load_tables.start()
+    load_modes.wait()
+    wide[...] = held[...].astype(jnp.float32)
     for p in range(2):
         for slot in range(3):
             rows = wide[pl.ds(2 * slot + p, LATS, stride=SLOTS), :]
             start = p * COLUMNS + slot * LATS
             rhs[start : start + LATS] = rows.astype(jnp.bfloat16)
+    load_tables.wait()
+    sends = []
 
     def put(band, real, imaginary):
         basis = jnp.concatenate(
             [real.astype(jnp.bfloat16), imaginary.astype(jnp.bfloat16)], axis=1
         )
         total = jnp.dot(basis, rhs[...], preferred_element_type=jnp.float32)
-        out[band] = total.astype(jnp.bfloat16)
+        bands[band] = total.astype(jnp.bfloat16)
+        sends.append(pltpu.make_async_copy(bands.at[band], out.at[band], osem.at[band]))
+        sends[-1].start()
 
     for b in range(LAT // 2 + 1):
         far_cos = local[2 * EXT_X + b : 2 * EXT_X + b + 1, :]
@@ -220,15 +235,25 @@
         put(b, cc + ss, cs - sc)
         if 0 < b < LAT // 2:
             put(LAT - b, cc - ss, cs + sc)
+    for send in sends:
+        send.wait()
 
 
 def latitude_row(modes, tables):
+    far = pl.BlockSpec(memory_space=pltpu.HBM)
     return pl.pallas_call(
         fourier_kernel,
+        in_specs=[far, far],
+        out_specs=far,
         out_shape=jax.ShapeDtypeStruct((LAT, EXT_X, LEV), jnp.bfloat16),
         scratch_shapes=[
+            pltpu.VMEM((LATS * SLOTS, LEV), jnp.bfloat16),
+            pltpu.VMEM((2 * EXT_X + 2 * FAR, COLUMNS), jnp.float32),
             pltpu.VMEM((LATS * SLOTS, LEV), jnp.float32),
             pltpu.VMEM((2 * COLUMNS, LEV), jnp.bfloat16),
+            pltpu.VMEM((LAT, EXT_X, LEV), jnp.bfloat16),
+            pltpu.SemaphoreType.DMA((2,)),
+            pltpu.SemaphoreType.DMA((LAT,)),
         ],
     )(modes, tables)
 
@@ -352,11 +377,12 @@
     wide = jnp.concatenate([west, winds, east], axis=2)
     tables = angle_tables()
     packed = lax.all_to_all(packed, "wave", 0, 0, tiled=True)
-    packed, wide, tables = lax.optimization_barrier((packed, wide, tables))
+    upper, lower = wide[:, -SOUTH_ROWS:], wide[:, :NORTH_ROWS]
+    packed, upper, lower, tables = lax.optimization_barrier((packed, upper, lower, tables))
     modes = modes_of(packed)
-    modes, wide = lax.optimization_barrier((modes, wide))
-    wind_s = from_below(wide[:, -SOUTH_ROWS:], "wave", False)
-    wind_n = from_above(wide[:, :NORTH_ROWS], "wave", False)
+    modes, upper, lower = lax.optimization_barrier((modes, upper, lower))
+    wind_s = from_below(upper, "wave", False)
+    wind_n = from_above(lower, "wave", False)
     modes = lax.all_to_all(modes.reshape(LATS, SLOTS, LEV), ("wave", "lat"), 0, 0, tiled=True)
     row = latitude_row(modes.reshape(LATS * SLOTS, LEV), tables)
     pairs = []

time: 170 us -> 147 us (0.86)
  Pallas kernels: 41.7 us -> 19.2 us
  local copies, waits for them, and re-layouts: 3.49 us -> 0.04 us
  waiting for transfers between devices: 46.7 us -> 49.1 us
    pallas_call x1, Pallas kernels: 28.6 us -> 6.13 us  [packed_inputs(): pl.pallas_call(packing_kernel, in_specs=[smem, smem, far, far, far], out_...]
    slice x2 -> x0, local copies, waits for them, and re-layouts: 3.45 us -> none  [the longest x1 1.74 us: per_device(): wind_s = from_below(wide[:, -SOUTH_ROWS:], 'wave', False)]
    ppermute x2, waiting for transfers between devices: 11.5 us -> 14.5 us  [from_above(): return lax.ppermute(block, axis, pairs)]
  transfers between devices with their start and end apart: 7 -> 7, of which waited for: 3 -> 3; matrix products, arithmetic and copies ran while one was open for 5% -> 4% of each run, Pallas kernels for 0% -> 0%
where the time goes in v5:
time: 147 us; the launch traced here: 145 us
  waiting for transfers between devices  49.1 us (33%)
  blocking collectives  42.5 us (29%)
  starting transfers between devices  28.3 us (19%)
  Pallas kernels  19.2 us (13%)
  other arithmetic  5.48 us (4%)
    all_to_all x1, waiting for transfers between devices, per_device(): packed = lax.all_to_all(packed, 'wave', 0, 0, tiled=True)  31.3 us
    all_to_all x1, blocking collectives, per_device(): lax.all_to_all(modes.reshape(LATS, SLOTS, LEV), ('wave', 'lat'), 0, 0, ti...  27.8 us
    all_to_all x1, blocking collectives, per_device(): middle = lax.all_to_all(row, 'lat', 0, 0, tiled=True)  14.7 us
    ppermute x2, waiting for transfers between devices, from_above(): return lax.ppermute(block, axis, pairs)  14.5 us
    all_to_all x1, starting transfers between devices, per_device(): packed = lax.all_to_all(packed, 'wave', 0, 0, tiled=True)  10.9 us
    pallas_call x1, Pallas kernels, advected(): pl.pallas_call(advect_kernel, in_specs=[pl.BlockSpec(memory_space=pltpu.S...  8.64 us
    ppermute x2, starting transfers between devices, from_above(): return lax.ppermute(block, axis, pairs)  6.64 us
    pallas_call x1, Pallas kernels, packed_inputs(): pl.pallas_call(packing_kernel, in_specs=[smem, smem, far, far, far], out_...  6.13 us
  transfers between devices with their start and end apart: 7, of which 3 were waited for; matrix products, arithmetic and copies ran while one was open for 4% of the time, Pallas kernels for 0%

profile of v5, /device:TPU:64, one launch (start us, length us, event | category | flops | bytes accessed | tf_op | source)
XLA Modules:
  0.0 144.8 jit_solution(17668278695778644174)
XLA Ops:
  0.0 6.1 %shard_map.91 = bf16[16,208,256]{2,1,0:T(8,128)(2,1)} custom-call(s32[40]{0:T(128)} %wavenumber.1, s32[1]{0:T(128)} %bitcast.1.first, bf16[1600,256]{1,0:T(8,128)(2,1)} %bitcast.13, bf16[40,128,128]{2,1,0:T(8,128)(2,1)} %vert.1, bf16[40,40,256]{2,1,0:T(8,128)(2,1)} %legendre.1), custom_call_target="tpu_custom_call" | custom-call | tf_op jit(solution)/shard_map/pallas_call | solution.py:129
  6.2 10.9 %all-to-all-start = ((bf16[16,208,256]{2,1,0:T(8,128)(2,1)}), bf16[16,208,256]{2,1,0:T(8,128)(2,1)S(1)}, u32[]{:S(2)}, u32[]{:S(2)}) async-start(bf16[16,208,256]{2,1,0:T(8,128)(2,1)} %shard_map.91), calls=%async_computation | async-start | bytes 3407872 | tf_op jit(solution)/shard_map/all_to_all | solution.py:379
  17.1 0.0 copy-start.4
  17.1 0.0 copy-start.5
  17.1 0.0 copy-start.6
  17.1 1.5 %fusion.2 = (bf16[1,16,80,128]{3,2,1,0:T(8,128)(2,1)S(1)}, bf16[1,16,80,128]{3,2,1,0:T(8,128)(2,1)S(1)}) fusion(f32[16,80,128]{2,1,0:T(8,128)S(1)} %copy-done.1, s32[16,80,128]{2,1,0:T(8,128)} %nf.1, f32[16,80,128]{2,1,0:T(8,128)S(1)} %copy-done, s32[16,80,128]{2,1,0:T(8,128)} %ef.1), kind=kLoop, calls=%fused_computation.7 | loop fusion | flops 1310720 | bytes 3276800 | tf_op jit(solution)/shard_map/stack | solution.py:369
  18.6 1.8 %collective-permute-start.1 = (bf16[2,16,8,128]{3,2,1,0:T(8,128)(2,1)S(1)}, bf16[2,16,8,128]{3,2,1,0:T(8,128)(2,1)S(1)}, u32[]{:S(2)}, u32[]{:S(2)}) collective-permute-start(bf16[2,16,8,128]{3,2,1,0:T(8,128)(2,1)S(1)} %get-tuple-element.20), channel_id=1, source_target_pairs={{1,0},{2,1},{3,2},{4,3},{5,4},{6,5},{7,6},{8,7},{9,8},{10,9},{11,1... | collective-permute-start | bytes 196616 | tf_op jit(solution)/shard_map/ppermute | solution.py:353
  20.5 0.3 fusion.14
  20.8 1.3 cosine_multiply_fusion
  22.1 0.9 pad_maximum_fusion.tables
  23.0 3.3 %collective-permute-done.west = bf16[2,16,8,128]{3,2,1,0:T(8,128)(2,1)S(1)} collective-permute-done((bf16[2,16,8,128]{3,2,1,0:T(8,128)(2,1)S(1)}, bf16[2,16,8,128]{3,2,1,0:T(8,128)(2,1)S(1)}, u32[]{:S(2)}, u32[]{:S(2)}) %collective-permute-start) | collective-permute-done | bytes 65568 | tf_op jit(solution)/shard_map/ppermute | solution.py:348
  26.3 0.8 pad_maximum_fusion.2
  27.0 0.8 pad_maximum_fusion.1
  27.8 31.3 %all-to-all-done = bf16[16,208,256]{2,1,0:T(8,128)(2,1)S(1)} async-done(((bf16[16,208,256]{2,1,0:T(8,128)(2,1)}), bf16[16,208,256]{2,1,0:T(8,128)(2,1)S(1)}, u32[]{:S(2)}, u32[]{:S(2)}) %all-to-all-start) | async-done | bytes 1703968 | tf_op jit(solution)/shard_map/all_to_all | solution.py:379
  59.1 0.6 shard_map.92
  59.7 27.8 %all_to_all.20 = bf16[256,8,128]{2,1,0:T(8,128)(2,1)} all-to-all(bf16[256,8,128]{2,1,0:T(8,128)(2,1)S(1)} %bitcast.11), channel_id=1, replica_groups=mesh['wave'=16,'lat'=16] {'wave','lat'}, dimensions={0} | all-to-all | bytes 1048576 | tf_op jit(solution)/shard_map/all_to_all | solution.py:386
  87.4 3.8 %shard_map.93 = bf16[16,96,128]{2,1,0:T(8,128)(2,1)} custom-call(bf16[2048,128]{1,0:T(8,128)(2,1)} %bitcast.12, f32[224,768]{1,0:T(8,128)} %pad_maximum_fusion.tables), custom_call_target="tpu_custom_call" | custom-call | tf_op jit(solution)/shard_map/pallas_call | solution.py:244
  91.3 3.8 %collective-permute-start.2 = (bf16[16,96,128]{2,1,0:T(8,128)(2,1)}, bf16[16,96,128]{2,1,0:T(8,128)(2,1)}, u32[]{:S(2)}, u32[]{:S(2)}) collective-permute-start(bf16[16,96,128]{2,1,0:T(8,128)(2,1)} %shard_map.93), channel_id=1, source_target_pairs={{8,24},{9,25},{10,26},{11,27},{12,28},{13,29},{14,30},{15,31},{16,... | collective-permute-start | bytes 1179656 | tf_op jit(solution)/shard_map/ppermute | solution.py:394
  95.0 14.7 %all_to_all.21.middle = bf16[16,96,128]{2,1,0:T(8,128)(2,1)S(1)} all-to-all(bf16[16,96,128]{2,1,0:T(8,128)(2,1)} %shard_map.93), channel_id=1, replica_groups=mesh['wave'=16,'lat'=16] {'lat'}, dimensions={0} | all-to-all | bytes 786432 | tf_op jit(solution)/shard_map/all_to_all | solution.py:395
  109.7 3.6 %all-to-all-start.3 = ((bf16[16,96,128]{2,1,0:T(8,128)(2,1)}), bf16[16,96,128]{2,1,0:T(8,128)(2,1)S(1)}, u32[]{:S(2)}, u32[]{:S(2)}) async-start(bf16[16,96,128]{2,1,0:T(8,128)(2,1)} %collective-permute-done.2), calls=%async_computation.3 | async-start | bytes 786432 | tf_op jit(solution)/shard_map/all_to_all | solution.py:396
  113.3 3.4 %collective-permute-start.3 = (bf16[2,7,96,128]{3,2,1,0:T(8,128)(2,1)}, bf16[2,7,96,128]{3,2,1,0:T(8,128)(2,1)}, u32[]{:S(2)}, u32[]{:S(2)}) collective-permute-start(bf16[2,7,96,128]{3,2,1,0:T(8,128)(2,1)} %pad_maximum_fusion.1), channel_id=1, source_target_pairs={{0,16},{16,32},{32,48},{48,64},{64,80},{80,96},{96,112},{112,128},... | collective-permute-start | bytes 1032200 | tf_op jit(solution)/shard_map/ppermute | solution.py:348
  116.7 4.8 %collective-permute-start.4 = (bf16[2,6,96,128]{3,2,1,0:T(8,128)(2,1)}, bf16[2,6,96,128]{3,2,1,0:T(8,128)(2,1)}, u32[]{:S(2)}, u32[]{:S(2)}) collective-permute-start(bf16[2,6,96,128]{3,2,1,0:T(8,128)(2,1)} %pad_maximum_fusion.2), channel_id=1, source_target_pairs={{16,0},{32,16},{48,32},{64,48},{80,64},{96,80},{112,96},{128,112},... | collective-permute-start | bytes 884744 | tf_op jit(solution)/shard_map/ppermute | solution.py:353
  121.6 14.5 %collective-permute-done.4.wind_n = bf16[2,6,96,128]{3,2,1,0:T(8,128)(2,1)} collective-permute-done((bf16[2,6,96,128]{3,2,1,0:T(8,128)(2,1)}, bf16[2,6,96,128]{3,2,1,0:T(8,128)(2,1)}, u32[]{:S(2)}, u32[]{:S(2)}) %collective-permute-start.4) | collective-permute-done | bytes 294944 | tf_op jit(solution)/shard_map/ppermute | solution.py:353
  136.1 8.6 %shard_map.94 = f32[16,80,128]{2,1,0:T(8,128)} custom-call(s32[1]{0:T(128)} %bitcast.where, bf16[16,96,128]{2,1,0:T(8,128)(2,1)S(1)} %all_to_all.21.middle, bf16[16,96,128]{2,1,0:T(8,128)(2,1)S(1)} %all-to-all-done.3.halo, f32[16,80,128]{2,1,0:T(8,128)S(1)} %copy-done, f32[16,80,128]{2,1,0:T(8,128)S(1)} %copy-done.1, s32[16,80,128]{2,1,0:T(8,128)S(1)} %copy-done.2, ...), custom_call_target="tpu_custom_call" | custom-call | tf_op jit(solution)/shard_map/pallas_call | solution.py:331
  (19 shorter events, 0.1 us)
Async XLA Ops:
  6.1 10.9 %copy-start = (f32[16,80,128]{2,1,0:T(8,128)S(1)}, f32[16,80,128]{2,1,0:T(8,128)}, u32[]{:S(2)}) copy-start(f32[16,80,128]{2,1,0:T(8,128)} %ce.1) | copy-start | bytes 1966084
  6.2 10.9 %copy-start.1 = (f32[16,80,128]{2,1,0:T(8,128)S(1)}, f32[16,80,128]{2,1,0:T(8,128)}, u32[]{:S(2)}) copy-start(f32[16,80,128]{2,1,0:T(8,128)} %cn.1) | copy-start | bytes 1966084
  6.2 52.9 %all-to-all-start = ((bf16[16,208,256]{2,1,0:T(8,128)(2,1)}), bf16[16,208,256]{2,1,0:T(8,128)(2,1)S(1)}, u32[]{:S(2)}, u32[]{:S(2)}) async-start(bf16[16,208,256]{2,1,0:T(8,128)(2,1)} %shard_map.91), calls=%async_computation | async-start | bytes 3407872 | tf_op jit(solution)/shard_map/all_to_all | solution.py:379
  17.1 3.4 %copy-start.4 = (s32[768]{0:T(1024)S(1)}, s32[768]{0:T(1024)}, u32[]{:S(2)}) copy-start(s32[768]{0:T(1024)} %constant.47.clone) | copy-start | bytes 9220
  17.1 3.7 %copy-start.5 = (f32[768]{0:T(1024)S(1)}, f32[768]{0:T(1024)}, u32[]{:S(2)}) copy-start(f32[768]{0:T(1024)} %constant.54) | copy-start | bytes 9220
  17.1 3.7 %copy-start.6 = (f32[768]{0:T(1024)S(1)}, f32[768]{0:T(1024)}, u32[]{:S(2)}) copy-start(f32[768]{0:T(1024)} %constant.55) | copy-start | bytes 9220
  18.6 4.3 %collective-permute-start.1 = (bf16[2,16,8,128]{3,2,1,0:T(8,128)(2,1)S(1)}, bf16[2,16,8,128]{3,2,1,0:T(8,128)(2,1)S(1)}, u32[]{:S(2)}, u32[]{:S(2)}) collective-permute-start(bf16[2,16,8,128]{3,2,1,0:T(8,128)(2,1)S(1)} %get-tuple-element.20), channel_id=1, source_target_pairs={{1,0},{2,1},{3,2},{4,3},{5,4},{6,5},{7,6},{8,7},{9,8},{10,9},{11,1... | collective-permute-start | bytes 196616 | tf_op jit(solution)/shard_map/ppermute | solution.py:353
  20.5 5.8 %collective-permute-start = (bf16[2,16,8,128]{3,2,1,0:T(8,128)(2,1)S(1)}, bf16[2,16,8,128]{3,2,1,0:T(8,128)(2,1)S(1)}, u32[]{:S(2)}, u32[]{:S(2)}) collective-permute-start(bf16[2,16,8,128]{3,2,1,0:T(8,128)(2,1)S(1)} %get-tuple-element.19), channel_id=1, source_target_pairs={{0,1},{1,2},{2,3},{3,4},{4,5},{5,6},{6,7},{7,8},{8,9},{9,10},{10,1... | collective-permute-start | bytes 196616 | tf_op jit(solution)/shard_map/ppermute | solution.py:348
  87.4 48.7 %copy-start.2 = (s32[16,80,128]{2,1,0:T(8,128)S(1)}, s32[16,80,128]{2,1,0:T(8,128)}, u32[]{:S(2)}) copy-start(s32[16,80,128]{2,1,0:T(8,128)} %ef.1) | copy-start | bytes 1966084
  87.4 48.7 %copy-start.3 = (s32[16,80,128]{2,1,0:T(8,128)S(1)}, s32[16,80,128]{2,1,0:T(8,128)}, u32[]{:S(2)}) copy-start(s32[16,80,128]{2,1,0:T(8,128)} %nf.1) | copy-start | bytes 1966084
  91.3 18.5 %collective-permute-start.2 = (bf16[16,96,128]{2,1,0:T(8,128)(2,1)}, bf16[16,96,128]{2,1,0:T(8,128)(2,1)}, u32[]{:S(2)}, u32[]{:S(2)}) collective-permute-start(bf16[16,96,128]{2,1,0:T(8,128)(2,1)} %shard_map.93), channel_id=1, source_target_pairs={{8,24},{9,25},{10,26},{11,27},{12,28},{13,29},{14,30},{15,31},{16,... | collective-permute-start | bytes 1179656 | tf_op jit(solution)/shard_map/ppermute | solution.py:394
  109.7 26.4 %all-to-all-start.3 = ((bf16[16,96,128]{2,1,0:T(8,128)(2,1)}), bf16[16,96,128]{2,1,0:T(8,128)(2,1)S(1)}, u32[]{:S(2)}, u32[]{:S(2)}) async-start(bf16[16,96,128]{2,1,0:T(8,128)(2,1)} %collective-permute-done.2), calls=%async_computation.3 | async-start | bytes 786432 | tf_op jit(solution)/shard_map/all_to_all | solution.py:396
  113.3 22.8 %collective-permute-start.3 = (bf16[2,7,96,128]{3,2,1,0:T(8,128)(2,1)}, bf16[2,7,96,128]{3,2,1,0:T(8,128)(2,1)}, u32[]{:S(2)}, u32[]{:S(2)}) collective-permute-start(bf16[2,7,96,128]{3,2,1,0:T(8,128)(2,1)} %pad_maximum_fusion.1), channel_id=1, source_target_pairs={{0,16},{16,32},{32,48},{48,64},{64,80},{80,96},{96,112},{112,128},... | collective-permute-start | bytes 1032200 | tf_op jit(solution)/shard_map/ppermute | solution.py:348
  116.7 19.4 %collective-permute-start.4 = (bf16[2,6,96,128]{3,2,1,0:T(8,128)(2,1)}, bf16[2,6,96,128]{3,2,1,0:T(8,128)(2,1)}, u32[]{:S(2)}, u32[]{:S(2)}) collective-permute-start(bf16[2,6,96,128]{3,2,1,0:T(8,128)(2,1)} %pad_maximum_fusion.2), channel_id=1, source_target_pairs={{16,0},{32,16},{48,32},{64,48},{80,64},{96,80},{112,96},{128,112},... | collective-permute-start | bytes 884744 | tf_op jit(solution)/shard_map/ppermute | solution.py:353

commit v6 on v5

--- a/solution.py
+++ b/solution.py
@@ -31,7 +31,7 @@
 PART_ROWS = 2 * ROWS + SHARE
 CHUNK = 8
 CHUNKS = ROWS // CHUNK
-FAR = 16
+FAR = 8
 COLUMNS = 3 * LATS
 SOUTH_ROWS = HALO - 1
 NORTH_ROWS = HALO - 2
@@ -85,19 +85,18 @@
             )
             for p in range(2):
                 scratch[p, pl.ds(r, ORDERS, stride=ROWS), :] = mixed[p * ORDERS : (p + 1) * ORDERS]
-    for several in loads:
-        several[0].wait()
-    for w in range(WAVE):
-        for slot in range(3):
-            order, start, size = owned(w, slot)
-            sends.append(
-                pltpu.make_async_copy(
-                    lbuf.at[order, pl.ds(start, size)],
-                    out.at[w, pl.ds(PART_ROWS + START_OF[slot], size)],
-                    osem.at[0, w, slot],
-                )
-            )
-            sends[-1].start()
+        loads[i][0].wait()
+        for w in range(WAVE):
+            for slot in range(3):
+                order, start, size = owned(w, slot)
+                if order // CHUNK == i:
+                    send = pltpu.make_async_copy(
+                        lbuf.at[order, pl.ds(start, size)],
+                        out.at[w, pl.ds(PART_ROWS + START_OF[slot], size)],
+                        osem.at[0, w, slot],
+                    )
+                    send.start()
+                    sends.append(send)
     for w in range(WAVE):
         for slot in range(3):
             order, start, size = owned(w, slot)
@@ -209,11 +208,14 @@
     load_tables.start()
     load_modes.wait()
     wide[...] = held[...].astype(jnp.float32)
-    for p in range(2):
-        for slot in range(3):
+    group = lax.broadcasted_iota(jnp.int32, (LATS, LEV), 0) // (2 * LAT)
+    for slot in range(3):
+        even = (group + ORDER_OF[0][slot]) % 2 == 0
+        for p in range(2):
             rows = wide[pl.ds(2 * slot + p, LATS, stride=SLOTS), :]
             start = p * COLUMNS + slot * LATS
-            rhs[start : start + LATS] = rows.astype(jnp.bfloat16)
+            rhs[start : start + LATS, :LEV] = rows.astype(jnp.bfloat16)
+            rhs[start : start + LATS, LEV:] = jnp.where(even, rows, -rows).astype(jnp.bfloat16)
     load_tables.wait()
     sends = []
 
@@ -221,19 +223,21 @@
         basis = jnp.concatenate(
             [real.astype(jnp.bfloat16), imaginary.astype(jnp.bfloat16)], axis=1
         )
-        total = jnp.dot(basis, rhs[...], preferred_element_type=jnp.float32)
-        bands[band] = total.astype(jnp.bfloat16)
-        sends.append(pltpu.make_async_copy(bands.at[band], out.at[band], osem.at[band]))
-        sends[-1].start()
-
-    for b in range(LAT // 2 + 1):
+        total = jnp.dot(basis, rhs[...], preferred_element_type=jnp.float32).astype(jnp.bfloat16)
+        for half in range(2):
+            place = (band + half * (LAT // 2)) % LAT
+            bands[place] = total[:, half * LEV : (half + 1) * LEV]
+            sends.append(pltpu.make_async_copy(bands.at[place], out.at[place], osem.at[place]))
+            sends[-1].start()
+
+    for b in range(LAT // 4 + 1):
         far_cos = local[2 * EXT_X + b : 2 * EXT_X + b + 1, :]
         far_sin = local[2 * EXT_X + FAR + b : 2 * EXT_X + FAR + b + 1, :]
         near_cos, near_sin = local[0:EXT_X], local[EXT_X : 2 * EXT_X]
         cc, ss = far_cos * near_cos, far_sin * near_sin
         cs, sc = far_cos * near_sin, far_sin * near_cos
         put(b, cc + ss, cs - sc)
-        if 0 < b < LAT // 2:
+        if 0 < b < LAT // 4:
             put(LAT - b, cc - ss, cs + sc)
     for send in sends:
         send.wait()
@@ -250,7 +254,7 @@
             pltpu.VMEM((LATS * SLOTS, LEV), jnp.bfloat16),
             pltpu.VMEM((2 * EXT_X + 2 * FAR, COLUMNS), jnp.float32),
             pltpu.VMEM((LATS * SLOTS, LEV), jnp.float32),
-            pltpu.VMEM((2 * COLUMNS, LEV), jnp.bfloat16),
+            pltpu.VMEM((2 * COLUMNS, 2 * LEV), jnp.bfloat16),
             pltpu.VMEM((LAT, EXT_X, LEV), jnp.bfloat16),
             pltpu.SemaphoreType.DMA((2,)),
             pltpu.SemaphoreType.DMA((LAT,)),
@@ -272,12 +276,12 @@
 
 
 def advect_kernel(
-    where, middle, halo, ce, cn, ef, nf, west, east, wind_s, wind_n, out, qa, qb, us, gs
+    where, tiles, ce, cn, ef, nf, west, east, wind_s, wind_n, out, qa, qb, us, gs
 ):
     band = where[0]
-    qa[0:HALO] = halo[HALO:].astype(jnp.float32)
-    qa[HALO : HALO + TILE_R] = middle[...].astype(jnp.float32)
-    qa[HALO + TILE_R :] = halo[:HALO].astype(jnp.float32)
+    qa[0:HALO] = tiles[HALO:, 1].astype(jnp.float32)
+    qa[HALO : HALO + TILE_R] = tiles[:, 0].astype(jnp.float32)
+    qa[HALO + TILE_R :] = tiles[:HALO, 1].astype(jnp.float32)
     qb[0:HALO] = jnp.zeros((HALO, EXT_X, LEV), jnp.float32)
     qb[HALO + TILE_R :] = jnp.zeros((HALO, EXT_X, LEV), jnp.float32)
     inner = slice(HALO, HALO + TILE_R)
@@ -327,11 +331,11 @@
         lax.fori_loop(low, high, row, (first, face(low - 1, slope(low - 1), first)))
 
 
-def advected(band, middle, halo, winds, halos):
+def advected(band, tiles, winds, halos):
     return pl.pallas_call(
         advect_kernel,
         in_specs=[pl.BlockSpec(memory_space=pltpu.SMEM)]
-        + [pl.BlockSpec(memory_space=pltpu.VMEM)] * 10,
+        + [pl.BlockSpec(memory_space=pltpu.VMEM)] * 9,
         out_shape=jax.ShapeDtypeStruct((TILE_R, TILE_X, LEV), jnp.float32),
         scratch_shapes=[
             pltpu.VMEM((EXT_R, EXT_X, LEV), jnp.float32),
@@ -340,7 +344,7 @@
             pltpu.VMEM((2, EXT_R, EXT_X, LEV), jnp.float32),
         ],
         compiler_params=PARAMS,
-    )(band[None], middle, halo, *winds, *halos)
+    )(band[None], tiles, *winds, *halos)
 
 
 def from_below(block, axis, wrap):
@@ -392,12 +396,11 @@
             if 0 <= to < WAVE:
                 pairs.append((w * LAT + l, to * LAT + l))
     next_row = lax.ppermute(row, ("wave", "lat"), pairs)
-    middle = lax.all_to_all(row, "lat", 0, 0, tiled=True)
-    halo = lax.all_to_all(next_row, "lat", 0, 0, tiled=True)
+    rows = jnp.stack([row, next_row], axis=1)
+    tiles = lax.all_to_all(rows, "lat", 0, 0, tiled=True)
     return advected(
         wave,
-        middle,
-        halo,
+        tiles,
         (courant_east, courant_north, east_flags, north_flags),
         (west, east, wind_s, wind_n),
     )

time: 147 us -> 149 us (1.014)
  waiting for transfers between devices: 49.1 us -> 64.2 us
  blocking collectives: 42.5 us -> 27.8 us
  other arithmetic: 5.48 us -> 7.34 us
    all_to_all x1 -> x0, blocking collectives: 14.7 us -> none  [per_device(): middle = lax.all_to_all(row, 'lat', 0, 0, tiled=True)]
    ppermute x1, waiting for transfers between devices: 0.01 us -> 10.8 us  [per_device(): next_row = lax.ppermute(row, ('wave', 'lat'), pairs)]
    ppermute x2, waiting for transfers between devices: 14.5 us -> 18.7 us  [from_above(): return lax.ppermute(block, axis, pairs)]
    another operation x0 -> x1, other arithmetic: none -> 1.95 us  [per_device(): rows = jnp.stack([row, next_row], axis=1)]
  transfers between devices with their start and end apart: 7 -> 7, of which waited for: 3 -> 4; matrix products, arithmetic and copies ran while one was open for 4% -> 4% of each run, Pallas kernels for 0% -> 0%
where the time goes in v6:
time: 149 us; the launch traced here: 147 us
  waiting for transfers between devices  64.2 us (43%)
  starting transfers between devices  28.5 us (19%)
  blocking collectives  27.8 us (19%)
  Pallas kernels  18.7 us (13%)
  other arithmetic  7.34 us (5%)
    all_to_all x1, waiting for transfers between devices, per_device(): packed = lax.all_to_all(packed, 'wave', 0, 0, tiled=True)  31.3 us
    all_to_all x1, blocking collectives, per_device(): lax.all_to_all(modes.reshape(LATS, SLOTS, LEV), ('wave', 'lat'), 0, 0, ti...  27.8 us
    ppermute x2, waiting for transfers between devices, from_above(): return lax.ppermute(block, axis, pairs)  18.7 us
    all_to_all x1, starting transfers between devices, per_device(): packed = lax.all_to_all(packed, 'wave', 0, 0, tiled=True)  10.9 us
    ppermute x1, waiting for transfers between devices, per_device(): next_row = lax.ppermute(row, ('wave', 'lat'), pairs)  10.8 us
    pallas_call x1, Pallas kernels, advected(): pl.pallas_call(advect_kernel, in_specs=[pl.BlockSpec(memory_space=pltpu.S...  8.64 us
    pallas_call x1, Pallas kernels, packed_inputs(): pl.pallas_call(packing_kernel, in_specs=[smem, smem, far, far, far], out_...  6.1 us
    ppermute x2, starting transfers between devices, from_above(): return lax.ppermute(block, axis, pairs)  5.98 us
  transfers between devices with their start and end apart: 7, of which 4 were waited for; matrix products, arithmetic and copies ran while one was open for 4% of the time, Pallas kernels for 0%

profile of v6, /device:TPU:64, one launch (start us, length us, event | category | flops | bytes accessed | tf_op | source)
XLA Modules:
  0.0 146.7 jit_solution(13799671489718228746)
XLA Ops:
  0.0 6.1 %shard_map.91 = bf16[16,208,256]{2,1,0:T(8,128)(2,1)} custom-call(s32[40]{0:T(128)} %wavenumber.1, s32[1]{0:T(128)} %bitcast.1.first, bf16[1600,256]{1,0:T(8,128)(2,1)} %bitcast.16, bf16[40,128,128]{2,1,0:T(8,128)(2,1)} %vert.1, bf16[40,40,256]{2,1,0:T(8,128)(2,1)} %legendre.1), custom_call_target="tpu_custom_call" | custom-call | tf_op jit(solution)/shard_map/pallas_call | solution.py:128
  6.1 10.9 %all-to-all-start = ((bf16[16,208,256]{2,1,0:T(8,128)(2,1)}), bf16[16,208,256]{2,1,0:T(8,128)(2,1)S(1)}, u32[]{:S(2)}, u32[]{:S(2)}) async-start(bf16[16,208,256]{2,1,0:T(8,128)(2,1)} %shard_map.91), calls=%async_computation | async-start | bytes 3407872 | tf_op jit(solution)/shard_map/all_to_all | solution.py:383
  17.1 0.0 copy-start.4
  17.1 0.0 copy-start.5
  17.1 1.5 %fusion.2 = (bf16[1,16,80,128]{3,2,1,0:T(8,128)(2,1)S(1)}, bf16[1,16,80,128]{3,2,1,0:T(8,128)(2,1)S(1)}) fusion(f32[16,80,128]{2,1,0:T(8,128)S(1)} %copy-done.1, s32[16,80,128]{2,1,0:T(8,128)} %nf.1, f32[16,80,128]{2,1,0:T(8,128)S(1)} %copy-done, s32[16,80,128]{2,1,0:T(8,128)} %ef.1), kind=kLoop, calls=%fused_computation.8 | loop fusion | flops 1310720 | bytes 3276800 | tf_op jit(solution)/shard_map/stack | solution.py:373
  18.6 1.8 %collective-permute-start.1 = (bf16[2,16,8,128]{3,2,1,0:T(8,128)(2,1)S(1)}, bf16[2,16,8,128]{3,2,1,0:T(8,128)(2,1)S(1)}, u32[]{:S(2)}, u32[]{:S(2)}) collective-permute-start(bf16[2,16,8,128]{3,2,1,0:T(8,128)(2,1)S(1)} %get-tuple-element.20), channel_id=1, source_target_pairs={{1,0},{2,1},{3,2},{4,3},{5,4},{6,5},{7,6},{8,7},{9,8},{10,9},{11,1... | collective-permute-start | bytes 196616 | tf_op jit(solution)/shard_map/ppermute | solution.py:357
  20.5 0.2 fusion.14
  20.7 1.3 cosine_multiply_fusion
  21.9 0.9 pad_maximum_fusion.1.tables
  22.8 3.4 %collective-permute-done.west = bf16[2,16,8,128]{3,2,1,0:T(8,128)(2,1)S(1)} collective-permute-done((bf16[2,16,8,128]{3,2,1,0:T(8,128)(2,1)S(1)}, bf16[2,16,8,128]{3,2,1,0:T(8,128)(2,1)S(1)}, u32[]{:S(2)}, u32[]{:S(2)}) %collective-permute-start) | collective-permute-done | bytes 65568 | tf_op jit(solution)/shard_map/ppermute | solution.py:352
  26.2 0.7 pad_maximum_fusion.3
  27.0 0.8 pad_maximum_fusion.2
  27.8 31.3 %all-to-all-done = bf16[16,208,256]{2,1,0:T(8,128)(2,1)S(1)} async-done(((bf16[16,208,256]{2,1,0:T(8,128)(2,1)}), bf16[16,208,256]{2,1,0:T(8,128)(2,1)S(1)}, u32[]{:S(2)}, u32[]{:S(2)}) %all-to-all-start) | async-done | bytes 1703968 | tf_op jit(solution)/shard_map/all_to_all | solution.py:383
  59.0 0.6 shard_map.92
  59.7 27.8 %all_to_all.15 = bf16[256,8,128]{2,1,0:T(8,128)(2,1)} all-to-all(bf16[256,8,128]{2,1,0:T(8,128)(2,1)S(1)} %bitcast.13), channel_id=1, replica_groups=mesh['wave'=16,'lat'=16] {'wave','lat'}, dimensions={0} | all-to-all | bytes 1048576 | tf_op jit(solution)/shard_map/all_to_all | solution.py:390
  87.4 3.4 %shard_map.93 = bf16[16,96,128]{2,1,0:T(8,128)(2,1)} custom-call(bf16[2048,128]{1,0:T(8,128)(2,1)} %bitcast.14, f32[208,768]{1,0:T(8,128)} %pad_maximum_fusion.1.tables), custom_call_target="tpu_custom_call" | custom-call | tf_op jit(solution)/shard_map/pallas_call | solution.py:248
  90.8 3.9 %collective-permute-start.2 = (bf16[16,96,128]{2,1,0:T(8,128)(2,1)}, bf16[16,96,128]{2,1,0:T(8,128)(2,1)S(1)}, u32[]{:S(2)}, u32[]{:S(2)}) collective-permute-start(bf16[16,96,128]{2,1,0:T(8,128)(2,1)} %shard_map.93), channel_id=1, source_target_pairs={{8,24},{9,25},{10,26},{11,27},{12,28},{13,29},{14,30},{15,31},{16,... | collective-permute-start | bytes 1179656 | tf_op jit(solution)/shard_map/ppermute | solution.py:398
  94.7 10.8 %collective-permute-done.2 = bf16[16,96,128]{2,1,0:T(8,128)(2,1)S(1)} collective-permute-done((bf16[16,96,128]{2,1,0:T(8,128)(2,1)}, bf16[16,96,128]{2,1,0:T(8,128)(2,1)S(1)}, u32[]{:S(2)}, u32[]{:S(2)}) %collective-permute-start.2) | collective-permute-done | bytes 393248 | tf_op jit(solution)/shard_map/ppermute | solution.py:398
  105.5 2.0 %pad_maximum_fusion = bf16[16,2,96,128]{3,2,1,0:T(8,128)(2,1)} fusion(bf16[16,1,96,128]{3,2,1,0:T(8,128)(2,1)S(1)} %bitcast.17, bf16[16,1,96,128]{3,2,1,0:T(8,128)(2,1)} %bitcast.15), kind=kLoop, calls=%fused_computation.2 | loop fusion | flops 393216 | bytes 1572864 | tf_op jit(solution)/shard_map/stack | solution.py:399
  107.5 3.6 %all-to-all-start.2 = ((bf16[16,2,96,128]{3,2,1,0:T(8,128)(2,1)}), bf16[16,2,96,128]{3,2,1,0:T(8,128)(2,1)S(1)}, u32[]{:S(2)}, u32[]{:S(2)}) async-start(bf16[16,2,96,128]{3,2,1,0:T(8,128)(2,1)} %pad_maximum_fusion), calls=%async_computation.2 | async-start | bytes 1572864 | tf_op jit(solution)/shard_map/all_to_all | solution.py:400
  111.1 4.1 %collective-permute-start.3 = (bf16[2,7,96,128]{3,2,1,0:T(8,128)(2,1)}, bf16[2,7,96,128]{3,2,1,0:T(8,128)(2,1)}, u32[]{:S(2)}, u32[]{:S(2)}) collective-permute-start(bf16[2,7,96,128]{3,2,1,0:T(8,128)(2,1)} %pad_maximum_fusion.2), channel_id=1, source_target_pairs={{0,16},{16,32},{32,48},{48,64},{64,80},{80,96},{96,112},{112,128},... | collective-permute-start | bytes 1032200 | tf_op jit(solution)/shard_map/ppermute | solution.py:352
  115.2 4.2 %collective-permute-start.4 = (bf16[2,6,96,128]{3,2,1,0:T(8,128)(2,1)}, bf16[2,6,96,128]{3,2,1,0:T(8,128)(2,1)}, u32[]{:S(2)}, u32[]{:S(2)}) collective-permute-start(bf16[2,6,96,128]{3,2,1,0:T(8,128)(2,1)} %pad_maximum_fusion.3), channel_id=1, source_target_pairs={{16,0},{32,16},{48,32},{64,48},{80,64},{96,80},{112,96},{128,112},... | collective-permute-start | bytes 884744 | tf_op jit(solution)/shard_map/ppermute | solution.py:357
  119.4 18.7 %collective-permute-done.4.wind_n = bf16[2,6,96,128]{3,2,1,0:T(8,128)(2,1)} collective-permute-done((bf16[2,6,96,128]{3,2,1,0:T(8,128)(2,1)}, bf16[2,6,96,128]{3,2,1,0:T(8,128)(2,1)}, u32[]{:S(2)}, u32[]{:S(2)}) %collective-permute-start.4) | collective-permute-done | bytes 294944 | tf_op jit(solution)/shard_map/ppermute | solution.py:357
  138.1 8.6 %shard_map.94 = f32[16,80,128]{2,1,0:T(8,128)} custom-call(s32[1]{0:T(128)} %bitcast.where, bf16[16,2,96,128]{3,2,1,0:T(8,128)(2,1)S(1)} %all-to-all-done.2.tiles, f32[16,80,128]{2,1,0:T(8,128)S(1)} %copy-done, f32[16,80,128]{2,1,0:T(8,128)S(1)} %copy-done.1, s32[16,80,128]{2,1,0:T(8,128)S(1)} %copy-done.2, s32[16,80,128]{2,1,0:T(8,128)S(1)} %copy-done.3, ...), custom_call_target="tpu_custom_call" | custom-call | tf_op jit(solution)/shard_map/pallas_call | solution.py:335
  (19 shorter events, 0.1 us)
Async XLA Ops:
  6.1 10.9 %copy-start = (f32[16,80,128]{2,1,0:T(8,128)S(1)}, f32[16,80,128]{2,1,0:T(8,128)}, u32[]{:S(2)}) copy-start(f32[16,80,128]{2,1,0:T(8,128)} %ce.1) | copy-start | bytes 1966084
  6.1 10.9 %copy-start.1 = (f32[16,80,128]{2,1,0:T(8,128)S(1)}, f32[16,80,128]{2,1,0:T(8,128)}, u32[]{:S(2)}) copy-start(f32[16,80,128]{2,1,0:T(8,128)} %cn.1) | copy-start | bytes 1966084
  6.1 52.9 %all-to-all-start = ((bf16[16,208,256]{2,1,0:T(8,128)(2,1)}), bf16[16,208,256]{2,1,0:T(8,128)(2,1)S(1)}, u32[]{:S(2)}, u32[]{:S(2)}) async-start(bf16[16,208,256]{2,1,0:T(8,128)(2,1)} %shard_map.91), calls=%async_computation | async-start | bytes 3407872 | tf_op jit(solution)/shard_map/all_to_all | solution.py:383
  17.1 3.4 %copy-start.4 = (s32[768]{0:T(1024)S(1)}, s32[768]{0:T(1024)}, u32[]{:S(2)}) copy-start(s32[768]{0:T(1024)} %constant.47.clone) | copy-start | bytes 9220
  17.1 3.6 %copy-start.5 = (f32[768]{0:T(1024)S(1)}, f32[768]{0:T(1024)}, u32[]{:S(2)}) copy-start(f32[768]{0:T(1024)} %constant.54) | copy-start | bytes 9220
  17.1 3.6 %copy-start.6 = (f32[768]{0:T(1024)S(1)}, f32[768]{0:T(1024)}, u32[]{:S(2)}) copy-start(f32[768]{0:T(1024)} %constant.55) | copy-start | bytes 9220
  18.6 4.2 %collective-permute-start.1 = (bf16[2,16,8,128]{3,2,1,0:T(8,128)(2,1)S(1)}, bf16[2,16,8,128]{3,2,1,0:T(8,128)(2,1)S(1)}, u32[]{:S(2)}, u32[]{:S(2)}) collective-permute-start(bf16[2,16,8,128]{3,2,1,0:T(8,128)(2,1)S(1)} %get-tuple-element.20), channel_id=1, source_target_pairs={{1,0},{2,1},{3,2},{4,3},{5,4},{6,5},{7,6},{8,7},{9,8},{10,9},{11,1... | collective-permute-start | bytes 196616 | tf_op jit(solution)/shard_map/ppermute | solution.py:357
  20.4 5.8 %collective-permute-start = (bf16[2,16,8,128]{3,2,1,0:T(8,128)(2,1)S(1)}, bf16[2,16,8,128]{3,2,1,0:T(8,128)(2,1)S(1)}, u32[]{:S(2)}, u32[]{:S(2)}) collective-permute-start(bf16[2,16,8,128]{3,2,1,0:T(8,128)(2,1)S(1)} %get-tuple-element.19), channel_id=1, source_target_pairs={{0,1},{1,2},{2,3},{3,4},{4,5},{5,6},{6,7},{7,8},{8,9},{9,10},{10,1... | collective-permute-start | bytes 196616 | tf_op jit(solution)/shard_map/ppermute | solution.py:352
  90.8 47.3 %copy-start.2 = (s32[16,80,128]{2,1,0:T(8,128)S(1)}, s32[16,80,128]{2,1,0:T(8,128)}, u32[]{:S(2)}) copy-start(s32[16,80,128]{2,1,0:T(8,128)} %ef.1) | copy-start | bytes 1966084
  90.8 47.2 %copy-start.3 = (s32[16,80,128]{2,1,0:T(8,128)S(1)}, s32[16,80,128]{2,1,0:T(8,128)}, u32[]{:S(2)}) copy-start(s32[16,80,128]{2,1,0:T(8,128)} %nf.1) | copy-start | bytes 1966084
  90.8 14.7 %collective-permute-start.2 = (bf16[16,96,128]{2,1,0:T(8,128)(2,1)}, bf16[16,96,128]{2,1,0:T(8,128)(2,1)S(1)}, u32[]{:S(2)}, u32[]{:S(2)}) collective-permute-start(bf16[16,96,128]{2,1,0:T(8,128)(2,1)} %shard_map.93), channel_id=1, source_target_pairs={{8,24},{9,25},{10,26},{11,27},{12,28},{13,29},{14,30},{15,31},{16,... | collective-permute-start | bytes 1179656 | tf_op jit(solution)/shard_map/ppermute | solution.py:398
  107.5 30.6 %all-to-all-start.2 = ((bf16[16,2,96,128]{3,2,1,0:T(8,128)(2,1)}), bf16[16,2,96,128]{3,2,1,0:T(8,128)(2,1)S(1)}, u32[]{:S(2)}, u32[]{:S(2)}) async-start(bf16[16,2,96,128]{3,2,1,0:T(8,128)(2,1)} %pad_maximum_fusion), calls=%async_computation.2 | async-start | bytes 1572864 | tf_op jit(solution)/shard_map/all_to_all | solution.py:400
  111.1 26.9 %collective-permute-start.3 = (bf16[2,7,96,128]{3,2,1,0:T(8,128)(2,1)}, bf16[2,7,96,128]{3,2,1,0:T(8,128)(2,1)}, u32[]{:S(2)}, u32[]{:S(2)}) collective-permute-start(bf16[2,7,96,128]{3,2,1,0:T(8,128)(2,1)} %pad_maximum_fusion.2), channel_id=1, source_target_pairs={{0,16},{16,32},{32,48},{48,64},{64,80},{80,96},{96,112},{112,128},... | collective-permute-start | bytes 1032200 | tf_op jit(solution)/shard_map/ppermute | solution.py:352
  115.2 22.8 %collective-permute-start.4 = (bf16[2,6,96,128]{3,2,1,0:T(8,128)(2,1)}, bf16[2,6,96,128]{3,2,1,0:T(8,128)(2,1)}, u32[]{:S(2)}, u32[]{:S(2)}) collective-permute-start(bf16[2,6,96,128]{3,2,1,0:T(8,128)(2,1)} %pad_maximum_fusion.3), channel_id=1, source_target_pairs={{16,0},{32,16},{48,32},{64,48},{80,64},{96,80},{112,96},{128,112},... | collective-permute-start | bytes 884744 | tf_op jit(solution)/shard_map/ppermute | solution.py:357

commit v7 on v6

--- a/solution.py
+++ b/solution.py
@@ -1,3 +1,4 @@
+import functools
 import math
 
 import jax
@@ -33,8 +34,8 @@
 CHUNKS = ROWS // CHUNK
 FAR = 8
 COLUMNS = 3 * LATS
-SOUTH_ROWS = HALO - 1
-NORTH_ROWS = HALO - 2
+UNROLL = 2
+EDGE = HALO - 1
 PARAMS = pltpu.CompilerParams(vmem_limit_bytes=24 * 1024 * 1024)
 
 
@@ -276,18 +277,20 @@
 
 
 def advect_kernel(
-    where, tiles, ce, cn, ef, nf, west, east, wind_s, wind_n, out, qa, qb, us, gs
+    where, middle, halo, ce, cn, ef, nf, west, east, early, late, out, qa, qb, us, gs
 ):
     band = where[0]
-    qa[0:HALO] = tiles[HALO:, 1].astype(jnp.float32)
-    qa[HALO : HALO + TILE_R] = tiles[:, 0].astype(jnp.float32)
-    qa[HALO + TILE_R :] = tiles[:HALO, 1].astype(jnp.float32)
+    odd = band % 2 == 1
+    qa[0:HALO] = halo[HALO:].astype(jnp.float32)
+    qa[HALO : HALO + TILE_R] = middle[...].astype(jnp.float32)
+    qa[HALO + TILE_R :] = halo[:HALO].astype(jnp.float32)
     qb[0:HALO] = jnp.zeros((HALO, EXT_X, LEV), jnp.float32)
     qb[HALO + TILE_R :] = jnp.zeros((HALO, EXT_X, LEV), jnp.float32)
     inner = slice(HALO, HALO + TILE_R)
     for d, (size, flag) in enumerate(((ce, ef), (cn, nf))):
-        us[d, HALO - SOUTH_ROWS : HALO] = wind_s[d].astype(jnp.float32)
-        us[d, HALO + TILE_R : HALO + TILE_R + NORTH_ROWS] = wind_n[d].astype(jnp.float32)
+        first, second = early[d].astype(jnp.float32), late[d].astype(jnp.float32)
+        us[d, HALO - EDGE : HALO] = jnp.where(odd, first, second)
+        us[d, HALO + TILE_R : HALO + TILE_R + EDGE] = jnp.where(odd, second, first)
         us[d, inner, 0:HALO] = west[d].astype(jnp.float32)
         us[d, inner, HALO + TILE_X :] = east[d].astype(jnp.float32)
         us[d, inner, HALO : HALO + TILE_X] = jnp.where(flag[...] > 0, size[...], -size[...])
@@ -298,44 +301,51 @@
             gs[d, r] = 0.5 * speed * (1.0 - speed)
         return carry
 
-    lax.fori_loop(HALO - SOUTH_ROWS, HALO + TILE_R + NORTH_ROWS, gains, 0)
+    lax.fori_loop(HALO - EDGE, HALO + TILE_R + EDGE, gains, 0)
+    keep = jnp.where(band == WAVE - 1, 0.0, 1.0)
     for t in range(1, STEPS + 1):
         old, new = (qa, qb) if t % 2 else (qb, qa)
-        low = jnp.where(band == 0, HALO, 2 * t)
-        high = jnp.where(band == WAVE - 1, HALO + TILE_R, EXT_R - 2 * t)
-
-        def slope(r):
-            here = old[r]
-            return minmod(old[r + 1] - here, here - old[r - 1])
-
-        def face(r, low_slope, high_slope):
-            return flux(us[1, r], gs[1, r], old[r], old[r + 1], low_slope, high_slope)
-
-        def row(r, carry):
-            here_slope, below = carry
-            here = old[r]
-            next_slope = slope(r + 1)
-            above = face(r, here_slope, next_slope)
-            right = shifted(here, -1)
-            jump = right - here
-            steep = minmod(jump, shifted(jump, 1))
-            east_face = flux(us[0, r], gs[0, r], here, right, steep, shifted(steep, -1))
-            fresh = here - (east_face - shifted(east_face, 1)) - (above - below)
-            if t == STEPS:
-                out[r - HALO] = fresh[HALO : HALO + TILE_X]
-            else:
-                new[r] = fresh
-            return next_slope, above
-
-        first = slope(low)
-        lax.fori_loop(low, high, row, (first, face(low - 1, slope(low - 1), first)))
-
-
-def advected(band, tiles, winds, halos):
+
+        def rows(i, carry, start):
+            slope, below = carry
+            first = start + UNROLL * i
+            here, above = old[first], old[first + 1]
+            jump = above - here
+            for k in range(UNROLL):
+                r = first + k
+                beyond = old[r + 2]
+                next_jump = beyond - above
+                next_slope = minmod(next_jump, jump)
+                top = flux(us[1, r], gs[1, r], here, above, slope, next_slope)
+                right = shifted(here, -1)
+                step = right - here
+                steep = minmod(step, shifted(step, 1))
+                east_face = flux(us[0, r], gs[0, r], here, right, steep, shifted(steep, -1))
+                fresh = here - (east_face - shifted(east_face, 1)) - (top - below)
+                if t == STEPS:
+                    out[r - HALO] = fresh[HALO : HALO + TILE_X]
+                else:
+                    new[r] = fresh
+                here, above, jump, slope, below = above, beyond, next_jump, next_slope, top
+            return slope, below
+
+        low, top_row, high = 2 * t, HALO + TILE_R, EXT_R - 2 * t
+        far, down, here, up = (old[low + d] for d in (-2, -1, 0, 1))
+        slope = minmod(up - here, here - down)
+        face = flux(us[1, low - 1], gs[1, low - 1], down, here, minmod(here - down, down - far), slope)
+        carry = lax.fori_loop(
+            0, (top_row - low) // UNROLL, functools.partial(rows, start=low), (slope, face)
+        )
+        if high > top_row:
+            carry = (carry[0], carry[1] * keep)
+            lax.fori_loop(0, (high - top_row) // UNROLL, functools.partial(rows, start=top_row), carry)
+
+
+def advected(band, middle, halo, winds, halos):
     return pl.pallas_call(
         advect_kernel,
         in_specs=[pl.BlockSpec(memory_space=pltpu.SMEM)]
-        + [pl.BlockSpec(memory_space=pltpu.VMEM)] * 9,
+        + [pl.BlockSpec(memory_space=pltpu.VMEM)] * 10,
         out_shape=jax.ShapeDtypeStruct((TILE_R, TILE_X, LEV), jnp.float32),
         scratch_shapes=[
             pltpu.VMEM((EXT_R, EXT_X, LEV), jnp.float32),
@@ -344,7 +354,7 @@
             pltpu.VMEM((2, EXT_R, EXT_X, LEV), jnp.float32),
         ],
         compiler_params=PARAMS,
-    )(band[None], tiles, *winds, *halos)
+    )(band[None], middle, halo, *winds, *halos)
 
 
 def from_below(block, axis, wrap):
@@ -381,12 +391,15 @@
     wide = jnp.concatenate([west, winds, east], axis=2)
     tables = angle_tables()
     packed = lax.all_to_all(packed, "wave", 0, 0, tiled=True)
-    upper, lower = wide[:, -SOUTH_ROWS:], wide[:, :NORTH_ROWS]
-    packed, upper, lower, tables = lax.optimization_barrier((packed, upper, lower, tables))
+    odd = wave % 2 == 1
+    upper, lower = wide[:, -EDGE:], wide[:, :EDGE]
+    early = lax.ppermute(jnp.where(odd, lower, upper), "wave", [(w, w ^ 1) for w in range(WAVE)])
+    late = jnp.where(odd, upper, lower)
+    packed, early, late, tables = lax.optimization_barrier((packed, early, late, tables))
     modes = modes_of(packed)
-    modes, upper, lower = lax.optimization_barrier((modes, upper, lower))
-    wind_s = from_below(upper, "wave", False)
-    wind_n = from_above(lower, "wave", False)
+    modes, late = lax.optimization_barrier((modes, late))
+    ends = [(w, w + 1) for w in range(1, WAVE - 1, 2)]
+    late = lax.ppermute(late, "wave", ends + [(j, i) for i, j in ends])
     modes = lax.all_to_all(modes.reshape(LATS, SLOTS, LEV), ("wave", "lat"), 0, 0, tiled=True)
     row = latitude_row(modes.reshape(LATS * SLOTS, LEV), tables)
     pairs = []
@@ -396,13 +409,14 @@
             if 0 <= to < WAVE:
                 pairs.append((w * LAT + l, to * LAT + l))
     next_row = lax.ppermute(row, ("wave", "lat"), pairs)
-    rows = jnp.stack([row, next_row], axis=1)
-    tiles = lax.all_to_all(rows, "lat", 0, 0, tiled=True)
+    middle = lax.all_to_all(row, "lat", 0, 0, tiled=True)
+    halo = lax.all_to_all(next_row, "lat", 0, 0, tiled=True)
     return advected(
         wave,
-        tiles,
+        middle,
+        halo,
         (courant_east, courant_north, east_flags, north_flags),
-        (west, east, wind_s, wind_n),
+        (west, east, early, late),
     )
 
 

time: 149 us -> 142 us (0.953)
  waiting for transfers between devices: 64.2 us -> 40.9 us
  blocking collectives: 27.8 us -> 42.4 us
  local copies, waits for them, and re-layouts: 0.05 us -> 3.48 us
    ppermute x0 -> x2, waiting for transfers between devices: none -> 18.6 us  [the longest x1 11.5 us: per_device(): late = lax.ppermute(late, 'wave', ends + [(j, i) for i, j in ends])]
    ppermute x2 -> x1, waiting for transfers between devices: 18.7 us -> 0.88 us  [from_above(): return lax.ppermute(block, axis, pairs)]
    all_to_all x0 -> x1, blocking collectives: none -> 14.7 us  [per_device(): middle = lax.all_to_all(row, 'lat', 0, 0, tiled=True)]
    all_to_all x1, waiting for transfers between devices: 31.3 us -> 17.8 us  [per_device(): packed = lax.all_to_all(packed, 'wave', 0, 0, tiled=True)]
    ppermute x1, waiting for transfers between devices: 10.8 us -> 0.01 us  [per_device(): next_row = lax.ppermute(row, ('wave', 'lat'), pairs)]
    ppermute x0 -> x2, starting transfers between devices: none -> 8.46 us  [the longest x1 4.89 us: per_device(): late = lax.ppermute(late, 'wave', ends + [(j, i) for i, j in ends])]
    ppermute x2 -> x1, starting transfers between devices: 5.98 us -> 1.75 us  [from_above(): return lax.ppermute(block, axis, pairs)]
    ppermute x2 -> x1, starting transfers between devices: 4.1 us -> 0.01 us  [from_below(): return lax.ppermute(block, axis, pairs)]
  transfers between devices with their start and end apart: 7 -> 7, of which waited for: 4 -> 5; matrix products, arithmetic and copies ran while one was open for 4% -> 5% of each run, Pallas kernels for 0% -> 0%
where the time goes in v7:
time: 142 us; the launch traced here: 139 us
  blocking collectives  42.4 us (30%)
  waiting for transfers between devices  40.9 us (29%)
  starting transfers between devices  28.4 us (20%)
  Pallas kernels  17.4 us (12%)
  other arithmetic  6.39 us (4%)
  local copies, waits for them, and re-layouts  3.48 us (2%)
    all_to_all x1, blocking collectives, per_device(): lax.all_to_all(modes.reshape(LATS, SLOTS, LEV), ('wave', 'lat'), 0, 0, ti...  27.7 us
    all_to_all x1, waiting for transfers between devices, per_device(): packed = lax.all_to_all(packed, 'wave', 0, 0, tiled=True)  17.8 us
    all_to_all x1, blocking collectives, per_device(): middle = lax.all_to_all(row, 'lat', 0, 0, tiled=True)  14.7 us
    ppermute x1, waiting for transfers between devices, per_device(): late = lax.ppermute(late, 'wave', ends + [(j, i) for i, j in ends])  11.5 us
    all_to_all x1, starting transfers between devices, per_device(): packed = lax.all_to_all(packed, 'wave', 0, 0, tiled=True)  10.9 us
    pallas_call x1, Pallas kernels, advected(): pl.pallas_call(advect_kernel, in_specs=[pl.BlockSpec(memory_space=pltpu.S...  7.19 us
    ppermute x1, waiting for transfers between devices, per_device(): lax.ppermute(jnp.where(odd, lower, upper), 'wave', [(w, w ^ 1) for w in r...  7.15 us
    pallas_call x1, Pallas kernels, packed_inputs(): pl.pallas_call(packing_kernel, in_specs=[smem, smem, far, far, far], out_...  6.1 us
  transfers between devices with their start and end apart: 7, of which 5 were waited for; matrix products, arithmetic and copies ran while one was open for 5% of the time, Pallas kernels for 0%

profile of v7, /device:TPU:64, one launch (start us, length us, event | category | flops | bytes accessed | tf_op | source)
XLA Modules:
  0.0 139.2 jit_solution(2172309044189871119)
XLA Ops:
  0.0 6.1 %shard_map.91 = bf16[16,208,256]{2,1,0:T(8,128)(2,1)} custom-call(s32[40]{0:T(128)} %wavenumber.1, s32[1]{0:T(128)} %bitcast.1.first, bf16[1600,256]{1,0:T(8,128)(2,1)} %bitcast.13, bf16[40,128,128]{2,1,0:T(8,128)(2,1)} %vert.1, bf16[40,40,256]{2,1,0:T(8,128)(2,1)} %legendre.1), custom_call_target="tpu_custom_call" | custom-call | tf_op jit(solution)/shard_map/pallas_call | solution.py:129
  6.1 10.9 %all-to-all-start = ((bf16[16,208,256]{2,1,0:T(8,128)(2,1)}), bf16[16,208,256]{2,1,0:T(8,128)(2,1)S(1)}, u32[]{:S(2)}, u32[]{:S(2)}) async-start(bf16[16,208,256]{2,1,0:T(8,128)(2,1)} %shard_map.91), calls=%async_computation | async-start | bytes 3407872 | tf_op jit(solution)/shard_map/all_to_all | solution.py:393
  17.1 1.5 %fusion.2 = (bf16[1,16,80,128]{3,2,1,0:T(8,128)(2,1)S(1)}, bf16[1,16,80,128]{3,2,1,0:T(8,128)(2,1)S(1)}) fusion(f32[16,80,128]{2,1,0:T(8,128)S(1)} %copy-done.1, s32[16,80,128]{2,1,0:T(8,128)} %nf.1, f32[16,80,128]{2,1,0:T(8,128)S(1)} %copy-done, s32[16,80,128]{2,1,0:T(8,128)} %ef.1), kind=kLoop, calls=%fused_computation.12 | loop fusion | flops 1310720 | bytes 3276800 | tf_op jit(solution)/shard_map/stack | solution.py:383
  19.3 1.8 %collective-permute-start.1 = (bf16[2,16,8,128]{3,2,1,0:T(8,128)(2,1)}, bf16[2,16,8,128]{3,2,1,0:T(8,128)(2,1)S(1)}, u32[]{:S(2)}, u32[]{:S(2)}) collective-permute-start(bf16[2,16,8,128]{3,2,1,0:T(8,128)(2,1)} %get-tuple-element.20), channel_id=1, source_target_pairs={{1,0},{2,1},{3,2},{4,3},{5,4},{6,5},{7,6},{8,7},{9,8},{10,9},{11,1... | collective-permute-start | bytes 196616 | tf_op jit(solution)/shard_map/ppermute | solution.py:367
  21.1 1.3 cosine_multiply_fusion
  22.4 0.9 collective-permute-done.1.east
  23.3 3.6 %collective-permute-done.west = bf16[2,16,8,128]{3,2,1,0:T(8,128)(2,1)S(1)} collective-permute-done((bf16[2,16,8,128]{3,2,1,0:T(8,128)(2,1)S(1)}, bf16[2,16,8,128]{3,2,1,0:T(8,128)(2,1)S(1)}, u32[]{:S(2)}, u32[]{:S(2)}) %collective-permute-start) | collective-permute-done | bytes 65568 | tf_op jit(solution)/shard_map/ppermute | solution.py:362
  26.9 1.8 %broadcast_select_fusion = (bf16[2,7,96,128]{3,2,1,0:T(8,128)(2,1)}, bf16[2,7,96,128]{3,2,1,0:T(8,128)(2,1)S(1)}) fusion(pred[]{:T(512)S(6)} %eq.15, bf16[2,16,8,128]{3,2,1,0:T(8,128)(2,1)S(1)} %collective-permute-done.1.east, bf16[1,16,80,128]{3,2,1,0:T(8,128)(2,1)S(1)} %get-tuple-element.25, bf16[1,16,80,128]{3,2,1,0:T(8,128)(2,1)} %copy-done.8, ...), kind=kLoop, calls=%fused_computation.10 | loop fusion | flops 3096576 | bytes 1474561 | tf_op jit(solution)/shard_map/jit(_where)/select_n | solution.py:397
  28.7 3.6 %collective-permute-start.2 = (bf16[2,7,96,128]{3,2,1,0:T(8,128)(2,1)S(1)}, bf16[2,7,96,128]{3,2,1,0:T(8,128)(2,1)S(1)}, u32[]{:S(2)}, u32[]{:S(2)}) collective-permute-start(bf16[2,7,96,128]{3,2,1,0:T(8,128)(2,1)S(1)} %get-tuple-element.18), channel_id=1, source_target_pairs={{0,16},{16,0},{32,48},{48,32},{64,80},{80,64},{96,112},{112,96},{1... | collective-permute-start | bytes 1032200 | tf_op jit(solution)/shard_map/ppermute | solution.py:396
  32.5 0.9 pad_maximum_fusion.tables
  33.3 7.2 %collective-permute-done.2.early = bf16[2,7,96,128]{3,2,1,0:T(8,128)(2,1)S(1)} collective-permute-done((bf16[2,7,96,128]{3,2,1,0:T(8,128)(2,1)S(1)}, bf16[2,7,96,128]{3,2,1,0:T(8,128)(2,1)S(1)}, u32[]{:S(2)}, u32[]{:S(2)}) %collective-permute-start.2) | collective-permute-done | bytes 344096 | tf_op jit(solution)/shard_map/ppermute | solution.py:396
  40.5 0.8 copy-done.4
  41.2 17.8 %all-to-all-done = bf16[16,208,256]{2,1,0:T(8,128)(2,1)S(1)} async-done(((bf16[16,208,256]{2,1,0:T(8,128)(2,1)}), bf16[16,208,256]{2,1,0:T(8,128)(2,1)S(1)}, u32[]{:S(2)}, u32[]{:S(2)}) %all-to-all-start) | async-done | bytes 1703968 | tf_op jit(solution)/shard_map/all_to_all | solution.py:393
  59.7 27.7 %all_to_all.20 = bf16[256,8,128]{2,1,0:T(8,128)(2,1)} all-to-all(bf16[256,8,128]{2,1,0:T(8,128)(2,1)S(1)} %bitcast.11), channel_id=1, replica_groups=mesh['wave'=16,'lat'=16] {'wave','lat'}, dimensions={0} | all-to-all | bytes 1048576 | tf_op jit(solution)/shard_map/all_to_all | solution.py:403
  87.4 3.5 %shard_map.93 = bf16[16,96,128]{2,1,0:T(8,128)(2,1)} custom-call(bf16[2048,128]{1,0:T(8,128)(2,1)} %bitcast.12, f32[208,768]{1,0:T(8,128)} %pad_maximum_fusion.tables), custom_call_target="tpu_custom_call" | custom-call | tf_op jit(solution)/shard_map/pallas_call | solution.py:249
  90.9 3.8 %collective-permute-start.3 = (bf16[16,96,128]{2,1,0:T(8,128)(2,1)}, bf16[16,96,128]{2,1,0:T(8,128)(2,1)}, u32[]{:S(2)}, u32[]{:S(2)}) collective-permute-start(bf16[16,96,128]{2,1,0:T(8,128)(2,1)} %shard_map.93), channel_id=1, source_target_pairs={{8,24},{9,25},{10,26},{11,27},{12,28},{13,29},{14,30},{15,31},{16,... | collective-permute-start | bytes 1179656 | tf_op jit(solution)/shard_map/ppermute | solution.py:411
  94.7 14.7 %all_to_all.21.middle = bf16[16,96,128]{2,1,0:T(8,128)(2,1)S(1)} all-to-all(bf16[16,96,128]{2,1,0:T(8,128)(2,1)} %shard_map.93), channel_id=1, replica_groups=mesh['wave'=16,'lat'=16] {'lat'}, dimensions={0} | all-to-all | bytes 786432 | tf_op jit(solution)/shard_map/all_to_all | solution.py:412
  109.4 3.6 %all-to-all-start.3 = ((bf16[16,96,128]{2,1,0:T(8,128)(2,1)}), bf16[16,96,128]{2,1,0:T(8,128)(2,1)S(1)}, u32[]{:S(2)}, u32[]{:S(2)}) async-start(bf16[16,96,128]{2,1,0:T(8,128)(2,1)} %collective-permute-done.3), calls=%async_computation.3 | async-start | bytes 786432 | tf_op jit(solution)/shard_map/all_to_all | solution.py:413
  112.9 4.9 %collective-permute-start.4 = (bf16[2,7,96,128]{3,2,1,0:T(8,128)(2,1)}, bf16[2,7,96,128]{3,2,1,0:T(8,128)(2,1)S(1)}, u32[]{:S(2)}, u32[]{:S(2)}) collective-permute-start(bf16[2,7,96,128]{3,2,1,0:T(8,128)(2,1)} %get-tuple-element.16), channel_id=1, source_target_pairs={{16,32},{48,64},{80,96},{112,128},{144,160},{176,192},{208,224},{3... | collective-permute-start | bytes 1032200 | tf_op jit(solution)/shard_map/ppermute | solution.py:402
  117.8 11.5 %collective-permute-done.4.late = bf16[2,7,96,128]{3,2,1,0:T(8,128)(2,1)S(1)} collective-permute-done((bf16[2,7,96,128]{3,2,1,0:T(8,128)(2,1)}, bf16[2,7,96,128]{3,2,1,0:T(8,128)(2,1)S(1)}, u32[]{:S(2)}, u32[]{:S(2)}) %collective-permute-start.4) | collective-permute-done | bytes 344096 | tf_op jit(solution)/shard_map/ppermute | solution.py:402
  129.3 0.7 copy-done.6
  130.1 1.0 copy-done.5
  131.1 1.0 copy-done.7
  132.0 7.2 %shard_map.94 = f32[16,80,128]{2,1,0:T(8,128)} custom-call(s32[1]{0:T(128)} %bitcast.where, bf16[16,96,128]{2,1,0:T(8,128)(2,1)S(1)} %all_to_all.21.middle, bf16[16,96,128]{2,1,0:T(8,128)(2,1)S(1)} %all-to-all-done.3.halo, f32[16,80,128]{2,1,0:T(8,128)S(1)} %copy-done, f32[16,80,128]{2,1,0:T(8,128)S(1)} %copy-done.1, s32[16,80,128]{2,1,0:T(8,128)S(1)} %copy-done.2, ...), custom_call_target="tpu_custom_call" | custom-call | tf_op jit(solution)/shard_map/pallas_call | solution.py:345
  (28 shorter events, 1.6 us)
Async XLA Ops:
  6.1 10.9 %copy-start = (f32[16,80,128]{2,1,0:T(8,128)S(1)}, f32[16,80,128]{2,1,0:T(8,128)}, u32[]{:S(2)}) copy-start(f32[16,80,128]{2,1,0:T(8,128)} %ce.1) | copy-start | bytes 1966084
  6.1 10.9 %copy-start.1 = (f32[16,80,128]{2,1,0:T(8,128)S(1)}, f32[16,80,128]{2,1,0:T(8,128)}, u32[]{:S(2)}) copy-start(f32[16,80,128]{2,1,0:T(8,128)} %cn.1) | copy-start | bytes 1966084
  6.1 52.9 %all-to-all-start = ((bf16[16,208,256]{2,1,0:T(8,128)(2,1)}), bf16[16,208,256]{2,1,0:T(8,128)(2,1)S(1)}, u32[]{:S(2)}, u32[]{:S(2)}) async-start(bf16[16,208,256]{2,1,0:T(8,128)(2,1)} %shard_map.91), calls=%async_computation | async-start | bytes 3407872 | tf_op jit(solution)/shard_map/all_to_all | solution.py:393
  17.1 4.0 %copy-start.9 = (s32[768]{0:T(1024)S(1)}, s32[768]{0:T(1024)}, u32[]{:S(2)}) copy-start(s32[768]{0:T(1024)} %constant.60.clone) | copy-start | bytes 9220
  17.1 4.0 %copy-start.10 = (f32[768]{0:T(1024)S(1)}, f32[768]{0:T(1024)}, u32[]{:S(2)}) copy-start(f32[768]{0:T(1024)} %constant.67) | copy-start | bytes 9220
  17.1 4.0 %copy-start.11 = (f32[768]{0:T(1024)S(1)}, f32[768]{0:T(1024)}, u32[]{:S(2)}) copy-start(f32[768]{0:T(1024)} %constant.68) | copy-start | bytes 9220
  18.6 2.5 %copy-start.8 = (bf16[1,16,80,128]{3,2,1,0:T(8,128)(2,1)}, bf16[1,16,80,128]{3,2,1,0:T(8,128)(2,1)S(1)}, u32[]{:S(2)}) copy-start(bf16[1,16,80,128]{3,2,1,0:T(8,128)(2,1)S(1)} %get-tuple-element.26) | copy-start | bytes 983044
  19.3 4.0 %collective-permute-start.1 = (bf16[2,16,8,128]{3,2,1,0:T(8,128)(2,1)}, bf16[2,16,8,128]{3,2,1,0:T(8,128)(2,1)S(1)}, u32[]{:S(2)}, u32[]{:S(2)}) collective-permute-start(bf16[2,16,8,128]{3,2,1,0:T(8,128)(2,1)} %get-tuple-element.20), channel_id=1, source_target_pairs={{1,0},{2,1},{3,2},{4,3},{5,4},{6,5},{7,6},{8,7},{9,8},{10,9},{11,1... | collective-permute-start | bytes 196616 | tf_op jit(solution)/shard_map/ppermute | solution.py:367
  21.1 5.8 %collective-permute-start = (bf16[2,16,8,128]{3,2,1,0:T(8,128)(2,1)S(1)}, bf16[2,16,8,128]{3,2,1,0:T(8,128)(2,1)S(1)}, u32[]{:S(2)}, u32[]{:S(2)}) collective-permute-start(bf16[2,16,8,128]{3,2,1,0:T(8,128)(2,1)S(1)} %get-tuple-element.19), channel_id=1, source_target_pairs={{0,1},{1,2},{2,3},{3,4},{4,5},{5,6},{6,7},{7,8},{8,9},{9,10},{10,1... | collective-permute-start | bytes 196616 | tf_op jit(solution)/shard_map/ppermute | solution.py:362
  28.7 11.8 %collective-permute-start.2 = (bf16[2,7,96,128]{3,2,1,0:T(8,128)(2,1)S(1)}, bf16[2,7,96,128]{3,2,1,0:T(8,128)(2,1)S(1)}, u32[]{:S(2)}, u32[]{:S(2)}) collective-permute-start(bf16[2,7,96,128]{3,2,1,0:T(8,128)(2,1)S(1)} %get-tuple-element.18), channel_id=1, source_target_pairs={{0,16},{16,0},{32,48},{48,32},{64,80},{80,64},{96,112},{112,96},{1... | collective-permute-start | bytes 1032200 | tf_op jit(solution)/shard_map/ppermute | solution.py:396
  40.5 0.8 copy-start.4
  87.4 42.7 %copy-start.2 = (s32[16,80,128]{2,1,0:T(8,128)S(1)}, s32[16,80,128]{2,1,0:T(8,128)}, u32[]{:S(2)}) copy-start(s32[16,80,128]{2,1,0:T(8,128)} %ef.1) | copy-start | bytes 1966084
  87.4 42.7 %copy-start.3 = (s32[16,80,128]{2,1,0:T(8,128)S(1)}, s32[16,80,128]{2,1,0:T(8,128)}, u32[]{:S(2)}) copy-start(s32[16,80,128]{2,1,0:T(8,128)} %nf.1) | copy-start | bytes 1966084
  90.9 18.5 %collective-permute-start.3 = (bf16[16,96,128]{2,1,0:T(8,128)(2,1)}, bf16[16,96,128]{2,1,0:T(8,128)(2,1)}, u32[]{:S(2)}, u32[]{:S(2)}) collective-permute-start(bf16[16,96,128]{2,1,0:T(8,128)(2,1)} %shard_map.93), channel_id=1, source_target_pairs={{8,24},{9,25},{10,26},{11,27},{12,28},{13,29},{14,30},{15,31},{16,... | collective-permute-start | bytes 1179656 | tf_op jit(solution)/shard_map/ppermute | solution.py:411
  109.4 20.7 %all-to-all-start.3 = ((bf16[16,96,128]{2,1,0:T(8,128)(2,1)}), bf16[16,96,128]{2,1,0:T(8,128)(2,1)S(1)}, u32[]{:S(2)}, u32[]{:S(2)}) async-start(bf16[16,96,128]{2,1,0:T(8,128)(2,1)} %collective-permute-done.3), calls=%async_computation.3 | async-start | bytes 786432 | tf_op jit(solution)/shard_map/all_to_all | solution.py:413
  112.9 16.4 %collective-permute-start.4 = (bf16[2,7,96,128]{3,2,1,0:T(8,128)(2,1)}, bf16[2,7,96,128]{3,2,1,0:T(8,128)(2,1)S(1)}, u32[]{:S(2)}, u32[]{:S(2)}) collective-permute-start(bf16[2,7,96,128]{3,2,1,0:T(8,128)(2,1)} %get-tuple-element.16), channel_id=1, source_target_pairs={{16,32},{48,64},{80,96},{112,128},{144,160},{176,192},{208,224},{3... | collective-permute-start | bytes 1032200 | tf_op jit(solution)/shard_map/ppermute | solution.py:402
  129.3 0.7 copy-start.6
  130.1 1.0 copy-start.5
  131.0 1.0 copy-start.7
